TPU v7x, 32 devices: a 4x2x2 block of a 4x4x8 slice. The times are simulated.
32 devices in a mesh: dp: 4 (over y, z), sp: 8 (over x, core).
Axes of the slice: x: 4, y: 2, z: 2, core: 2. Of those that a mesh axis runs over, the one named last changes fastest.
The devices are a block of a 4x4x8 slice.
Arguments:
- x_in: bfloat16 [8, 2048, 2304], P('dp', 'sp'), parts along dimension 0
- dy_in: bfloat16 [8, 2048, 2304], P('dp', 'sp'), parts along dimension 0
- positions: int32 [8192], P(('dp', 'sp')), parts along dimension 0
- w_q: bfloat16 [2304, 2048], replicated
- w_k: bfloat16 [2304, 1024], replicated
- w_v: bfloat16 [2304, 1024], replicated
- w_o: bfloat16 [2048, 2304], replicated
- w_pre: float32 [2304], replicated
- w_post: float32 [2304], replicated
- q_norm: float32 [256], replicated
- k_norm: float32 [256], replicated
Outputs:
- output 1: bfloat16 [8, 2048, 2304], P('dp', 'sp'), parts along dimension 0
- output 2: bfloat16 [8, 2048, 2304], P('dp', 'sp'), parts along dimension 0
- output 3: bfloat16 [9216, 2048], P('dp'), parts along dimension 0
- output 4: bfloat16 [9216, 1024], P('dp'), parts along dimension 0
- output 5: bfloat16 [9216, 1024], P('dp'), parts along dimension 0
- output 6: bfloat16 [8192, 2304], P('dp'), parts along dimension 0
- output 7: float32 [9216], P('dp'), parts along dimension 0
- output 8: float32 [9216], P('dp'), parts along dimension 0
- output 9: float32 [1024], P('dp'), parts along dimension 0
- output 10: float32 [1024], P('dp'), parts along dimension 0
There are 4 independent parts. A program takes and returns all parts, laid end to end along the dimension named above; an argument that names none is the same for every part.
All inputs are finite; a program needn't handle non-finite values.
Results may differ from a plain program's by a relative error of at most 0.02.
Values are sent between devices in bfloat16 or wider.
A program may use at most 768 MiB of HBM per device.

v0:
```python
import functools
import jax
import jax.numpy as jnp
from jax import lax
from jax.sharding import PartitionSpec as P

EPS = 1e-6
ROPE_BASE = 1000000.0
ROPE_SCALE = 8.0
NEG_BIG = -1e30
Q_BLOCK = 1024


def rms_scale(x_f32, weight):
    inv_rms = lax.rsqrt(jnp.mean(x_f32 * x_f32, axis=-1, keepdims=True) + EPS)
    return x_f32 * inv_rms * (1.0 + weight)


def pre_norm(x_f32, weight):
    return rms_scale(x_f32, weight).astype(jnp.bfloat16)


def post_norm(proj, weight):
    return rms_scale(proj.astype(jnp.float32), weight)


def rope_tables(positions, head):
    half_dim = head // 2
    inv_freq = ROPE_BASE ** (-jnp.arange(half_dim, dtype=jnp.float32) * 2.0 / head)
    angles = (positions.astype(jnp.float32) / ROPE_SCALE)[:, None] * inv_freq[None, :]
    return jnp.cos(angles), jnp.sin(angles)


def norm_rope(heads_bf, weight, cosines, sines):
    half_dim = heads_bf.shape[-1] // 2
    normed = rms_scale(heads_bf.astype(jnp.float32), weight)
    first = normed[..., :half_dim]
    second = normed[..., half_dim:]
    cos_b = cosines[None, :, None, :]
    sin_b = sines[None, :, None, :]
    rotated = jnp.concatenate([first * cos_b - second * sin_b, second * cos_b + first * sin_b], axis=-1)
    return rotated.astype(jnp.bfloat16)


def causal_mask(start, block, end):
    row_ids = start + jnp.arange(block)
    col_ids = jnp.arange(end)
    return row_ids[:, None] >= col_ids[None, :]


def attention_fwd(q_all, k_all, v_all):
    batch, seq, q_heads, head = q_all.shape
    kv_loc = k_all.shape[2]
    scale = head ** -0.5
    block = min(Q_BLOCK, seq)
    q_grp = q_all.reshape(batch, seq, kv_loc, q_heads // kv_loc, head)
    pieces = []
    row_lse = []
    for index in range(seq // block):
        start = index * block
        end = start + block
        scores = jnp.einsum('bqkgh,bskh->bkgqs', q_grp[:, start:end], k_all[:, :end], preferred_element_type=jnp.float32) * scale
        scores = jnp.where(causal_mask(start, block, end), scores, NEG_BIG)
        row_max = jnp.max(scores, axis=-1, keepdims=True)
        exp_scores = jnp.exp(scores - row_max)
        row_sum = jnp.sum(exp_scores, axis=-1, keepdims=True)
        attn_prob = (exp_scores / row_sum).astype(jnp.bfloat16)
        pieces.append(jnp.einsum('bkgqs,bskh->bqkgh', attn_prob, v_all[:, :end], preferred_element_type=jnp.float32).astype(jnp.bfloat16))
        row_lse.append(row_max + jnp.log(row_sum))
    return jnp.concatenate(pieces, axis=1).reshape(batch, seq, q_heads, head), row_lse


def attention_bwd(q_all, k_all, v_all, row_lse, d_out):
    batch, seq, q_heads, head = q_all.shape
    kv_loc = k_all.shape[2]
    per_kv = q_heads // kv_loc
    scale = head ** -0.5
    block = min(Q_BLOCK, seq)
    q_grp = q_all.reshape(batch, seq, kv_loc, per_kv, head)
    do_grp = d_out.reshape(batch, seq, kv_loc, per_kv, head)
    dk_acc = jnp.zeros(k_all.shape, jnp.float32)
    dv_acc = jnp.zeros(v_all.shape, jnp.float32)
    dq_pieces = []
    for index in range(seq // block):
        start = index * block
        end = start + block
        q_blk = q_grp[:, start:end]
        do_blk = do_grp[:, start:end]
        k_pre = k_all[:, :end]
        v_pre = v_all[:, :end]
        scores = jnp.einsum('bqkgh,bskh->bkgqs', q_blk, k_pre, preferred_element_type=jnp.float32) * scale
        scores = jnp.where(causal_mask(start, block, end), scores, NEG_BIG)
        attn_prob = jnp.exp(scores - row_lse[index])
        d_prob = jnp.einsum('bqkgh,bskh->bkgqs', do_blk, v_pre, preferred_element_type=jnp.float32)
        d_score = (attn_prob * (d_prob - jnp.sum(d_prob * attn_prob, axis=-1, keepdims=True)) * scale).astype(jnp.bfloat16)
        dq_pieces.append(jnp.einsum('bkgqs,bskh->bqkgh', d_score, k_pre, preferred_element_type=jnp.float32).astype(jnp.bfloat16))
        dk_part = jnp.einsum('bkgqs,bqkgh->bskh', d_score, q_blk, preferred_element_type=jnp.float32)
        dv_part = jnp.einsum('bkgqs,bqkgh->bskh', attn_prob.astype(jnp.bfloat16), do_blk, preferred_element_type=jnp.float32)
        dk_acc = lax.dynamic_update_slice(dk_acc, dk_acc[:, :end] + dk_part, (0, 0, 0, 0))
        dv_acc = lax.dynamic_update_slice(dv_acc, dv_acc[:, :end] + dv_part, (0, 0, 0, 0))
    dq_all = jnp.concatenate(dq_pieces, axis=1).reshape(batch, seq, q_heads, head)
    return dq_all, dk_acc.astype(jnp.bfloat16), dv_acc.astype(jnp.bfloat16)


def fold_copies(grad_wide, kv_heads, rep):
    if rep == 1:
        return grad_wide
    batch, seq_loc, wide, head = grad_wide.shape
    summed = jnp.sum(grad_wide.reshape(batch, seq_loc, kv_heads, rep, head), axis=3, dtype=jnp.float32)
    return summed.astype(jnp.bfloat16)


def solution(mesh):
    group = mesh.shape['sp']

    def to_heads(arr):
        return lax.all_to_all(arr, 'sp', 2, 1, tiled=True)

    def to_tokens(arr):
        return lax.all_to_all(arr, 'sp', 1, 2, tiled=True)

    def device_step(x_in, dy_in, positions, w_q, w_k, w_v, w_o, w_pre, w_post, q_norm, k_norm):
        batch, seq_loc, width = x_in.shape
        head = q_norm.shape[0]
        heads = w_q.shape[1] // head
        kv_heads = w_k.shape[1] // head
        rep = max(1, group // kv_heads)
        x_f32 = x_in.astype(jnp.float32)
        normed, pre_pull = jax.vjp(pre_norm, x_f32, w_pre)
        q_proj = jnp.einsum('bsd,dn->bsn', normed, w_q, preferred_element_type=jnp.float32).astype(jnp.bfloat16).reshape(batch, seq_loc, heads, head)
        k_proj = jnp.einsum('bsd,dn->bsn', normed, w_k, preferred_element_type=jnp.float32).astype(jnp.bfloat16).reshape(batch, seq_loc, kv_heads, head)
        v_proj = jnp.einsum('bsd,dn->bsn', normed, w_v, preferred_element_type=jnp.float32).astype(jnp.bfloat16).reshape(batch, seq_loc, kv_heads, head)
        cosines, sines = rope_tables(positions, head)
        q_rot, q_pull = jax.vjp(functools.partial(norm_rope, cosines=cosines, sines=sines), q_proj, q_norm)
        k_rot, k_pull = jax.vjp(functools.partial(norm_rope, cosines=cosines, sines=sines), k_proj, k_norm)
        q_all = to_heads(q_rot)
        k_all = to_heads(jnp.repeat(k_rot, rep, axis=2))
        v_all = to_heads(jnp.repeat(v_proj, rep, axis=2))
        o_all, row_lse = attention_fwd(q_all, k_all, v_all)
        o_flat = to_tokens(o_all).reshape(batch, seq_loc, heads * head)
        proj = jnp.einsum('bsn,nd->bsd', o_flat, w_o, preferred_element_type=jnp.float32).astype(jnp.bfloat16)
        post, post_pull = jax.vjp(post_norm, proj, w_post)
        y_out = (x_f32 + post).astype(jnp.bfloat16)
        dy_f32 = dy_in.astype(jnp.float32)
        d_proj, dw_post = post_pull(dy_f32)
        dw_o = jnp.einsum('bsn,bsd->nd', o_flat, d_proj, preferred_element_type=jnp.float32)
        d_oflat = jnp.einsum('bsd,nd->bsn', d_proj, w_o, preferred_element_type=jnp.float32).astype(jnp.bfloat16)
        d_oall = to_heads(d_oflat.reshape(batch, seq_loc, heads, head))
        dq_all, dk_all, dv_all = attention_bwd(q_all, k_all, v_all, row_lse, d_oall)
        dq_rot = to_tokens(dq_all)
        dk_rot = fold_copies(to_tokens(dk_all), kv_heads, rep)
        dv_proj = fold_copies(to_tokens(dv_all), kv_heads, rep)
        dq_proj, dq_norm = q_pull(dq_rot)
        dk_proj, dk_norm = k_pull(dk_rot)
        dq_flat = dq_proj.reshape(batch, seq_loc, heads * head)
        dk_flat = dk_proj.reshape(batch, seq_loc, kv_heads * head)
        dv_flat = dv_proj.reshape(batch, seq_loc, kv_heads * head)
        dw_q = jnp.einsum('bsd,bsn->dn', normed, dq_flat, preferred_element_type=jnp.float32)
        dw_k = jnp.einsum('bsd,bsn->dn', normed, dk_flat, preferred_element_type=jnp.float32)
        dw_v = jnp.einsum('bsd,bsn->dn', normed, dv_flat, preferred_element_type=jnp.float32)
        d_normed = (jnp.einsum('bsn,dn->bsd', dq_flat, w_q, preferred_element_type=jnp.float32)
                    + jnp.einsum('bsn,dn->bsd', dk_flat, w_k, preferred_element_type=jnp.float32)
                    + jnp.einsum('bsn,dn->bsd', dv_flat, w_v, preferred_element_type=jnp.float32)).astype(jnp.bfloat16)
        dx_norm, dw_pre = pre_pull(d_normed)
        dx_out = (dy_f32 + dx_norm).astype(jnp.bfloat16)
        sums = lax.psum((dw_q, dw_k, dw_v, dw_o, dw_pre, dw_post, dq_norm, dk_norm), 'sp')
        return (y_out, dx_out, sums[0].astype(jnp.bfloat16), sums[1].astype(jnp.bfloat16), sums[2].astype(jnp.bfloat16), sums[3].astype(jnp.bfloat16), sums[4], sums[5], sums[6], sums[7])

    token_spec = P('dp', 'sp', None)
    return jax.shard_map(device_step, mesh=mesh,
                         in_specs=(token_spec, token_spec, P(('dp', 'sp')), P(None, None), P(None, None), P(None, None), P(None, None), P(None), P(None), P(None), P(None)),
                         out_specs=(token_spec, token_spec, P('dp', None), P('dp', None), P('dp', None), P('dp', None), P('dp'), P('dp'), P('dp'), P('dp')),
                         check_vma=False)
```

profile of v0, /device:TPU:120, one launch (start us, length us, event | category | flops | bytes accessed | tf_op | source)
XLA Modules:
  0.0 1011.2 jit_solution(223677872739995872)
XLA Ops:
  0.6 2.2 fusion.44
  4.1 5.7 fusion.92
  12.9 4.6 all-to-all-start
  17.5 6.3 fusion.98
  27.9 2.9 copy.271
  35.9 8.7 all-to-all-done
  46.2 4.7 all-to-all-start.1
  51.0 10.4 %fusion.79 = f32[2,256,2048]{2,1,0:T(8,128)} fusion(bf16[2304,2048]{1,0:T(8,128)(2,1)} %param.14, bf16[2,256,2304]{2,1,0:T(8,128)(2,1)S(1)} %copy-done.5, f32[2304]{0:T(1024)S(1)} %broadcast_add_fusion.1, f32[2,256]{1,0:T(2,128)S(1)} %fusion.116), kind=kOutput, calls=%fused_computation.110 | convolution fusion | flops 4838653952 | bytes 16002048 | tf_op jit(solution)/shard_map/bsd,dn->bsn/dot_general | solution.py:130
  61.6 4.2 copy.359
  66.6 2.6 fusion.73
  71.6 6.3 all-to-all-done.1
  77.9 4.8 all-to-all-start.2
  83.0 3.1 iota_compare_fusion
  86.2 4.1 copy.269
  90.2 4.2 reshape.361
  94.4 3.2 copy.358
  97.6 3.1 copy.273
  100.7 9.0 all-to-all-done.2
  115.0 2.4 copy-done
  119.2 8.1 fusion.126
  127.4 8.1 fusion.4
  135.5 8.8 fusion.104
  145.8 6.1 copy.284
  152.0 4.7 all-to-all-start.3
  156.7 27.0 %all-to-all-done.3 = bf16[2,2048,1,256]{3,0,2,1:T(2,128)(2,1)} async-done(((bf16[2,2048,1,256]{3,0,2,1:T(2,128)(2,1)}), bf16[2,2048,1,256]{3,0,2,1:T(2,128)(2,1)}, u32[]{:S(2)}, u32[]{:S(2)}) %all-to-all-start.3) | async-done | bytes 2097184 | tf_op jit(solution)/shard_map/all_to_all | solution.py:120
  183.7 4.1 copy.367
  187.7 4.2 reshape.366
  191.9 9.5 fusion.42
  201.5 4.8 fusion.40
  206.3 9.0 fusion.82
  216.9 4.7 all-to-all-start.4
  221.7 12.4 %convolution_bitcast_fusion = f32[2048,2304]{1,0:T(8,128)} fusion(bf16[2,256,2048]{2,1,0:T(8,128)(2,1)} %reshape.366, bf16[2,256,2304]{2,1,0:T(8,128)(2,1)} %param.12, bf16[2,256,2304]{2,1,0:T(8,128)(2,1)} %copy-done.17, f32[2,256]{1,0:T(2,128)S(1)} %multiply_multiply_fusion.4, f32[2304]{0:T(1024)S(1)} %broadcast_add_fusion, f32[2,256]{1,0:T(2,128)S(1)} %fusion.117), kind=kOutput, calls=%fused_computation.11 | convolution fusion | flops 4841275392 | bytes 25703424 | tf_op jit(solution)/shard_map/bsn,bsd->nd/dot_general | solution.py:146
  234.1 14.6 %all-to-all-done.4 = bf16[2,256,8,256]{3,1,0,2:T(8,128)(2,1)} async-done(((bf16[2,256,8,256]{3,1,0,2:T(8,128)(2,1)}), bf16[2,256,8,256]{3,1,0,2:T(8,128)(2,1)}, u32[]{:S(2)}, u32[]{:S(2)}) %all-to-all-start.4) | async-done | bytes 2097184 | tf_op jit(solution)/shard_map/all_to_all | solution.py:117
  250.6 5.4 fusion.86
  256.1 4.7 fusion.18
  260.8 11.9 %fusion = (f32[2,1024]{1,0:T(2,128)S(1)}, f32[2,2048,1024]{2,1,0:T(8,128)}) fusion(f32[2,1,1,1024,2048]{3,4,0,2,1:T(8,128)} %get-tuple-element.38, f32[2,1024]{1,0:T(2,128)S(1)} %log_add_fusion, bf16[2,2048,256]{1,2,0:T(8,128)(2,1)S(1)} %copy-done.12, bf16[2,2048,1,1,256]{4,1,0,3,2:T(8,128)(2,1)S(1)} %bitcast.295), kind=kOutput, calls=%fused_computation.3 | convolution fusion | flops 2160064512 | bytes 36716544 | tf_op jit(solution)/shard_map/bqkgh,bskh->bkgqs/dot_general | solution.py:94
  272.7 10.8 %fusion.68 = bf16[2,2048,1,256]{1,3,0,2:T(8,128)(2,1)} fusion(f32[2,1024,1,256]{1,3,0,2:T(8,128)S(1)} %fusion.86, f32[2,1,1,1024,2048]{3,4,0,2,1:T(8,128)} %get-tuple-element.38, f32[2,1024]{1,0:T(2,128)S(1)} %log_add_fusion, bf16[2,2048,1,1,256]{4,1,0,3,2:T(8,128)(2,1)S(1)} %bitcast.296), kind=kOutput, calls=%fused_computation.97 | convolution fusion | flops 2157969408 | bytes 22028288 | tf_op jit(solution)/shard_map/bkgqs,bqkgh->bskh/dot_general | solution.py:98
  283.5 6.1 copy.314
  289.6 4.5 all-to-all-start.7
  294.2 7.2 fusion.65
  304.9 11.9 %fusion.17 = bf16[2,1024,2048]{1,2,0:T(8,128)(2,1)S(1)} fusion(f32[2,2048,1024]{2,1,0:T(8,128)} %get-tuple-element.46, f32[2,1,1,1024,2048]{3,4,0,2,1:T(8,128)} %get-tuple-element.38, f32[2,1024]{1,0:T(2,128)S(1)} %get-tuple-element.45, f32[2,1024]{1,0:T(2,128)S(1)} %log_add_fusion), kind=kLoop, calls=%fused_computation.29 | loop fusion | flops 20971520 | bytes 41959424 | tf_op jit(solution)/shard_map/reshape.59
  316.8 3.4 copy-done.10
  320.2 4.3 fusion.69
  324.5 6.1 copy.304
  330.7 4.9 all-to-all-start.6
  335.6 3.9 fusion.111
  339.5 5.8 fusion.107
  346.8 6.1 copy.294
  353.0 5.0 reduce_sum.212
  359.9 6.7 convolution_bitcast_fusion.2
  366.6 5.2 all-to-all-start.5
  371.8 6.0 reduce_sum.210
  377.8 2.8 copy.353
  382.6 3.4 multiply_reduce_fusion.1
  386.0 2.4 fusion.85
  388.6 5.4 convolution_bitcast_fusion.3
  394.0 4.4 fusion.51
  398.4 4.6 fusion.47
  409.5 2.7 fusion.61
  412.2 3.9 copy.298
  416.1 11.1 %convolution_bitcast_fusion.1 = f32[2304,2048]{1,0:T(8,128)} fusion(bf16[2,256,2048]{1,2,0:T(8,128)(2,1)} %bitcast.312, bf16[2,256,2304]{2,1,0:T(8,128)(2,1)S(1)} %copy-done.5, f32[2304]{0:T(1024)S(1)} %copy-done.40, f32[2,256]{1,0:T(2,128)S(1)} %copy-done.49), kind=kOutput, calls=%fused_computation.12 | convolution fusion | flops 4836556800 | bytes 23342080 | tf_op jit(solution)/shard_map/bsd,bsn->dn/dot_general | solution.py:158
  427.2 12.0 %fusion.38 = (f32[2304]{0:T(1024)S(1)}, f32[2,256]{1,0:T(2,128)S(1)}, bf16[2,256,2304]{2,1,0:T(8,128)(2,1)S(1)}) fusion(bf16[2,256,2304]{2,1,0:T(8,128)(2,1)S(1)} %copy-done.5, f32[2,256]{1,0:T(2,128)S(1)} %copy-done.49, f32[2304]{0:T(1024)S(1)} %copy-done.40, f32[2,256,2304]{2,1,0:T(8,128)} %fusion.51, f32[2,256,2304]{2,1,0:T(8,128)} %fusion.47, ...), kind=kOutput, calls=%fused_computation.67 | convolution fusion | flops 4844811776 | bytes 25712640 | tf_op jit(solution)/shard_map/bsn,dn->bsd/dot_general | solution.py:161
  439.3 3.1 fusion.39
  442.4 568.2 %all-reduce.8 = (bf16[2304,2048]{1,0:T(8,128)(2,1)}, bf16[2304,1024]{1,0:T(8,128)(2,1)}, bf16[2304,1024]{1,0:T(8,128)(2,1)}, bf16[2048,2304]{1,0:T(8,128)(2,1)},...) all-reduce(f32[2304,2048]{1,0:T(8,128)} %convolution_bitcast_fusion, ...), channel_id=1, replica_groups=mesh['dp'=4,'sp'=8] {'sp'}, use_global_device_ids=true, to_apply=%region_16.17 | all-reduce | flops 14160896 | bytes 84975616 | tf_op jit(solution)/shard_map/psum | solution.py:166
  (176 shorter events, 46.3 us)
Async XLA Ops:
  3.4 47.5 %copy-start.48 = (f32[2,256]{1,0:T(2,128)}, f32[2,256]{1,0:T(2,128)S(1)}, u32[]{:S(2)}) copy-start(f32[2,256]{1,0:T(2,128)S(1)} %fusion.116) | copy-start | bytes 6148
  4.1 46.8 %copy-start.39 = (f32[2304]{0:T(1024)}, f32[2304]{0:T(1024)S(1)}, u32[]{:S(2)}) copy-start(f32[2304]{0:T(1024)S(1)} %broadcast_add_fusion.1) | copy-start | bytes 27652
  11.3 6.1 copy-start.4
  12.9 31.8 %all-to-all-start = ((bf16[2,256,8,256]{1,3,0,2:T(8,128)(2,1)}), bf16[2,256,8,256]{1,3,0,2:T(8,128)(2,1)}, u32[]{:S(2)}, u32[]{:S(2)}) async-start(bf16[2,256,8,256]{1,3,0,2:T(8,128)(2,1)} %bitcast.298), calls=%async_computation | async-start | bytes 4194304 | tf_op jit(solution)/shard_map/all_to_all | solution.py:117
  26.0 1.3 copy-start.6
  27.3 3.6 copy-start.50
  27.3 3.7 copy-start.51
  30.8 3.5 copy-start.2
  30.9 1.7 copy-start.36
  31.0 3.3 copy-start.43
  31.0 3.3 copy-start.34
  31.6 2.7 copy-start.23
  31.6 29.8 %copy-start.21 = (f32[256,128]{0,1:T(8,128)}, f32[256,128]{0,1:T(8,128)S(1)}, u32[]{:S(2)}) copy-start(f32[256,128]{0,1:T(8,128)S(1)} %get-tuple-element.35) | copy-start | bytes 393220
  35.9 15.0 %copy-start.5 = (bf16[2,256,2304]{2,1,0:T(8,128)(2,1)S(1)}, bf16[2,256,2304]{2,1,0:T(8,128)(2,1)}, u32[]{:S(2)}) copy-start(bf16[2,256,2304]{2,1,0:T(8,128)(2,1)} %param.11) | copy-start | bytes 7077892
  46.2 31.7 %all-to-all-start.1 = ((bf16[2,256,8,256]{3,1,0,2:T(8,128)(2,1)}), bf16[2,256,8,256]{3,1,0,2:T(8,128)(2,1)}, u32[]{:S(2)}, u32[]{:S(2)}) async-start(bf16[2,256,8,256]{3,1,0,2:T(8,128)(2,1)} %bitcast.299), calls=%async_computation.1 | async-start | bytes 4194304 | tf_op jit(solution)/shard_map/all_to_all | solution.py:117
  51.0 10.5 %copy-start.24 = (f32[256,128]{0,1:T(8,128)S(1)}, f32[256,128]{0,1:T(8,128)}, u32[]{:S(2)}) copy-start(f32[256,128]{0,1:T(8,128)} %copy-done.23) | copy-start | bytes 393220
  61.5 7.7 copy-start.25
  61.6 7.6 copy-start.27
  66.5 2.7 copy-start.32
  66.5 2.7 copy-start.45
  66.6 2.6 copy-start.30
  77.9 31.8 %all-to-all-start.2 = ((bf16[2,256,8,256]{3,1,0,2:T(8,128)(2,1)}), bf16[2,256,8,256]{3,1,0,2:T(8,128)(2,1)}, u32[]{:S(2)}, u32[]{:S(2)}) async-start(bf16[2,256,8,256]{3,1,0,2:T(8,128)(2,1)} %copy.278), calls=%async_computation.2 | async-start | bytes 4194304 | tf_op jit(solution)/shard_map/all_to_all | solution.py:117
  109.7 2.2 copy-start.18
  111.6 7.6 copy-start.13
  113.8 3.5 copy-start
  113.8 3.5 copy-start.15
  117.3 1.9 copy-start.20
  127.4 8.1 copy-start.11
  145.8 10.9 %copy-start.47 = (f32[2304]{0:T(1024)S(1)}, f32[2304]{0:T(1024)}, u32[]{:S(2)}) copy-start(f32[2304]{0:T(1024)} %param.19) | copy-start | bytes 27652
  152.0 31.7 %all-to-all-start.3 = ((bf16[2,2048,1,256]{3,0,2,1:T(2,128)(2,1)}), bf16[2,2048,1,256]{3,0,2,1:T(2,128)(2,1)}, u32[]{:S(2)}, u32[]{:S(2)}) async-start(bf16[2,2048,1,256]{3,0,2,1:T(2,128)(2,1)} %copy.284), calls=%async_computation.3 | async-start | bytes 4194304 | tf_op jit(solution)/shard_map/all_to_all | solution.py:120
  191.9 9.6 copy-start.8
  201.5 4.8 copy-start.17
  216.9 31.7 %all-to-all-start.4 = ((bf16[2,256,8,256]{3,1,0,2:T(8,128)(2,1)}), bf16[2,256,8,256]{3,1,0,2:T(8,128)(2,1)}, u32[]{:S(2)}, u32[]{:S(2)}) async-start(bf16[2,256,8,256]{3,1,0,2:T(8,128)(2,1)} %bitcast.300), calls=%async_computation.4 | async-start | bytes 4194304 | tf_op jit(solution)/shard_map/all_to_all | solution.py:117
  248.7 7.3 slice-start
  250.6 5.4 slice-start.1
  250.6 5.4 copy-start.16
  256.1 4.7 copy-start.12
  289.6 41.1 %all-to-all-start.7 = ((bf16[2,2048,1,256]{3,0,2,1:T(2,128)(2,1)}), bf16[2,2048,1,256]{3,0,2,1:T(2,128)(2,1)}, u32[]{:S(2)}, u32[]{:S(2)}) async-start(bf16[2,2048,1,256]{3,0,2,1:T(2,128)(2,1)} %copy.314), calls=%async_computation.7 | async-start | bytes 4194304 | tf_op jit(solution)/shard_map/all_to_all | solution.py:120
  294.1 9.2 copy-start.14
  301.3 2.0 copy-start.7
  316.8 3.4 copy-start.10
  330.7 35.9 %all-to-all-start.6 = ((bf16[2,2048,1,256]{3,0,2,1:T(2,128)(2,1)}), bf16[2,2048,1,256]{3,0,2,1:T(2,128)(2,1)}, u32[]{:S(2)}, u32[]{:S(2)}) async-start(bf16[2,2048,1,256]{3,0,2,1:T(2,128)(2,1)} %copy.304), calls=%async_computation.6 | async-start | bytes 4194304 | tf_op jit(solution)/shard_map/all_to_all | solution.py:120
  335.6 4.0 copy-start.19
  346.8 13.1 %copy-start.40 = (f32[2304]{0:T(1024)S(1)}, f32[2304]{0:T(1024)}, u32[]{:S(2)}) copy-start(f32[2304]{0:T(1024)} %copy-done.39) | copy-start | bytes 27652
  346.8 13.1 %copy-start.49 = (f32[2,256]{1,0:T(2,128)S(1)}, f32[2,256]{1,0:T(2,128)}, u32[]{:S(2)}) copy-start(f32[2,256]{1,0:T(2,128)} %copy-done.48) | copy-start | bytes 6148
  366.6 36.4 %all-to-all-start.5 = ((bf16[2,2048,1,256]{3,0,2,1:T(2,128)(2,1)}), bf16[2,2048,1,256]{3,0,2,1:T(2,128)(2,1)}, u32[]{:S(2)}, u32[]{:S(2)}) async-start(bf16[2,2048,1,256]{3,0,2,1:T(2,128)(2,1)} %copy.294), calls=%async_computation.5 | async-start | bytes 4194304 | tf_op jit(solution)/shard_map/all_to_all | solution.py:120
  371.8 9.1 copy-start.22
  380.6 1.9 copy-start.3
  380.6 1.9 copy-start.35
  380.6 1.9 copy-start.44
  380.9 5.0 copy-start.37
  386.0 8.0 slice-start.2
  386.0 12.4 %slice-start.4 = ((s8[4718592]{0:T(1024)(128)(4,1)}), s8[4194304]{0:T(1024)(128)(4,1)S(1)}, s32[]{:S(2)}) async-start(s8[4718592]{0:T(1024)(128)(4,1)} %bitcast.321), calls=%async_computation.12 | async-start | bytes 8388608
  388.6 5.4 copy-start.29
  388.6 5.4 slice-start.3
  388.6 9.8 slice-start.5
  404.9 1.0 copy-start.28
  405.9 2.2 copy-start.1
  405.9 2.2 copy-start.31
  405.9 2.2 copy-start.46
  408.1 1.4 copy-start.33
  427.2 12.1 %copy-start.42 = (f32[2,256]{1,0:T(2,128)S(1)}, f32[2,256]{1,0:T(2,128)}, u32[]{:S(2)}) copy-start(f32[2,256]{1,0:T(2,128)} %copy-done.41) | copy-start | bytes 6148
  427.2 12.1 %copy-start.9 = (bf16[2,256,2304]{2,1,0:T(8,128)(2,1)S(1)}, bf16[2,256,2304]{2,1,0:T(8,128)(2,1)}, u32[]{:S(2)}) copy-start(bf16[2,256,2304]{2,1,0:T(8,128)(2,1)} %param.12) | copy-start | bytes 7077892
  439.3 3.1 copy-start.38
  (3 other events, 2.2 us)
where the time goes:
time: 1020 us; the launch traced here: 1010 us
  blocking collectives  568 us (56%)
  matrix products  167 us (16%)
  local copies, waits for them, and re-layouts  93.1 us (9%)
  other arithmetic  77.3 us (8%)
  waiting for transfers between devices  65.6 us (6%)
  starting transfers between devices  38.2 us (4%)
    psum x1, blocking collectives, device_step(): lax.psum((dw_q, dw_k, dw_v, dw_o, dw_pre, dw_post, dq_norm, dk_norm), 'sp')  568 us
    all_to_all x4, waiting for transfers between devices, to_heads(): return lax.all_to_all(arr, 'sp', 2, 1, tiled=True)  38.6 us
    all_to_all x4, waiting for transfers between devices, to_tokens(): return lax.all_to_all(arr, 'sp', 1, 2, tiled=True)  27 us
  transfers between devices with their start and end apart: 8, of which 5 were waited for; matrix products, arithmetic and copies ran while one was open for 16% of the time, Pallas kernels for 0%

commit v1 on v0

v1 whole, which is shorter than its diff:
```python
import functools
import jax
import jax.numpy as jnp
from jax import lax
from jax.experimental import pallas as pl
from jax.experimental.pallas import tpu as pltpu
from jax.sharding import PartitionSpec as P

EPS = 1e-6
ROPE_BASE = 1000000.0
ROPE_SCALE = 8.0
NEG_BIG = -1e30
BLK = 256
BF = jnp.bfloat16
F32 = jnp.float32


def rms_scale(x_f32, weight):
    inv_rms = lax.rsqrt(jnp.mean(x_f32 * x_f32, axis=-1, keepdims=True) + EPS)
    return x_f32 * inv_rms * (1.0 + weight)


def pre_norm(x_f32, weight):
    return rms_scale(x_f32, weight).astype(BF)


def post_norm(proj, weight):
    return rms_scale(proj.astype(F32), weight)


def rope_tables(positions, head):
    half_dim = head // 2
    inv_freq = ROPE_BASE ** (-jnp.arange(half_dim, dtype=F32) * 2.0 / head)
    angles = (positions.astype(F32) / ROPE_SCALE)[:, None] * inv_freq[None, :]
    return jnp.cos(angles), jnp.sin(angles)


def norm_rope(head_bf, weight, cosines, sines):
    half_dim = head_bf.shape[-1] // 2
    normed = rms_scale(head_bf.astype(F32), weight)
    first = normed[..., :half_dim]
    second = normed[..., half_dim:]
    rotated = jnp.concatenate([first * cosines - second * sines, second * cosines + first * sines], axis=-1)
    return rotated.astype(BF)


def nt(lhs, rhs):
    return lax.dot_general(lhs, rhs, (((1,), (1,)), ((), ())), preferred_element_type=F32)


def nn(lhs, rhs):
    return lax.dot_general(lhs, rhs, (((1,), (0,)), ((), ())), preferred_element_type=F32)


def tn(lhs, rhs):
    return lax.dot_general(lhs, rhs, (((0,), (0,)), ((), ())), preferred_element_type=F32)


def fwd_kernel(q_ref, k_ref, v_ref, o_ref, lse_ref, s_scr, acc):
    seq, head = q_ref.shape
    scale = head ** -0.5
    lower = lax.broadcasted_iota(jnp.int32, (BLK, BLK), 0) >= lax.broadcasted_iota(jnp.int32, (BLK, BLK), 1)

    def fold(x, op):
        out = x[:, :128]
        for c in range(1, x.shape[1] // 128):
            out = op(out, x[:, c * 128:(c + 1) * 128])
        return out

    @pl.loop(0, seq // BLK)
    def _(i):
        rows = pl.ds(pl.multiple_of(i * BLK, BLK), BLK)
        q = q_ref[rows, :]
        s = jnp.where(lower, nt(q, k_ref[rows, :]) * scale, NEG_BIG)
        s_scr[:, rows] = s

        def pass1(j, m):
            cols = pl.ds(pl.multiple_of(j * BLK, BLK), BLK)
            s = nt(q, k_ref[cols, :]) * scale
            s_scr[:, cols] = s
            return jnp.maximum(m, fold(s, jnp.maximum))

        m = lax.fori_loop(0, i, pass1, fold(s, jnp.maximum))
        m = jnp.max(m, axis=1, keepdims=True)

        def pass2(j, l):
            cols = pl.ds(pl.multiple_of(j * BLK, BLK), BLK)
            p = jnp.exp(s_scr[:, cols] - m)
            s_scr[:, cols] = p
            return l + fold(p, jnp.add)

        l = lax.fori_loop(0, i + 1, pass2, jnp.zeros((BLK, 128), F32))
        l = jnp.sum(l, axis=1, keepdims=True)
        inv = 1.0 / l
        acc[...] = jnp.zeros_like(acc)

        @pl.loop(0, i + 1)
        def _(j):
            cols = pl.ds(pl.multiple_of(j * BLK, BLK), BLK)
            acc[...] += nn((s_scr[:, cols] * inv).astype(BF), v_ref[cols, :])

        o_ref[rows, :] = acc[...].astype(BF)
        lse_ref[rows, :] = m + jnp.log(l)


def attn_fwd(q, k, v):
    seq, head = q.shape
    pairs = seq * (seq + BLK) // 2
    return pl.pallas_call(
        fwd_kernel,
        out_shape=(jax.ShapeDtypeStruct((seq, head), BF), jax.ShapeDtypeStruct((seq, 1), F32)),
        in_specs=[pl.BlockSpec(memory_space=pltpu.VMEM)] * 3,
        out_specs=(pl.BlockSpec(memory_space=pltpu.VMEM),) * 2,
        scratch_shapes=[pltpu.VMEM((BLK, seq), F32), pltpu.VMEM((BLK, head), F32)],
        cost_estimate=pl.CostEstimate(flops=4 * pairs * head, bytes_accessed=8 * seq * head, transcendentals=pairs),
        compiler_params=pltpu.CompilerParams(vmem_limit_bytes=32 * 1024 * 1024),
        name='attn_fwd',
    )(q, k, v)


def bwd_kernel(q_ref, k_ref, v_ref, do_ref, lse_ref, dl_ref, dq_ref, dk_ref, dv_ref, dq_acc):
    seq, head = q_ref.shape
    scale = head ** -0.5
    upper = lax.broadcasted_iota(jnp.int32, (BLK, BLK), 0) <= lax.broadcasted_iota(jnp.int32, (BLK, BLK), 1)
    dq_acc[...] = jnp.zeros_like(dq_acc)
    dk_ref[...] = jnp.zeros_like(dk_ref)
    dv_ref[...] = jnp.zeros_like(dv_ref)

    @pl.loop(0, seq // BLK)
    def _(j):
        cols = pl.ds(pl.multiple_of(j * BLK, BLK), BLK)
        k = k_ref[cols, :]
        v = v_ref[cols, :]

        def step(i, masked):
            rows = pl.ds(pl.multiple_of(i * BLK, BLK), BLK)
            q = q_ref[rows, :]
            do = do_ref[rows, :]
            st = nt(k, q) * scale
            if masked:
                st = jnp.where(upper, st, NEG_BIG)
            pt = jnp.exp(st - lse_ref[0:1, rows])
            dpt = nt(v, do)
            dst = (pt * (dpt - dl_ref[0:1, rows]) * scale).astype(BF)
            dv_ref[cols, :] += nn(pt.astype(BF), do)
            dk_ref[cols, :] += nn(dst, q)
            dq_acc[rows, :] += tn(dst, k)

        step(j, True)

        @pl.loop(j + 1, seq // BLK)
        def _(i):
            step(i, False)

    dq_ref[...] = dq_acc[...].astype(BF)


def attn_bwd(q, k, v, do, lse, delta):
    seq, head = q.shape
    pairs = seq * (seq + BLK) // 2
    return pl.pallas_call(
        bwd_kernel,
        out_shape=(jax.ShapeDtypeStruct((seq, head), BF), jax.ShapeDtypeStruct((seq, head), F32), jax.ShapeDtypeStruct((seq, head), F32)),
        in_specs=[pl.BlockSpec(memory_space=pltpu.VMEM)] * 6,
        out_specs=(pl.BlockSpec(memory_space=pltpu.VMEM),) * 3,
        scratch_shapes=[pltpu.VMEM((seq, head), F32)],
        cost_estimate=pl.CostEstimate(flops=10 * pairs * head, bytes_accessed=20 * seq * head, transcendentals=pairs),
        compiler_params=pltpu.CompilerParams(vmem_limit_bytes=32 * 1024 * 1024),
        name='attn_bwd',
    )(q, k, v, do, lse, delta)


def solution(mesh):
    group = mesh.shape['sp']

    def device_step(x_in, dy_in, positions, w_q, w_k, w_v, w_o, w_pre, w_post, q_norm, k_norm):
        batch, seq_loc, width = x_in.shape
        head = q_norm.shape[0]
        heads = w_q.shape[1] // head
        kv_heads = w_k.shape[1] // head
        rep = group // kv_heads
        assert heads == group and rep == 2
        me = lax.axis_index('sp')
        kv = me // rep
        even = (me % rep) == 0
        swap = [(d, d ^ 1) for d in range(group)]

        def cols(w, index):
            return lax.dynamic_slice(w, (0, index * head), (w.shape[0], head))

        w_qkv = jnp.concatenate([cols(w_q, me), cols(w_k, kv), cols(w_v, kv)], axis=1)
        wo_mine = lax.dynamic_slice(w_o, (me * head, 0), (head, width))

        x_f32 = [x_in[b].astype(F32) for b in range(batch)]
        dy_f32 = [dy_in[b].astype(F32) for b in range(batch)]
        a_all, pre_pulls = [], []
        for b in range(batch):
            normed, pull = jax.vjp(pre_norm, x_f32[b], w_pre)
            pre_pulls.append(pull)
            a_all.append(lax.all_gather(normed, 'sp', axis=0, tiled=True))
        pos_all = lax.all_gather(positions, 'sp', axis=0, tiled=True)
        cosines, sines = rope_tables(pos_all, head)
        roper = functools.partial(norm_rope, cosines=cosines, sines=sines)

        saved = []
        dproj_all = []
        y_out, dw_post = [], 0.0
        for b in range(batch):
            qkv = nn(a_all[b], w_qkv).astype(BF)
            q_rot, q_pull = jax.vjp(roper, qkv[:, :head], q_norm)
            k_rot, k_pull = jax.vjp(roper, qkv[:, head:2 * head], k_norm)
            v_raw = qkv[:, 2 * head:]
            o, lse = attn_fwd(q_rot, k_rot, v_raw)
            saved.append((q_rot, k_rot, v_raw, o, lse, q_pull, k_pull))
            o_tok = lax.all_to_all(o, 'sp', 0, 1, tiled=True)
            proj = nn(o_tok, w_o).astype(BF)
            post, post_pull = jax.vjp(post_norm, proj, w_post)
            y_out.append((x_f32[b] + post).astype(BF))
            d_proj, dwp = post_pull(dy_f32[b])
            dw_post = dw_post + dwp
            dproj_all.append(lax.all_gather(d_proj, 'sp', axis=0, tiled=True))

        d_mine, dqkv_tok = [], []
        dq_norm = dk_norm = 0.0
        for b in range(batch):
            q_rot, k_rot, v_raw, o, lse, q_pull, k_pull = saved[b]
            d_o = nt(dproj_all[b], wo_mine).astype(BF)
            delta = jnp.sum(d_o.astype(F32) * o.astype(F32), axis=1)[None, :]
            dq_rot, dk_part, dv_part = attn_bwd(q_rot, k_rot, v_raw, d_o, lse.reshape(1, -1), delta)
            other = lax.ppermute(jnp.where(even, dv_part, dk_part), 'sp', swap)
            dkv = (jnp.where(even, dk_part, dv_part) + other).astype(BF)
            dq_proj, dqn = q_pull(dq_rot)
            dk_proj, dkn = k_pull(dkv)
            dq_norm = dq_norm + dqn
            dk_norm = dk_norm + jnp.where(even, dkn, 0.0)
            d_two = jnp.concatenate([dq_proj, jnp.where(even, dk_proj, dkv)], axis=1)
            d_mine.append(d_two)
            dqkv_tok.append(lax.all_to_all(d_two, 'sp', 0, 1, tiled=True))

        dw_o = sum(tn(saved[b][3], dproj_all[b]) for b in range(batch)).astype(BF)
        dw_o_all = lax.all_gather(dw_o, 'sp', axis=0, tiled=True)
        dw_two = sum(tn(a_all[b], d_mine[b]) for b in range(batch)).astype(BF)
        dw_all = lax.all_gather(dw_two, 'sp', axis=0, tiled=False)
        dw_all = dw_all.reshape(group, width, 2, head)
        dw_q_all = dw_all[:, :, 0].transpose(1, 0, 2).reshape(width, heads * head)
        dw_kv = dw_all[:, :, 1].reshape(kv_heads, rep, width, head)
        dw_k_all = dw_kv[:, 0].transpose(1, 0, 2).reshape(width, kv_heads * head)
        dw_v_all = dw_kv[:, 1].transpose(1, 0, 2).reshape(width, kv_heads * head)

        dx_out, dw_pre = [], 0.0
        for b in range(batch):
            d_tok = dqkv_tok[b].reshape(seq_loc, group, 2, head)
            dq_flat = d_tok[:, :, 0].reshape(seq_loc, heads * head)
            dkv_tok = d_tok[:, :, 1].reshape(seq_loc, kv_heads, rep, head)
            dk_flat = dkv_tok[:, :, 0].reshape(seq_loc, kv_heads * head)
            dv_flat = dkv_tok[:, :, 1].reshape(seq_loc, kv_heads * head)
            d_normed = (nt(dq_flat, w_q) + nt(dk_flat, w_k) + nt(dv_flat, w_v)).astype(BF)
            dx_norm, dwp = pre_pulls[b](d_normed)
            dw_pre = dw_pre + dwp
            dx_out.append((dy_f32[b] + dx_norm).astype(BF))
        small = lax.psum((dw_pre, dw_post, dq_norm, dk_norm), 'sp')
        return (jnp.stack(y_out), jnp.stack(dx_out), dw_q_all, dw_k_all, dw_v_all, dw_o_all) + small

    token_spec = P('dp', 'sp', None)
    return jax.shard_map(device_step, mesh=mesh,
                         in_specs=(token_spec, token_spec, P(('dp', 'sp')), P(None, None), P(None, None), P(None, None), P(None, None), P(None), P(None), P(None), P(None)),
                         out_specs=(token_spec, token_spec, P('dp', None), P('dp', None), P('dp', None), P('dp', None), P('dp'), P('dp'), P('dp'), P('dp')),
                         check_vma=False)
```

time: 1020 us -> 769 us (0.75)
  blocking collectives: 568 us -> 35.4 us
  waiting for transfers between devices: 65.6 us -> 266 us
  local copies, waits for them, and re-layouts: 93.1 us -> 193 us
  Pallas kernels: 0 us -> 75.6 us
  matrix products: 167 us -> 100 us
  other arithmetic: 77.3 us -> 51.1 us
  starting transfers between devices: 38.2 us -> 19 us
  between operations: 2.22 us -> 15.6 us
    psum x1, blocking collectives: 568 us -> 24.4 us  [device_step(): small = lax.psum((dw_pre, dw_post, dq_norm, dk_norm), 'sp')]
    all_gather x0 -> x6, waiting for transfers between devices: none -> 171 us  [the longest x2 95 us: device_step(): dproj_all.append(lax.all_gather(d_proj, 'sp', axis=0, tiled=True))]
    pallas_call x0 -> x4, Pallas kernels: none -> 75.6 us  [the longest x2 38 us: attn_fwd(): pl.pallas_call(fwd_kernel, out_shape=(jax.ShapeDtypeStruct((seq, head), B...]
    dot_general x24 -> x16, matrix products: 167 us -> 100 us  [the longest x8 37.9 us: nt(): lax.dot_general(lhs, rhs, (((1,), (1,)), ((), ())), preferred_element_typ...]
    transpose x0 -> x4, local copies, waits for them, and re-layouts: none -> 62 us  [the longest x1 40.6 us: device_step(): dw_q_all = dw_all[:, :, 0].transpose(1, 0, 2).reshape(width, heads * head)]
    slice x0 -> x13, local copies, waits for them, and re-layouts: none -> 45.7 us  [the longest x1 35.9 us: device_step(): dw_kv = dw_all[:, :, 1].reshape(kv_heads, rep, width, head)]
    unnamed x120 -> x131, local copies, waits for them, and re-layouts: 19.3 us -> 45.1 us
    all_to_all x8 -> x4, waiting for transfers between devices: 65.6 us -> 90.2 us  [the longest x2 82 us: device_step(): dqkv_tok.append(lax.all_to_all(d_two, 'sp', 0, 1, tiled=True))]
  transfers between devices with their start and end apart: 8 -> 12, of which waited for: 5 -> 8; matrix products, arithmetic and copies ran while one was open for 16% -> 17% of each run, Pallas kernels for 0% -> 7%
where the time goes in v1:
time: 769 us; the launch traced here: 756 us
  waiting for transfers between devices  266 us (35%)
  local copies, waits for them, and re-layouts  193 us (25%)
  matrix products  100 us (13%)
  Pallas kernels  75.6 us (10%)
  other arithmetic  51.1 us (7%)
  blocking collectives  35.4 us (5%)
  starting transfers between devices  19 us (2%)
  between operations  15.6 us (2%)
    all_gather x2, waiting for transfers between devices, device_step(): dproj_all.append(lax.all_gather(d_proj, 'sp', axis=0, tiled=True))  95 us
    all_to_all x2, waiting for transfers between devices, device_step(): dqkv_tok.append(lax.all_to_all(d_two, 'sp', 0, 1, tiled=True))  82 us
    all_gather x2, waiting for transfers between devices, device_step(): a_all.append(lax.all_gather(normed, 'sp', axis=0, tiled=True))  76.2 us
    unnamed x131, local copies, waits for them, and re-layouts  45.1 us
    transpose x1, local copies, waits for them, and re-layouts, device_step(): dw_q_all = dw_all[:, :, 0].transpose(1, 0, 2).reshape(width, heads * head)  40.6 us
    pallas_call x2, Pallas kernels, attn_fwd(): pl.pallas_call(fwd_kernel, out_shape=(jax.ShapeDtypeStruct((seq, head), B...  38 us
    dot_general x8, matrix products, nt(): lax.dot_general(lhs, rhs, (((1,), (1,)), ((), ())), preferred_element_typ...  37.9 us
    pallas_call x2, Pallas kernels, attn_bwd(): pl.pallas_call(bwd_kernel, out_shape=(jax.ShapeDtypeStruct((seq, head), B...  37.6 us
  transfers between devices with their start and end apart: 12, of which 8 were waited for; matrix products, arithmetic and copies ran while one was open for 17% of the time, Pallas kernels for 7%

profile of v1, /device:TPU:120, one launch (start us, length us, event | category | flops | bytes accessed | tf_op | source)
XLA Modules:
  0.0 756.1 jit_solution(16975456967940859426)
XLA Ops:
  7.3 2.3 fusion.35
  10.8 2.0 fusion.23
  13.8 11.0 %all-gather.1 = s32[8,1,256]{2,1,0:T(1,128)S(1)} all-gather(s32[1,1,256]{2,1,0:T(1,128)S(1)} %bitcast.141), channel_id=1, replica_groups=mesh['dp'=4,'sp'=8] {'sp'}, dimensions={0}, use_global_device_ids=true | all-gather | bytes 9216 | tf_op jit(solution)/shard_map/all_gather | solution.py:201
  27.6 2.4 constant_dynamic-slice_fusion.2
  30.0 35.5 %all-gather.11.cloned.1.call-done = bf16[2048,2304]{1,0:T(8,128)(2,1)} async-done(((bf16[256,2304]{1,0:T(8,128)(2,1)}), bf16[2048,2304]{1,0:T(8,128)(2,1)}) %all-gather.11.cloned.1.call-update) | async-done | bytes 9437200 | tf_op jit(solution)/shard_map/all_gather | solution.py:200
  65.5 10.3 %convolution_convert_fusion.2 = bf16[2048,768]{1,0:T(8,128)(2,1)S(1)} fusion(bf16[2048,2304]{1,0:T(8,128)(2,1)} %all-gather.11.cloned.1.call-done, bf16[2304,256]{1,0:T(8,128)(2,1)S(1)} %constant_dynamic-slice_fusion, bf16[2304,256]{1,0:T(8,128)(2,1)S(1)} %constant_dynamic-slice_fusion.1, bf16[2304,256]{1,0:T(8,128)(2,1)} %constant_dynamic-slice_fusion.2), kind=kOutput, calls=%fused_computation.60 | convolution fusion | flops 7259947008 | bytes 16121856 | tf_op jit(solution)/shard_map/dot_general | solution.py:52
  75.9 1.6 copy-done.15
  78.1 40.7 %all-gather.9.cloned.1.call-done = bf16[2048,2304]{1,0:T(8,128)(2,1)} async-done(((bf16[256,2304]{1,0:T(8,128)(2,1)}), bf16[2048,2304]{1,0:T(8,128)(2,1)}) %all-gather.9.cloned.1.call-update) | async-done | bytes 9437200 | tf_op jit(solution)/shard_map/all_gather | solution.py:200
  118.8 10.5 %convolution_convert_fusion.3 = bf16[2048,768]{1,0:T(8,128)(2,1)S(1)} fusion(bf16[2048,2304]{1,0:T(8,128)(2,1)} %all-gather.9.cloned.1.call-done, bf16[2304,256]{1,0:T(8,128)(2,1)S(1)} %constant_dynamic-slice_fusion, bf16[2304,256]{1,0:T(8,128)(2,1)S(1)} %constant_dynamic-slice_fusion.1, bf16[2304,256]{1,0:T(8,128)(2,1)} %constant_dynamic-slice_fusion.2), kind=kOutput, calls=%fused_computation.61 | convolution fusion | flops 7259947008 | bytes 16121856 | tf_op jit(solution)/shard_map/dot_general | solution.py:52
  130.0 1.6 fusion.20
  131.7 6.2 fusion.98
  138.1 19.0 %attn_fwd.3 = (bf16[2048,256]{1,0:T(8,128)(2,1)S(1)}, f32[2048,1]{1,0:T(8,128)S(1)}) custom-call(bf16[2048,256]{1,0:T(8,128)(2,1)S(1)} %pad_maximum_fusion.9.q_ref, bf16[2048,256]{1,0:T(8,128)(2,1)S(1)} %pad_maximum_fusion.10.k_ref, bf16[2048,256]{1,0:T(8,128)(2,1)S(1)} %slice.133.v_ref), custom_call_target="tpu_custom_call" | custom-call | flops 2415919104 | bytes 4194304 | tf_op jit(solution)/shard_map/attn_fwd/pallas_call | solution.py:109
  159.4 4.9 all-to-all-start.1
  166.1 19.0 %attn_fwd.2 = (bf16[2048,256]{1,0:T(8,128)(2,1)S(1)}, f32[2048,1]{1,0:T(8,128)S(1)}) custom-call(bf16[2048,256]{1,0:T(8,128)(2,1)S(1)} %pad_maximum_fusion.7.q_ref, bf16[2048,256]{1,0:T(8,128)(2,1)S(1)} %pad_maximum_fusion.8.k_ref, bf16[2048,256]{1,0:T(8,128)(2,1)S(1)} %slice.126.v_ref), custom_call_target="tpu_custom_call" | custom-call | flops 2415919104 | bytes 4194304 | tf_op jit(solution)/shard_map/attn_fwd/pallas_call | solution.py:109
  187.5 4.7 all-to-all-start
  192.3 7.7 %fusion.33 = (f32[256]{0:T(256)S(1)}, bf16[256,2304]{1,0:T(8,128)(2,1)}) fusion(bf16[256,2048]{0,1:T(8,128)(2,1)} %bitcast.12, bf16[2048,2304]{1,0:T(8,128)(2,1)} %param.17), kind=kOutput, calls=%fused_computation.96 | convolution fusion | flops 2418278144 | bytes 11666432 | tf_op jit(solution)/shard_map/dot_general | solution.py:52
  200.0 8.2 %all-to-all-done = bf16[8,256,256]{1,2,0:T(8,128)(2,1)} async-done(((bf16[8,256,256]{1,2,0:T(8,128)(2,1)}), bf16[8,256,256]{1,2,0:T(8,128)(2,1)}, u32[]{:S(2)}, u32[]{:S(2)}) %all-to-all-start) | async-done | bytes 1048608 | tf_op jit(solution)/shard_map/all_to_all | solution.py:215
  208.2 6.9 fusion.31
  215.1 1.8 fusion.28
  216.9 3.7 fusion.90
  221.6 49.5 %all-gather.13.cloned.1.call-done = bf16[2048,2304]{1,0:T(8,128)(2,1)} async-done(((bf16[256,2304]{1,0:T(8,128)(2,1)}), bf16[2048,2304]{1,0:T(8,128)(2,1)}) %all-gather.13.cloned.1.call-update) | async-done | bytes 9437200 | tf_op jit(solution)/shard_map/all_gather | solution.py:221
  271.1 7.7 %fusion.143 = f32[256,2304]{1,0:T(8,128)} fusion(bf16[2048,256]{1,0:T(8,128)(2,1)S(1)} %get-tuple-element.20, bf16[2048,2304]{1,0:T(8,128)(2,1)} %all-gather.13.cloned.1.call-done), kind=kOutput, calls=%fused_computation.252 | convolution fusion | flops 2415919104 | bytes 12845056 | tf_op jit(solution)/shard_map/dot_general | solution.py:56
  278.9 45.5 %all-gather.15.cloned.1.call-done = bf16[2048,2304]{1,0:T(8,128)(2,1)} async-done(((bf16[256,2304]{1,0:T(8,128)(2,1)}), bf16[2048,2304]{1,0:T(8,128)(2,1)}) %all-gather.15.cloned.1.call-update) | async-done | bytes 9437200 | tf_op jit(solution)/shard_map/all_gather | solution.py:221
  324.3 7.8 %fusion.4 = bf16[256,2304]{1,0:T(8,128)(2,1)} fusion(f32[256,2304]{1,0:T(8,128)} %fusion.143, bf16[2048,256]{1,0:T(8,128)(2,1)S(1)} %get-tuple-element.21, bf16[2048,2304]{1,0:T(8,128)(2,1)} %all-gather.15.cloned.1.call-done), kind=kOutput, calls=%fused_computation.30 | convolution fusion | flops 2417098752 | bytes 14024704 | tf_op jit(solution)/shard_map/dot_general | solution.py:56
  333.8 1.6 reduce
  335.4 6.8 multiply_reduce_fusion.1
  342.3 18.9 %attn_bwd.2 = (bf16[2048,256]{1,0:T(8,128)(2,1)S(1)}, f32[2048,256]{1,0:T(8,128)S(1)}, f32[2048,256]{1,0:T(8,128)S(1)}) custom-call(bf16[2048,256]{1,0:T(8,128)(2,1)S(1)} %copy-done.9, bf16[2048,256]{1,0:T(8,128)(2,1)S(1)} %copy-done.7, bf16[2048,256]{1,0:T(8,128)(2,1)S(1)} %copy-done.5, bf16[2048,256]{1,0:T(8,128)(2,1)S(1)} %get-tuple-element.157.do_ref, ...), custom_call_target="tpu_custom_call" | custom-call | flops 6039797760 | bytes 10485760 | tf_op jit(solution)/shard_map/attn_bwd/pallas_call | solution.py:161
  361.9 4.4 multiply_reduce_fusion
  366.3 18.7 %attn_bwd.3 = (bf16[2048,256]{1,0:T(8,128)(2,1)S(1)}, f32[2048,256]{1,0:T(8,128)S(1)}, f32[2048,256]{1,0:T(8,128)S(1)}) custom-call(bf16[2048,256]{1,0:T(8,128)(2,1)S(1)} %copy-done.3, bf16[2048,256]{1,0:T(8,128)(2,1)S(1)} %copy-done.1, bf16[2048,256]{1,0:T(8,128)(2,1)S(1)} %slice.133.v_ref, bf16[2048,256]{1,0:T(8,128)(2,1)S(1)} %get-tuple-element.159.do_ref, ...), custom_call_target="tpu_custom_call" | custom-call | flops 6039797760 | bytes 10485760 | tf_op jit(solution)/shard_map/attn_bwd/pallas_call | solution.py:161
  386.5 3.0 collective-permute-done.1
  390.1 5.4 fusion.109
  395.5 3.7 fusion.43
  399.4 1.6 fusion.45
  401.0 2.0 fusion.118
  403.1 5.1 fusion.133
  408.3 6.4 add_convert_fusion
  414.7 1.7 pad_maximum_fusion.3
  416.4 2.4 copy.69
  418.8 3.8 all-to-all-start.2
  422.6 2.7 pad_maximum_fusion.4
  425.3 3.9 copy.74
  429.2 41.5 %all-to-all-done.2 = bf16[8,256,512]{1,2,0:T(8,128)(2,1)S(1)} async-done(((bf16[8,256,512]{1,2,0:T(8,128)(2,1)}), bf16[8,256,512]{1,2,0:T(8,128)(2,1)S(1)}, u32[]{:S(2)}, u32[]{:S(2)}) %all-to-all-start.2) | async-done | bytes 2097184 | tf_op jit(solution)/shard_map/all_to_all | solution.py:238
  472.0 4.3 all-to-all-start.3
  476.3 3.0 pad_maximum_fusion.1
  483.4 2.0 copy.72
  485.4 40.5 %all-to-all-done.3 = bf16[8,256,512]{1,2,0:T(8,128)(2,1)S(1)} async-done(((bf16[8,256,512]{1,2,0:T(8,128)(2,1)}), bf16[8,256,512]{1,2,0:T(8,128)(2,1)S(1)}, u32[]{:S(2)}, u32[]{:S(2)}) %all-to-all-start.3) | async-done | bytes 2097184 | tf_op jit(solution)/shard_map/all_to_all | solution.py:238
  528.8 6.8 fusion.142
  537.2 4.0 fusion.3
  541.2 7.3 fusion.141
  550.4 5.6 fusion.24
  556.0 24.4 %all-reduce.8 = (f32[2304]{0:T(1024)}, f32[2304]{0:T(1024)}, f32[256]{0:T(256)}, f32[256]{0:T(256)}) all-reduce(f32[2304]{0:T(1024)S(1)} %add.224, f32[2304]{0:T(1024)S(1)} %add.225, f32[256]{0:T(256)S(1)} %add.226, f32[256]{0:T(256)S(1)} %select_add_fusion), channel_id=1, replica_groups=mesh['dp'=4,'sp'=8] {'sp'}, use_global_device_ids=true, to_apply=%region_20.21 | all-reduce | flops 5120 | bytes 40960 | tf_op jit(solution)/shard_map/psum | solution.py:261
  580.4 4.0 fusion.92
  584.4 1.6 pad_maximum_fusion.2
  586.0 26.4 %reshape.233 = bf16[8,2304,2,256]{3,2,1,0:T(2,128)(2,1)} reshape(bf16[18432,512]{1,0:T(8,128)(2,1)} %all-gather.19.cloned.1.call-done) | data formatting | bytes 37748736 | tf_op jit(solution)/shard_map/reshape | solution.py:244
  612.5 35.9 %fusion.136 = (bf16[8,2304,1,256]{3,2,1,0:T(2,128)(2,1)S(1)}, bf16[8,2304,1,256]{3,2,1,0:T(2,128)(2,1)}) fusion(bf16[8,2304,2,256]{3,2,1,0:T(2,128)(2,1)} %reshape.233), kind=kLoop, calls=%fused_computation.245 | loop fusion | bytes 37748736 | tf_op jit(solution)/shard_map/slice | solution.py:246
  648.4 4.8 copy.91
  653.2 8.1 %slice_bitcast_fusion = (bf16[2304,4,256]{2,0,1:T(8,128)(2,1)}, bf16[2304,4,256]{2,0,1:T(8,128)(2,1)}) fusion(bf16[4,2,2304,256]{3,2,1,0:T(8,128)(2,1)} %bitcast.115), kind=kLoop, calls=%fused_computation | loop fusion | bytes 18874368 | tf_op jit(solution)/shard_map/transpose | solution.py:248
  661.3 6.6 copy.82
  667.9 6.6 copy.85
  674.5 6.6 copy.81
  681.1 6.6 copy.84
  687.7 40.6 %copy.92 = bf16[8,2304,1,256]{1,3,0,2:T(8,128)(2,1)} copy(bf16[8,2304,1,256]{3,2,1,0:T(2,128)(2,1)} %get-tuple-element.89) | data formatting | bytes 18874368 | tf_op jit(solution)/shard_map/transpose | solution.py:245
  728.4 12.6 %copy.83 = bf16[2304,2048]{1,0:T(8,128)(2,1)} copy(bf16[2304,2048]{0,1:T(8,128)(2,1)} %bitcast.116) | data formatting | bytes 18874368
  741.0 8.0 %copy.94 = bf16[2048,2304]{1,0:T(8,128)(2,1)} copy(bf16[2048,2304]{1,0:T(8,128)(2,1)} %all-gather.17.cloned.1.call-done) | data formatting | bytes 18874368
  (204 shorter events, 29.8 us)
Async XLA Ops:
  7.2 3.7 copy-start.12
  7.2 58.3 %all-gather.11.cloned.1.call-start = ((), (), s32[]{:S(2)}) async-start(), calls=%async_computation.5 | async-start | bytes 10616832 | tf_op jit(solution)/shard_map/all_gather | solution.py:200
  9.6 3.2 copy-start.37
  10.1 2.7 copy-start.39
  10.8 2.0 copy-start.34
  12.9 12.0 %copy-start.46 = (f32[256]{0:T(256)S(1)}, f32[256]{0:T(256)}, u32[]{:S(2)}) copy-start(f32[256]{0:T(256)} %param.20) | copy-start | bytes 3076
  12.9 12.0 %copy-start.47 = (f32[256]{0:T(256)S(1)}, f32[256]{0:T(256)}, u32[]{:S(2)}) copy-start(f32[256]{0:T(256)} %param.21) | copy-start | bytes 3076
  13.0 105.9 %all-gather.9.cloned.1.call-start = ((), (), s32[]{:S(2)}) async-start(), calls=%async_computation.4 | async-start | bytes 10616832 | tf_op jit(solution)/shard_map/all_gather | solution.py:200
  118.8 11.2 %copy-start.16 = (bf16[2048,768]{1,0:T(8,128)(2,1)S(1)}, bf16[2048,768]{1,0:T(8,128)(2,1)}, u32[]{:S(2)}) copy-start(bf16[2048,768]{1,0:T(8,128)(2,1)} %copy-done.15) | copy-start | bytes 9437188
  129.3 2.3 copy-start.18
  138.0 19.2 %copy-start = (bf16[2048,256]{1,0:T(8,128)(2,1)}, bf16[2048,256]{1,0:T(8,128)(2,1)S(1)}, u32[]{:S(2)}) copy-start(bf16[2048,256]{1,0:T(8,128)(2,1)S(1)} %pad_maximum_fusion.10.k_ref) | copy-start | bytes 3145732
  138.1 19.1 %copy-start.2 = (bf16[2048,256]{1,0:T(8,128)(2,1)}, bf16[2048,256]{1,0:T(8,128)(2,1)S(1)}, u32[]{:S(2)}) copy-start(bf16[2048,256]{1,0:T(8,128)(2,1)S(1)} %pad_maximum_fusion.9.q_ref) | copy-start | bytes 3145732
  158.1 6.2 copy-start.36
  159.4 28.0 %all-to-all-start.1 = ((bf16[8,256,256]{1,2,0:T(8,128)(2,1)}), bf16[8,256,256]{1,2,0:T(8,128)(2,1)}, u32[]{:S(2)}, u32[]{:S(2)}) async-start(bf16[8,256,256]{1,2,0:T(8,128)(2,1)} %copy.67), calls=%async_computation.1 | async-start | bytes 2097152 | tf_op jit(solution)/shard_map/all_to_all | solution.py:215
  165.8 19.4 %copy-start.4 = (bf16[2048,256]{1,0:T(8,128)(2,1)}, bf16[2048,256]{1,0:T(8,128)(2,1)S(1)}, u32[]{:S(2)}) copy-start(bf16[2048,256]{1,0:T(8,128)(2,1)S(1)} %slice.126.v_ref) | copy-start | bytes 3145732
  166.0 19.2 %copy-start.6 = (bf16[2048,256]{1,0:T(8,128)(2,1)}, bf16[2048,256]{1,0:T(8,128)(2,1)S(1)}, u32[]{:S(2)}) copy-start(bf16[2048,256]{1,0:T(8,128)(2,1)S(1)} %pad_maximum_fusion.8.k_ref) | copy-start | bytes 3145732
  166.1 19.1 %copy-start.8 = (bf16[2048,256]{1,0:T(8,128)(2,1)}, bf16[2048,256]{1,0:T(8,128)(2,1)S(1)}, u32[]{:S(2)}) copy-start(bf16[2048,256]{1,0:T(8,128)(2,1)S(1)} %pad_maximum_fusion.7.q_ref) | copy-start | bytes 3145732
  187.5 20.7 %all-to-all-start = ((bf16[8,256,256]{1,2,0:T(8,128)(2,1)}), bf16[8,256,256]{1,2,0:T(8,128)(2,1)}, u32[]{:S(2)}, u32[]{:S(2)}) async-start(bf16[8,256,256]{1,2,0:T(8,128)(2,1)} %copy.65), calls=%async_computation | async-start | bytes 2097152 | tf_op jit(solution)/shard_map/all_to_all | solution.py:215
  192.2 78.9 %all-gather.13.cloned.1.call-start = ((), (), s32[]{:S(2)}) async-start(), calls=%async_computation.6 | async-start | bytes 10616832 | tf_op jit(solution)/shard_map/all_gather | solution.py:221
  208.2 6.9 copy-start.20
  208.2 6.9 copy-start.21
  215.1 1.8 copy-start.13
  220.7 103.6 %all-gather.15.cloned.1.call-start = ((), (), s32[]{:S(2)}) async-start(), calls=%async_computation.7 | async-start | bytes 10616832 | tf_op jit(solution)/shard_map/all_gather | solution.py:221
  221.4 364.6 %all-gather.17.cloned.1.call-start = ((), (), s32[]{:S(2)}) async-start(), calls=%async_computation.8 | async-start | bytes 10616832 | tf_op jit(solution)/shard_map/all_gather | solution.py:241
  332.2 253.9 %all-gather.19.cloned.1.call-start = ((), (), s32[]{:S(2)}) async-start(), calls=%async_computation.9 | async-start | bytes 21233664 | tf_op jit(solution)/shard_map/all_gather | solution.py:243
  335.4 6.9 copy-start.5
  335.4 6.9 copy-start.7
  335.4 6.9 copy-start.9
  335.4 26.5 %slice-start.4 = ((s8[9437184]{0:T(1024)(128)(4,1)}), s8[4194304]{0:T(1024)(128)(4,1)S(1)}, s32[]{:S(2)}) async-start(s8[9437184]{0:T(1024)(128)(4,1)} %bitcast.123), calls=%async_computation.14 | async-start | bytes 8388608
  335.4 26.5 %slice-start.5 = ((s8[9437184]{0:T(1024)(128)(4,1)}), s8[4194304]{0:T(1024)(128)(4,1)S(1)}, s32[]{:S(2)}) async-start(s8[9437184]{0:T(1024)(128)(4,1)} %bitcast.123), calls=%async_computation.15 | async-start | bytes 8388608
  342.3 19.6 %slice-start.6 = ((s8[9437184]{0:T(1024)(128)(4,1)}), s8[1048576]{0:T(1024)(128)(4,1)S(1)}, s32[]{:S(2)}) async-start(s8[9437184]{0:T(1024)(128)(4,1)} %bitcast.123), calls=%async_computation.16 | async-start | bytes 2097152
  361.5 4.8 copy-start.1
  361.5 4.8 copy-start.3
  361.5 24.4 %collective-permute-start = (f32[2048,256]{1,0:T(8,128)S(1)}, f32[2048,256]{1,0:T(8,128)S(1)}, u32[]{:S(2)}, u32[]{:S(2)}) collective-permute-start(f32[2048,256]{1,0:T(8,128)S(1)} %broadcast_select_fusion.1), channel_id=1, source_target_pairs={{0,1},{1,0},{2,3},{3,2},{4,5},{5,4},{6,7},{7,6},{8,9},{9,8},{10,11... | collective-permute-start | bytes 6291464 | tf_op jit(solution)/shard_map/ppermute | solution.py:230
  385.3 4.3 collective-permute-start.1
  390.1 5.4 copy-start.17
  390.1 5.4 copy-start.19
  395.5 7.5 slice-start.12
  395.5 7.5 slice-start.13
  399.4 3.7 slice-start.14
  401.0 2.0 copy-start.26
  401.0 7.2 slice-start.9
  403.0 5.2 copy-start.28
  403.0 5.2 copy-start.27
  403.1 5.2 slice-start.10
  403.1 5.2 slice-start.11
  418.8 51.9 %all-to-all-start.2 = ((bf16[8,256,512]{1,2,0:T(8,128)(2,1)}), bf16[8,256,512]{1,2,0:T(8,128)(2,1)S(1)}, u32[]{:S(2)}, u32[]{:S(2)}) async-start(bf16[8,256,512]{1,2,0:T(8,128)(2,1)} %copy.69), calls=%async_computation.2 | async-start | bytes 4194304 | tf_op jit(solution)/shard_map/all_to_all | solution.py:238
  429.2 47.1 %copy-start.25 = (bf16[1,256,2304]{2,1,0:T(8,128)(2,1)S(1)}, bf16[1,256,2304]{2,1,0:T(8,128)(2,1)}, u32[]{:S(2)}) copy-start(bf16[1,256,2304]{2,1,0:T(8,128)(2,1)} %get-tuple-element.100) | copy-start | bytes 3538948
  472.0 53.9 %all-to-all-start.3 = ((bf16[8,256,512]{1,2,0:T(8,128)(2,1)}), bf16[8,256,512]{1,2,0:T(8,128)(2,1)S(1)}, u32[]{:S(2)}, u32[]{:S(2)}) async-start(bf16[8,256,512]{1,2,0:T(8,128)(2,1)} %copy.74), calls=%async_computation.3 | async-start | bytes 4194304 | tf_op jit(solution)/shard_map/all_to_all | solution.py:238
  476.3 3.1 copy-start.24
  527.0 8.6 %slice-start = ((s8[4718592]{0:T(1024)(128)(4,1)}), s8[524288]{0:T(1024)(128)(4,1)S(1)}, s32[]{:S(2)}) async-start(s8[4718592]{0:T(1024)(128)(4,1)} %bitcast.117), calls=%async_computation.10 | async-start | bytes 1048576
  528.8 6.8 slice-start.1
  537.2 4.0 copy-start.32
  537.2 11.4 %slice-start.2 = ((s8[4718592]{0:T(1024)(128)(4,1)}), s8[4194304]{0:T(1024)(128)(4,1)S(1)}, s32[]{:S(2)}) async-start(s8[4718592]{0:T(1024)(128)(4,1)} %bitcast.119), calls=%async_computation.12 | async-start | bytes 8388608
  537.2 13.0 %slice-start.7 = ((s8[4718592]{0:T(1024)(128)(4,1)}), s8[4194304]{0:T(1024)(128)(4,1)S(1)}, s32[]{:S(2)}) async-start(s8[4718592]{0:T(1024)(128)(4,1)} %bitcast.129), calls=%async_computation.17 | async-start | bytes 8388608
  541.2 9.0 %copy-start.22 = (f32[256,2304]{1,0:T(8,128)}, f32[256,2304]{1,0:T(8,128)S(1)}, u32[]{:S(2)}) copy-start(f32[256,2304]{1,0:T(8,128)S(1)} %fusion.3) | copy-start | bytes 7077892
  541.2 7.4 slice-start.3
  541.2 8.9 %slice-start.8 = ((s8[4718592]{0:T(1024)(128)(4,1)}), s8[524288]{0:T(1024)(128)(4,1)S(1)}, s32[]{:S(2)}) async-start(s8[4718592]{0:T(1024)(128)(4,1)} %bitcast.129), calls=%async_computation.18 | async-start | bytes 1048576
  548.6 1.7 copy-start.33
  548.6 1.7 copy-start.35
  548.6 1.7 copy-start.38
  548.7 1.7 copy-start.40
  550.4 30.0 %copy-start.42 = (f32[256]{0:T(256)S(1)}, f32[256]{0:T(256)}, u32[]{:S(2)}) copy-start(f32[256]{0:T(256)} %copy-done.41) | copy-start | bytes 3076
  550.4 30.0 %copy-start.44 = (f32[256]{0:T(256)S(1)}, f32[256]{0:T(256)}, u32[]{:S(2)}) copy-start(f32[256]{0:T(256)} %copy-done.43) | copy-start | bytes 3076
  (11 other events, 12.6 us)
Sparse Core Ops, SparseCore 0:
  13.1 52.3 all-gather.10
  67.7 51.1 all-gather.8
  220.8 50.2 all-gather.12
  273.2 51.1 all-gather.14
  332.3 51.1 all-gather.16
  414.8 134.3 all-gather.18

commit v2 on v1

v2 whole, which is shorter than its diff:
```python
import functools
import math
import jax
import jax.numpy as jnp
from jax import lax
from jax.experimental import pallas as pl
from jax.experimental.pallas import tpu as pltpu
from jax.sharding import PartitionSpec as P

EPS = 1e-6
ROPE_BASE = 1000000.0
ROPE_SCALE = 8.0
NEG_BIG = -1e30
HALF_PI = (1.5625, 0.0081787109375, 0.00011730194091796875, 3.129243850708008e-07, 9.920935796805404e-10)
BWD_BLK = 256
BF = jnp.bfloat16
F32 = jnp.float32
MESH = pl.DeviceIdType.MESH


def rms_scale(x_f32, weight):
    inv_rms = lax.rsqrt(jnp.mean(x_f32 * x_f32, axis=-1, keepdims=True) + EPS)
    return x_f32 * inv_rms * (1.0 + weight)


def pre_norm(x_f32, weight):
    return rms_scale(x_f32, weight).astype(BF)


def post_norm(proj, weight):
    return rms_scale(proj.astype(F32), weight)


def norm_rope(head_bf, weight, cosines, sines):
    half_dim = head_bf.shape[-1] // 2
    normed = rms_scale(head_bf.astype(F32), weight)
    first = normed[..., :half_dim]
    second = normed[..., half_dim:]
    rotated = jnp.concatenate([first * cosines - second * sines, second * cosines + first * sines], axis=-1)
    return rotated.astype(BF)


def nt(lhs, rhs):
    return lax.dot_general(lhs, rhs, (((1,), (1,)), ((), ())), preferred_element_type=F32)


def nn(lhs, rhs):
    return lax.dot_general(lhs, rhs, (((1,), (0,)), ((), ())), preferred_element_type=F32)


def tn(lhs, rhs):
    return lax.dot_general(lhs, rhs, (((0,), (0,)), ((), ())), preferred_element_type=F32)


def others_barrier(group, me):
    barrier = pltpu.get_barrier_semaphore()
    for step in range(1, group):
        pl.semaphore_signal(barrier, inc=1, device_id={'sp': lax.rem(me + step, group)}, device_id_type=MESH)
    pl.semaphore_wait(barrier, group - 1)


def block_of(index, size):
    return pl.ds(pl.multiple_of(index * size, size), size)


def fold(x, op):
    out = x[:, :128]
    for c in range(1, x.shape[1] // 128):
        out = op(out, x[:, c * 128:(c + 1) * 128])
    return out


class Attention:
    def __init__(self, group, me, q_ref, k_ref, v_ref, o_ref, lse_ref, tok_ref, s_scr, acc, send_sem, recv_sem):
        self.group, self.me = group, me
        self.refs = q_ref, k_ref, v_ref, o_ref, lse_ref, tok_ref, s_scr, acc
        self.sems = send_sem, recv_sem
        self.blk, self.head = acc.shape
        self.mine = block_of(me, self.head)

    def copy_to(self, step):
        o_ref, tok_ref = self.refs[3], self.refs[5]
        peer = lax.rem(self.me + step, self.group)
        return pltpu.make_async_remote_copy(
            src_ref=o_ref.at[block_of(peer, self.blk), :],
            dst_ref=tok_ref.at[:, self.mine],
            send_sem=self.sems[0].at[step],
            recv_sem=self.sems[1].at[step],
            device_id={'sp': peer},
            device_id_type=MESH,
        )

    def blocks(self, first, last):
        q_ref, k_ref, v_ref, o_ref, lse_ref, _, s_scr, acc = self.refs
        blk, head = self.blk, self.head
        scale = head ** -0.5
        lower = lax.broadcasted_iota(jnp.int32, (blk, blk), 0) >= lax.broadcasted_iota(jnp.int32, (blk, blk), 1)

        @pl.loop(first, last)
        def _(step):
            i = lax.rem(self.me + step, self.group)
            rows = block_of(i, blk)
            q = q_ref[rows, :]
            s = jnp.where(lower, nt(q, k_ref[rows, :]) * scale, NEG_BIG)
            s_scr[:, rows] = s

            def pass1(j, m):
                cols = block_of(j, blk)
                s = nt(q, k_ref[cols, :]) * scale
                s_scr[:, cols] = s
                return jnp.maximum(m, fold(s, jnp.maximum))

            m = lax.fori_loop(0, i, pass1, fold(s, jnp.maximum))
            m = jnp.max(m, axis=1, keepdims=True)

            @pl.when(step > 1)
            def _():
                self.copy_to(step - 1).start()

            def pass2(j, l):
                cols = block_of(j, blk)
                p = jnp.exp(s_scr[:, cols] - m)
                s_scr[:, cols] = p
                return l + fold(p, jnp.add)

            l = lax.fori_loop(0, i + 1, pass2, jnp.zeros((blk, min(128, blk)), F32))
            l = jnp.sum(l, axis=1, keepdims=True)
            inv = 1.0 / l
            acc[...] = jnp.zeros_like(acc)

            @pl.loop(0, i + 1)
            def _(j):
                cols = block_of(j, blk)
                acc[...] += nn((s_scr[:, cols] * inv).astype(BF), v_ref[cols, :])

            o_ref[rows, :] = acc[...].astype(BF)
            lse_ref[rows, :] = m + jnp.log(l)

    def flush(self):
        o_ref, tok_ref = self.refs[3], self.refs[5]
        tok_ref[:, self.mine] = o_ref[block_of(self.me, self.blk), :]
        self.copy_to(self.group - 1).start()

    def finish(self):
        @pl.loop(1, self.group)
        def _(step):
            self.copy_to(step).wait()


def fwd_kernel(group, *refs):
    me = lax.axis_index('sp')
    others_barrier(group, me)
    attention = Attention(group, me, *refs)
    attention.blocks(0, group)
    attention.flush()
    attention.finish()


def attn_scratch(group, blk, seq, head):
    return [pltpu.VMEM((blk, seq), F32), pltpu.VMEM((blk, head), F32), pltpu.SemaphoreType.DMA((group,)), pltpu.SemaphoreType.DMA((group,))]


def attn_outs(group, blk, seq, head):
    return jax.ShapeDtypeStruct((seq, head), BF), jax.ShapeDtypeStruct((seq, 1), F32), jax.ShapeDtypeStruct((blk, group * head), BF)


def attn_fwd(q, k, v, group, cid):
    seq, head = q.shape
    blk = seq // group
    pairs = seq * (seq + blk) // 2
    return pl.pallas_call(
        functools.partial(fwd_kernel, group),
        out_shape=attn_outs(group, blk, seq, head),
        in_specs=[pl.BlockSpec(memory_space=pltpu.VMEM)] * 3,
        out_specs=(pl.BlockSpec(memory_space=pltpu.VMEM),) * 3,
        scratch_shapes=attn_scratch(group, blk, seq, head),
        cost_estimate=pl.CostEstimate(flops=24 * pairs * head, bytes_accessed=8 * seq * head, transcendentals=pairs),
        compiler_params=pltpu.CompilerParams(vmem_limit_bytes=32 * 1024 * 1024, collective_id=cid, has_side_effects=True),
        name='attn_fwd',
    )(q, k, v)


RIGHT_0, RIGHT_1, RIGHT_F, LEFT_1, LEFT_0, LEFT_F, SIB, SIB_L0, SIB_L1, SIB_R0, SIB_R1, SIB_O0, SIB_O1 = range(13)


def table_block(pos_row, freq_row):
    size = pos_row.shape[1]
    eye = lax.broadcasted_iota(jnp.int32, (size, size), 0) == lax.broadcasted_iota(jnp.int32, (size, size), 1)
    pos = jnp.sum(jnp.where(eye, jnp.broadcast_to(pos_row, (size, size)), 0.0), axis=1, keepdims=True)
    angle = pos / ROPE_SCALE * freq_row
    turn = jnp.floor(angle * (2.0 / math.pi) + 0.5)
    rest = angle
    for part in HALF_PI:
        rest = rest - turn * part
    sq = rest * rest
    sin_r = rest + rest * sq * (-1.6666654611e-1 + sq * (8.3321608736e-3 + sq * -1.9515295891e-4))
    cos_r = 1.0 - 0.5 * sq + sq * sq * (4.166664568298827e-2 + sq * (-1.388731625493765e-3 + sq * 2.443315711809948e-5))
    quarter = turn - 4.0 * jnp.floor(turn * 0.25)
    odd = (quarter == 1.0) | (quarter == 3.0)
    cosines = jnp.where(odd, sin_r, cos_r)
    sines = jnp.where(odd, cos_r, sin_r)
    cosines = jnp.where((quarter == 1.0) | (quarter == 2.0), -cosines, cosines)
    sines = jnp.where(quarter >= 2.0, -sines, sines)
    return cosines, sines


def first_kernel(group, x_ref, pos_ref, freq_ref, wpre_ref, qn_ref, kn_ref, wq_ref, wk_ref, wv_ref,
                 full_ref, qr_ref, kr_ref, v_ref, qw_ref, kw_ref, cos_ref, sin_ref, o_ref, lse_ref, tok_ref,
                 buf, w_ref, pos_all, s_scr, acc, o_send, o_recv, send_sem, recv_sem, out_sem, w_sem, p_send, p_recv):
    batch, blk, _ = x_ref.shape
    head = qn_ref.shape[1]
    chips = group // 2
    me = lax.axis_index('sp')
    core, chip = lax.rem(me, 2), me // 2

    def device(chip_step, other):
        return 2 * lax.rem(chip + chips + chip_step, chips) + (1 - core if other else core)

    right, left, far, sib = device(1, False), device(-1, False), device(2, False), device(0, True)
    half = blk // 2
    halves = [pl.ds(0, half), pl.ds(half, half)]
    loads = [pltpu.make_async_copy(ref.at[:, block_of(index, head)], w_ref.at[:, pl.ds(place * head, head)], w_sem.at[place])
             for place, (ref, index) in enumerate(((wq_ref, me), (wk_ref, chip), (wv_ref, chip)))]
    for load in loads:
        load.start()

    @pl.loop(0, batch * 4)
    def _(t):
        rows = block_of(lax.rem(t, 4), blk // 4)
        x = x_ref[t // 4, rows, :].astype(F32)
        inv = lax.rsqrt(jnp.mean(x * x, axis=-1, keepdims=True) + EPS)
        buf[t // 4, me, rows, :] = (x * inv * (1.0 + wpre_ref[...])).astype(BF)

    others_barrier(group, me)

    def pos_copy(step):
        return pltpu.make_async_remote_copy(
            src_ref=pos_ref,
            dst_ref=pos_all.at[me],
            send_sem=p_send.at[step],
            recv_sem=p_recv.at[step],
            device_id={'sp': lax.rem(me + step, group)},
            device_id_type=MESH,
        )

    for step in range(1, group):
        pos_copy(step).start()

    def send(b, which, owner, rows, to):
        return pltpu.make_async_remote_copy(
            src_ref=buf.at[b, owner, rows],
            dst_ref=buf.at[b, owner, rows],
            send_sem=send_sem.at[b, which],
            recv_sem=recv_sem.at[b, which],
            device_id={'sp': to},
            device_id_type=MESH,
        )

    def plan(b):
        table = {}
        for which, rows, to in ((RIGHT_0, 0, right), (RIGHT_1, 1, right), (LEFT_1, 1, left), (LEFT_0, 0, left)):
            table[which] = send(b, which, me, halves[rows], to)
        table[SIB] = send(b, SIB, me, pl.ds(0, blk), sib)
        table[RIGHT_F] = send(b, RIGHT_F, left, halves[0], right)
        table[LEFT_F] = send(b, LEFT_F, right, halves[1], left)
        for which, owner, rows in ((SIB_L0, left, 0), (SIB_L1, left, 1), (SIB_R0, right, 0), (SIB_R1, right, 1), (SIB_O0, far, 0), (SIB_O1, far, 1)):
            table[which] = send(b, which, owner, halves[rows], sib)
        return table

    plans = [plan(b) for b in range(batch)]

    def go(b, *which):
        for w in which:
            plans[b][w].start()

    def got(b, *which):
        for w in which:
            plans[b][w].wait_recv()

    def out_copy(b, owner):
        return pltpu.make_async_copy(buf.at[b, owner], full_ref.at[b, block_of(owner, blk), :], out_sem.at[b, owner])

    def norm_rope_block(raw, weight, cosines, sines):
        x = raw.astype(F32)
        normed = x * lax.rsqrt(jnp.mean(x * x, axis=-1, keepdims=True) + EPS) * (1.0 + weight)
        first, second = normed[:, :head // 2], normed[:, head // 2:]
        return jnp.concatenate([first * cosines - second * sines, second * cosines + first * sines], axis=1).astype(BF)

    def project(b, owner):
        out_copy(b, owner).start()
        rows = block_of(owner, blk)
        qkv = nn(buf[b, owner], w_ref[...]).astype(BF)
        cosines, sines = cos_ref[rows, :], sin_ref[rows, :]
        q_raw, k_raw = qkv[:, :head], qkv[:, head:2 * head]
        qw_ref[b, rows, :] = q_raw
        kw_ref[b, rows, :] = k_raw
        v_ref[b, rows, :] = qkv[:, 2 * head:]
        qr_ref[b, rows, :] = norm_rope_block(q_raw, qn_ref[...], cosines, sines)
        kr_ref[b, rows, :] = norm_rope_block(k_raw, kn_ref[...], cosines, sines)

    def project_own(b):
        got(b, SIB)

        @pl.loop(0, 2)
        def _(t):
            project(b, 2 * chip + lax.rem(core + t, 2))

    def project_near(b):
        got(b, SIB_L0, SIB_R1, SIB_L1, SIB_R0)

        @pl.loop(0, 4)
        def _(t):
            project(b, 2 * lax.rem(chip + 1 + 2 * lax.rem(t, 2), chips) + lax.rem(core + t // 2, 2))

    def project_far(b):
        got(b, RIGHT_F, LEFT_F)
        go(b, SIB_O0, SIB_O1)
        got(b, SIB_O0, SIB_O1)

        @pl.loop(0, 2)
        def _(t):
            project(b, 2 * lax.rem(chip + 2, chips) + lax.rem(core + t, 2))

    go(0, RIGHT_0, LEFT_1, RIGHT_1, LEFT_0, SIB)
    pos_all[me] = pos_ref[...]
    for step in range(1, group):
        pos_copy(step).wait()

    @pl.loop(0, group)
    def _(owner):
        cosines, sines = table_block(pos_all[owner], freq_ref[...])
        cos_ref[block_of(owner, blk), :] = cosines
        sin_ref[block_of(owner, blk), :] = sines

    for load in loads:
        load.wait()
    project_own(0)
    for b in range(batch):
        if b:
            project_own(b)
            attention = Attention(group, me, qr_ref.at[b - 1], kr_ref.at[b - 1], v_ref.at[b - 1], o_ref, lse_ref, tok_ref, s_scr, acc, o_send, o_recv)
            attention.blocks(0, group // 2)
        got(b, RIGHT_0, LEFT_1)
        go(b, RIGHT_F, LEFT_F, SIB_L0, SIB_R1)
        if b + 1 < batch:
            go(b + 1, RIGHT_0, LEFT_1, RIGHT_1, LEFT_0, SIB)
        if b:
            attention.blocks(group // 2, group)
            attention.flush()
        got(b, RIGHT_1, LEFT_0)
        go(b, SIB_L1, SIB_R0)
        project_near(b)
        project_far(b)
    attention.finish()
    for b in range(batch):
        for w in range(13):
            plans[b][w].wait_send()

        @pl.loop(0, group)
        def _(owner):
            out_copy(b, owner).wait()


def first(x, pos, freq, w_pre, q_norm, k_norm, w_q, w_k, w_v, group, cid):
    batch, blk, width = x.shape
    head = q_norm.shape[0]
    seq = group * blk
    assert batch == 2 and group == 8
    heads_out = jax.ShapeDtypeStruct((batch, seq, head), BF)
    table = jax.ShapeDtypeStruct((seq, head // 2), F32)
    vmem = pl.BlockSpec(memory_space=pltpu.VMEM)
    anywhere = pl.BlockSpec(memory_space=pl.ANY)
    dma = pltpu.SemaphoreType.DMA
    return pl.pallas_call(
        functools.partial(first_kernel, group),
        out_shape=(jax.ShapeDtypeStruct((batch, seq, width), BF),) + (heads_out,) * 5 + (table,) * 2 + attn_outs(group, blk, seq, head),
        in_specs=[vmem] * 6 + [anywhere] * 3,
        out_specs=(anywhere,) + (vmem,) * 10,
        scratch_shapes=[pltpu.VMEM((batch, group, blk, width), BF), pltpu.VMEM((width, 3 * head), BF), pltpu.VMEM((group, 1, blk), F32)]
        + attn_scratch(group, blk, seq, head)
        + [dma((batch, 13)), dma((batch, 13)), dma((batch, group)), dma((3,)), dma((group,)), dma((group,))],
        cost_estimate=pl.CostEstimate(flops=90 * 10 ** 9, bytes_accessed=2 * batch * seq * width, transcendentals=seq * seq),
        compiler_params=pltpu.CompilerParams(vmem_limit_bytes=60 * 1024 * 1024, collective_id=cid, has_side_effects=True),
        name='first',
    )(x, pos, freq, w_pre[None, :], q_norm[None, :], k_norm[None, :], w_q, w_k, w_v)


def bwd_kernel(q_ref, k_ref, v_ref, do_ref, lse_ref, dl_ref, dq_ref, dk_ref, dv_ref, dq_acc):
    seq, head = q_ref.shape
    scale = head ** -0.5
    upper = lax.broadcasted_iota(jnp.int32, (BWD_BLK, BWD_BLK), 0) <= lax.broadcasted_iota(jnp.int32, (BWD_BLK, BWD_BLK), 1)
    dq_acc[...] = jnp.zeros_like(dq_acc)
    dk_ref[...] = jnp.zeros_like(dk_ref)
    dv_ref[...] = jnp.zeros_like(dv_ref)

    @pl.loop(0, seq // BWD_BLK)
    def _(j):
        cols = pl.ds(pl.multiple_of(j * BWD_BLK, BWD_BLK), BWD_BLK)
        k = k_ref[cols, :]
        v = v_ref[cols, :]

        def step(i, masked):
            rows = pl.ds(pl.multiple_of(i * BWD_BLK, BWD_BLK), BWD_BLK)
            q = q_ref[rows, :]
            do = do_ref[rows, :]
            st = nt(k, q) * scale
            if masked:
                st = jnp.where(upper, st, NEG_BIG)
            pt = jnp.exp(st - lse_ref[0:1, rows])
            dpt = nt(v, do)
            dst = (pt * (dpt - dl_ref[0:1, rows]) * scale).astype(BF)
            dv_ref[cols, :] += nn(pt.astype(BF), do)
            dk_ref[cols, :] += nn(dst, q)
            dq_acc[rows, :] += tn(dst, k)

        step(j, True)

        @pl.loop(j + 1, seq // BWD_BLK)
        def _(i):
            step(i, False)

    dq_ref[...] = dq_acc[...].astype(BF)


def attn_bwd(q, k, v, do, lse, delta):
    seq, head = q.shape
    blk = BWD_BLK
    pairs = seq * (seq + blk) // 2
    return pl.pallas_call(
        bwd_kernel,
        out_shape=(jax.ShapeDtypeStruct((seq, head), BF), jax.ShapeDtypeStruct((seq, head), F32), jax.ShapeDtypeStruct((seq, head), F32)),
        in_specs=[pl.BlockSpec(memory_space=pltpu.VMEM)] * 6,
        out_specs=(pl.BlockSpec(memory_space=pltpu.VMEM),) * 3,
        scratch_shapes=[pltpu.VMEM((seq, head), F32)],
        cost_estimate=pl.CostEstimate(flops=10 * pairs * head, bytes_accessed=20 * seq * head, transcendentals=pairs),
        compiler_params=pltpu.CompilerParams(vmem_limit_bytes=32 * 1024 * 1024),
        name='attn_bwd',
    )(q, k, v, do, lse, delta)


def move_kernel(*refs):
    for src, dst in zip(refs[:len(refs) // 2], refs[len(refs) // 2:]):
        dst[...] = src[...].reshape(dst.shape)


def move(grid, out_shapes, in_specs, out_specs, operands):
    size = sum(s.size for s in out_shapes)
    return pl.pallas_call(
        move_kernel,
        grid=grid,
        out_shape=out_shapes,
        in_specs=in_specs,
        out_specs=out_specs,
        cost_estimate=pl.CostEstimate(flops=20 * size, bytes_accessed=4 * size, transcendentals=0),
        compiler_params=pltpu.CompilerParams(vmem_limit_bytes=32 * 1024 * 1024),
    )(*operands)


def spread_q(parts):
    group, rows, head = parts.shape
    return move((group,), (jax.ShapeDtypeStruct((rows, group * head), BF),),
                [pl.BlockSpec((1, rows, head), lambda c: (c, 0, 0))], (pl.BlockSpec((rows, head), lambda c: (0, c)),), (parts,))[0]


def spread_kv(parts):
    group, rows, head = parts.shape
    shape = jax.ShapeDtypeStruct((rows, group // 2 * head), BF)
    out = pl.BlockSpec((rows, head), lambda c: (0, c))
    return move((group // 2,), (shape, shape),
                [pl.BlockSpec((1, rows, head), lambda c: (2 * c, 0, 0)), pl.BlockSpec((1, rows, head), lambda c: (2 * c + 1, 0, 0))], (out, out), (parts, parts))


def place(whole):
    rows, wide = whole.shape
    spec = pl.BlockSpec((rows // 8, wide), lambda r: (r, 0))
    return move((8,), (jax.ShapeDtypeStruct((rows, wide), BF),), [spec], (spec,), (whole,))[0]


def solution(mesh):
    group = mesh.shape['sp']

    def device_step(x_in, dy_in, positions, w_q, w_k, w_v, w_o, w_pre, w_post, q_norm, k_norm):
        batch, seq_loc, width = x_in.shape
        head = q_norm.shape[0]
        heads = w_q.shape[1] // head
        kv_heads = w_k.shape[1] // head
        rep = group // kv_heads
        assert heads == group and rep == 2
        me = lax.axis_index('sp')
        even = (me % rep) == 0
        swap = [(d, d ^ 1) for d in range(group)]
        wo_mine = lax.dynamic_slice(w_o, (me * head, 0), (head, width))

        x_f32 = [x_in[b].astype(F32) for b in range(batch)]
        dy_f32 = [dy_in[b].astype(F32) for b in range(batch)]
        inv_freq = ROPE_BASE ** (-jnp.arange(head // 2, dtype=F32) * 2.0 / head)
        (a_both, q_both, k_both, v_both, q_raw, k_raw, cosines, sines, o_first, lse_first, tok_first) = first(
            x_in, positions.astype(F32)[None, :], inv_freq[None, :], w_pre, q_norm, k_norm, w_q, w_k, w_v, group, 0)
        roper = functools.partial(norm_rope, cosines=cosines, sines=sines)
        a_all = [a_both[b] for b in range(batch)]

        saved = []
        dproj_all = []
        y_out, dw_post = [], 0.0
        for b in range(batch):
            q_rot, k_rot, v_raw = q_both[b], k_both[b], v_both[b]
            _, q_pull = jax.vjp(roper, q_raw[b], q_norm)
            _, k_pull = jax.vjp(roper, k_raw[b], k_norm)
            if b == 0:
                o, lse, o_tok = o_first, lse_first, tok_first
            else:
                o, lse, o_tok = attn_fwd(q_rot, k_rot, v_raw, group, b)
            saved.append((q_rot, k_rot, v_raw, o, lse, q_pull, k_pull))
            proj = nn(o_tok, w_o).astype(BF)
            post, post_pull = jax.vjp(post_norm, proj, w_post)
            y_out.append((x_f32[b] + post).astype(BF))
            d_proj, dwp = post_pull(dy_f32[b])
            dw_post = dw_post + dwp
            dproj_all.append(lax.all_gather(d_proj, 'sp', axis=0, tiled=True))
            if b + 1 < batch:
                q_both, _ = lax.optimization_barrier((q_both, d_proj))

        dproj_all[0], _ = lax.optimization_barrier((dproj_all[0], d_proj))
        d_mine, dqkv_tok = [], []
        dq_norm = dk_norm = 0.0
        dw_o = 0.0
        for b in range(batch):
            q_rot, k_rot, v_raw, o, lse, q_pull, k_pull = saved[b]
            if b:
                dproj_all[b], _ = lax.optimization_barrier((dproj_all[b], d_mine[b - 1]))
            dw_o = dw_o + tn(o, dproj_all[b])
            if b + 1 == batch:
                dw_o_all = lax.all_gather(dw_o.astype(BF), 'sp', axis=0, tiled=True)
            d_o = nt(dproj_all[b], wo_mine).astype(BF)
            delta = jnp.sum(d_o.astype(F32) * o.astype(F32), axis=1)[None, :]
            dq_rot, dk_part, dv_part = attn_bwd(q_rot, k_rot, v_raw, d_o, lse.reshape(1, -1), delta)
            other = lax.ppermute(jnp.where(even, dv_part, dk_part), 'sp', swap)
            dkv = (jnp.where(even, dk_part, dv_part) + other).astype(BF)
            dq_proj, dqn = q_pull(dq_rot)
            dk_proj, dkn = k_pull(dkv)
            dq_norm = dq_norm + dqn
            dk_norm = dk_norm + jnp.where(even, dkn, 0.0)
            d_two = jnp.concatenate([dq_proj, jnp.where(even, dk_proj, dkv)], axis=1)
            d_mine.append(d_two)
            if b:
                d_two, dqkv_tok[b - 1] = lax.optimization_barrier((d_two, dqkv_tok[b - 1]))
            dqkv_tok.append(lax.all_to_all(d_two, 'sp', 0, 1, tiled=True))

        dw_q_part = sum(tn(a_all[b], d_mine[b][:, :head]) for b in range(batch)).astype(BF)
        dw_q_parts = lax.all_gather(dw_q_part, 'sp', axis=0, tiled=False)
        dw_kv_part = sum(tn(a_all[b], d_mine[b][:, head:]) for b in range(batch)).astype(BF)
        dw_kv_parts = lax.all_gather(dw_kv_part, 'sp', axis=0, tiled=False)
        dw_o_all = place(dw_o_all)
        dqkv_tok[1], dw_o_all = lax.optimization_barrier((dqkv_tok[1], dw_o_all))

        d_tok = jnp.concatenate(dqkv_tok, axis=0)
        d_tok = [d_tok[:, j * head:(j + 1) * head] for j in range(2 * group)]
        d_normed = (nt(jnp.concatenate(d_tok[0::2], axis=1), w_q)
                    + nt(jnp.concatenate(d_tok[1::4], axis=1), w_k)
                    + nt(jnp.concatenate(d_tok[3::4], axis=1), w_v)).astype(BF).reshape(batch, seq_loc, width)
        _, pre_pull = jax.vjp(pre_norm, x_in.astype(F32), w_pre)
        dx_norm, dw_pre = pre_pull(d_normed)
        dx_out = (dy_in.astype(F32) + dx_norm).astype(BF)
        dw_q_all = spread_q(dw_q_parts)
        dw_k_all, dw_v_all = spread_kv(dw_kv_parts)
        small = lax.psum((dw_pre, dw_post, dq_norm, dk_norm), 'sp')
        return (jnp.stack(y_out), dx_out, dw_q_all, dw_k_all, dw_v_all, dw_o_all) + small

    token_spec = P('dp', 'sp', None)
    return jax.shard_map(device_step, mesh=mesh,
                         in_specs=(token_spec, token_spec, P(('dp', 'sp')), P(None, None), P(None, None), P(None, None), P(None, None), P(None), P(None), P(None), P(None)),
                         out_specs=(token_spec, token_spec, P('dp', None), P('dp', None), P('dp', None), P('dp', None), P('dp'), P('dp'), P('dp'), P('dp')),
                         check_vma=False)
```

time: 769 us -> 514 us (0.67)
  the two profiles are of different devices: /device:TPU:120 before, /device:TPU:80 now
where the time goes in v2:
time: 514 us; the launch traced here: 505 us
  Pallas kernels  190 us (37%)
  waiting for transfers between devices  99.6 us (19%)
  matrix products  74.9 us (15%)
  local copies, waits for them, and re-layouts  51.7 us (10%)
  other arithmetic  39.4 us (8%)
  blocking collectives  24.3 us (5%)
  between operations  15.2 us (3%)
  starting transfers between devices  9.86 us (2%)
    pallas_call x1, Pallas kernels, first(): pl.pallas_call(functools.partial(first_kernel, group), out_shape=(jax.Sha...  100 us
    all_to_all x2, waiting for transfers between devices, device_step(): dqkv_tok.append(lax.all_to_all(d_two, 'sp', 0, 1, tiled=True))  73.3 us
    pallas_call x2, Pallas kernels, attn_bwd(): pl.pallas_call(bwd_kernel, out_shape=(jax.ShapeDtypeStruct((seq, head), B...  38.2 us
    pallas_call x1, Pallas kernels, attn_fwd(): pl.pallas_call(functools.partial(fwd_kernel, group), out_shape=attn_outs(...  37.9 us
    dot_general x5, matrix products, nt(): lax.dot_general(lhs, rhs, (((1,), (1,)), ((), ())), preferred_element_typ...  37.2 us
    unnamed x136, local copies, waits for them, and re-layouts  34.7 us
    dot_general x6, matrix products, tn(): lax.dot_general(lhs, rhs, (((0,), (0,)), ((), ())), preferred_element_typ...  28.2 us
    psum x1, blocking collectives, device_step(): small = lax.psum((dw_pre, dw_post, dq_norm, dk_norm), 'sp')  24.3 us
  transfers between devices with their start and end apart: 9, of which 5 were waited for; matrix products, arithmetic and copies ran while one was open for 23% of the time, Pallas kernels for 17%

profile of v2, /device:TPU:80, one launch (start us, length us, event | category | flops | bytes accessed | tf_op | source)
XLA Modules:
  0.0 504.5 jit_solution(18136924295607175852)
XLA Ops:
  7.8 1.2 convert_element_type.152
  9.0 1.3 broadcast_in_dim.60.wpre_ref
  11.0 100.2 %first.1 = (bf16[2,2048,2304]{2,1,0:T(8,128)(2,1)}, bf16[2,2048,256]{2,1,0:T(8,128)(2,1)}, bf16[2,2048,256]{2,1,0:T(8,128)(2,1)}, bf16[2,2048,256]{2,1,0:T(8,128...) custom-call(bf16[2,256,2304]{2,1,0:T(8,128)(2,1)} %x_ref.1, ...), custom_call_target="tpu_custom_call" | custom-call | flops 89999998976 | bytes 18874368 | tf_op jit(solution)/shard_map/first/pallas_call | solution.py:374
  111.3 6.8 %fusion.44 = (f32[256]{0:T(256)S(1)}, bf16[256,2304]{1,0:T(8,128)(2,1)S(1)}) fusion(bf16[256,2048]{1,0:T(8,128)(2,1)} %get-tuple-element.39, bf16[2048,2304]{1,0:T(8,128)(2,1)} %param.17), kind=kOutput, calls=%fused_computation.84 | convolution fusion | flops 2418278144 | bytes 11666432 | tf_op jit(solution)/shard_map/dot_general | solution.py:48
  118.1 1.2 fusion.40
  119.3 1.6 fusion.42
  121.4 1.5 copy-done.41
  122.9 1.1 slice_bitcast_fusion.1
  124.9 1.1 slice_bitcast_fusion
  126.0 37.9 %attn_fwd.1 = (bf16[2048,256]{1,0:T(8,128)(2,1)S(1)}, f32[2048,1]{1,0:T(8,128)S(1)}, bf16[256,2048]{1,0:T(8,128)(2,1)S(1)}) custom-call(bf16[2048,256]{1,0:T(8,128)(2,1)S(1)} %slice_bitcast_fusion.5.refs_0_.q_ref, bf16[2048,256]{1,0:T(8,128)(2,1)S(1)} %get-tuple-element.118.refs_1_.k_ref, bf16[2048,256]{1,0:T(8,128)(2,1)S(1)} %get-tuple-element.116.refs_2_.v_ref), custom_call_target="tpu_custom_call" | custom-call | flops 14495514624 | bytes 4194304 | tf_op jit(solution)/shard_map/attn_fwd/pallas_call | solution.py:171
  163.9 2.7 fusion.46
  166.7 1.2 fusion.41
  168.4 3.0 fusion.68
  171.6 1.6 reduce
  173.1 2.4 slice_bitcast_fusion.2.q_ref
  175.5 11.4 %all-gather.10.cloned.1.call-done = bf16[2048,2304]{1,0:T(8,128)(2,1)} async-done(((bf16[256,2304]{1,0:T(8,128)(2,1)}), bf16[2048,2304]{1,0:T(8,128)(2,1)}) %all-gather.10.cloned.1.call-update) | async-done | bytes 9437200 | tf_op jit(solution)/shard_map/all_gather | solution.py:519
  187.0 7.2 %multiply_reduce_fusion.1 = (f32[2048]{0:T(1024)S(1)}, bf16[2048,256]{1,0:T(8,128)(2,1)S(1)}) fusion(bf16[2048,256]{1,0:T(8,128)(2,1)} %get-tuple-element.47, bf16[2048,2304]{1,0:T(8,128)(2,1)} %all-gather.10.cloned.1.call-done, bf16[2048,2304]{1,0:T(8,128)(2,1)} %param.17, s32[]{:T(128)S(6)} %select_n.52), kind=kOutput, calls=%fused_computation.118 | convolution fusion | flops 2418538496 | bytes 12722180 | tf_op jit(solution)/shard_map/dot_general | solution.py:44
  194.2 19.3 %attn_bwd.2 = (bf16[2048,256]{1,0:T(8,128)(2,1)S(1)}, f32[2048,256]{1,0:T(8,128)S(1)}, f32[2048,256]{1,0:T(8,128)S(1)}) custom-call(bf16[2048,256]{1,0:T(8,128)(2,1)S(1)} %copy-done.3, bf16[2048,256]{1,0:T(8,128)(2,1)S(1)} %copy-done.8, bf16[2048,256]{1,0:T(8,128)(2,1)S(1)} %copy-done.9, bf16[2048,256]{1,0:T(8,128)(2,1)S(1)} %get-tuple-element.125.do_ref, ...), custom_call_target="tpu_custom_call" | custom-call | flops 6039797760 | bytes 10485760 | tf_op jit(solution)/shard_map/attn_bwd/pallas_call | solution.py:429
  214.2 1.0 copy-done.15
  217.1 4.1 fusion.103
  223.2 2.4 fusion.55
  227.4 1.0 copy-done.36
  228.4 1.5 pad_maximum_fusion.1
  229.9 10.5 %all-gather.8.cloned.1.call-done = bf16[2048,2304]{1,0:T(8,128)(2,1)} async-done(((bf16[256,2304]{1,0:T(8,128)(2,1)}), bf16[2048,2304]{1,0:T(8,128)(2,1)}) %all-gather.8.cloned.1.call-update) | async-done | bytes 9437200 | tf_op jit(solution)/shard_map/all_gather | solution.py:519
  240.3 7.8 %fusion.25 = bf16[256,2304]{1,0:T(8,128)(2,1)} fusion(f32[256,2304]{1,0:T(8,128)} %fusion.103, bf16[2048,256]{1,0:T(8,128)(2,1)S(1)} %get-tuple-element.57, bf16[2048,2304]{1,0:T(8,128)(2,1)} %all-gather.8.cloned.1.call-done), kind=kOutput, calls=%fused_computation.39 | convolution fusion | flops 2417098752 | bytes 14024704 | tf_op jit(solution)/shard_map/dot_general | solution.py:52
  248.6 6.8 %multiply_reduce_fusion = (f32[2048]{0:T(1024)S(1)}, bf16[2048,256]{1,0:T(8,128)(2,1)S(1)}) fusion(bf16[2048,256]{1,0:T(8,128)(2,1)S(1)} %get-tuple-element.57, bf16[2048,2304]{1,0:T(8,128)(2,1)} %all-gather.8.cloned.1.call-done, bf16[2048,2304]{1,0:T(8,128)(2,1)} %param.17, s32[]{:T(128)S(6)} %select_n.52), kind=kOutput, calls=%fused_computation.114 | convolution fusion | flops 2418538496 | bytes 12722180 | tf_op jit(solution)/shard_map/dot_general | solution.py:44
  255.5 18.9 %attn_bwd.3 = (bf16[2048,256]{1,0:T(8,128)(2,1)S(1)}, f32[2048,256]{1,0:T(8,128)S(1)}, f32[2048,256]{1,0:T(8,128)S(1)}) custom-call(bf16[2048,256]{1,0:T(8,128)(2,1)S(1)} %slice_bitcast_fusion.5.refs_0_.q_ref, bf16[2048,256]{1,0:T(8,128)(2,1)S(1)} %copy-done.5, bf16[2048,256]{1,0:T(8,128)(2,1)S(1)} %copy-done.7, ...), custom_call_target="tpu_custom_call" | custom-call | flops 6039797760 | bytes 10485760 | tf_op jit(solution)/shard_map/attn_bwd/pallas_call | solution.py:429
  275.2 4.1 collective-permute-done.1
  279.4 1.4 fusion.100
  280.7 1.4 multiply_add_fusion.3
  284.5 2.9 fusion.2
  287.4 4.0 fusion.29
  291.6 2.3 fusion.67
  293.9 1.2 fusion.70
  296.1 5.5 %fusion = f32[2304,256]{1,0:T(8,128)S(1)} fusion(bf16[2048,256]{1,0:T(8,128)(2,1)S(1)} %fusion.70, bf16[2,2048,2304]{2,1,0:T(8,128)(2,1)} %get-tuple-element.64), kind=kOutput, calls=%fused_computation | convolution fusion | flops 2415919104 | bytes 12845056 | tf_op jit(solution)/shard_map/dot_general | solution.py:52
  301.6 1.1 slice-done.15
  302.7 1.2 slice-done.16
  304.4 3.9 fusion.26
  308.5 2.4 copy.25
  310.8 3.9 all-to-all-start
  314.8 2.7 pad_maximum_fusion.2
  317.5 47.1 %all-to-all-done = bf16[8,256,512]{1,2,0:T(8,128)(2,1)S(1)} async-done(((bf16[8,256,512]{1,2,0:T(8,128)(2,1)}), bf16[8,256,512]{1,2,0:T(8,128)(2,1)S(1)}, u32[]{:S(2)}, u32[]{:S(2)}) %all-to-all-start) | async-done | bytes 2097184 | tf_op jit(solution)/shard_map/all_to_all | solution.py:547
  364.6 1.3 copy-done.23
  365.9 3.9 copy.26
  369.9 4.7 all-to-all-start.1
  376.2 1.6 pad_maximum_fusion
  378.6 1.5 constant_dynamic-update-slice_fusion.1
  380.1 4.2 copy-done.1
  384.3 4.7 shard_map.186
  389.0 26.2 %all-to-all-done.1 = bf16[8,256,512]{1,2,0:T(8,128)(2,1)} async-done(((bf16[8,256,512]{1,2,0:T(8,128)(2,1)}), bf16[8,256,512]{1,2,0:T(8,128)(2,1)}, u32[]{:S(2)}, u32[]{:S(2)}) %all-to-all-start.1) | async-done | bytes 2097184 | tf_op jit(solution)/shard_map/all_to_all | solution.py:547
  415.2 3.0 constant_dynamic-update-slice_fusion
  421.2 1.0 slice_dynamic-update-slice_fusion.4
  424.1 1.0 slice_dynamic-update-slice_fusion.1
  425.1 1.8 fusion.102
  426.9 7.0 %fusion.72 = f32[512,2304]{1,0:T(8,128)} fusion(bf16[2304,1024]{1,0:T(8,128)(2,1)} %wk_ref.1, bf16[512,256]{0,1:T(8,128)(2,1)S(1)} %get-tuple-element.96, bf16[512,256]{0,1:T(8,128)(2,1)S(1)} %get-tuple-element.97, bf16[512,256]{0,1:T(8,128)(2,1)S(1)} %get-tuple-element.98, bf16[512,256]{0,1:T(8,128)(2,1)S(1)} %get-tuple-element.99), kind=kOutput, calls=%fused_computation.123 | convolution fusion | flops 2420113408 | bytes 10485760 | tf_op jit(solution)/shard_map/dot_general | solution.py:44
  433.9 11.5 %convolution_add_fusion = f32[512,2304]{1,0:T(8,128)} fusion(f32[512,2304]{1,0:T(8,128)} %fusion.72, bf16[512,2048]{0,1:T(8,128)(2,1)S(1)} %get-tuple-element.100, bf16[2304,2048]{1,0:T(8,128)(2,1)} %wq_ref.1), kind=kOutput, calls=%fused_computation.20 | convolution fusion | flops 4833017856 | bytes 20971520 | tf_op jit(solution)/shard_map/dot_general | solution.py:44
  445.4 4.7 fusion.18
  450.1 1.8 fusion.13
  451.9 24.3 %all-reduce.8 = (f32[2304]{0:T(1024)}, f32[2304]{0:T(1024)}, f32[256]{0:T(256)}, f32[256]{0:T(256)}) all-reduce(f32[2304]{0:T(1024)S(1)} %get-tuple-element.80, f32[2304]{0:T(1024)S(1)} %add.182, f32[256]{0:T(256)S(1)} %add.183, f32[256]{0:T(256)S(1)} %select_add_fusion), channel_id=1, replica_groups=mesh['dp'=4,'sp'=8] {'sp'}, use_global_device_ids=true, to_apply=%region_17.18 | all-reduce | flops 5120 | bytes 40960 | tf_op jit(solution)/shard_map/psum | solution.py:566
  476.3 5.4 %fusion.15 = bf16[2,256,2304]{2,1,0:T(8,128)(2,1)} fusion(bf16[2,256,2304]{2,1,0:T(8,128)(2,1)S(1)} %copy-done.11, bf16[2,256,2304]{2,1,0:T(8,128)(2,1)} %param.12, f32[2,256]{1,0:T(2,128)S(1)} %multiply_multiply_fusion.4, f32[2,256]{1,0:T(2,128)S(1)} %fusion.93, f32[2304]{0:T(1024)S(1)} %broadcast_add_fusion, bf16[512,2304]{1,0:T(8,128)(2,1)} %copy-done.14), kind=kLoop, calls=%fused_computation.24 | loop fusion | flops 11796480 | bytes 9450496 | tf_op jit(solution)/shard_map/convert_element_type | solution.py:563
  481.7 3.7 copy-done.2
  485.3 4.7 shard_map.187
  490.1 3.7 copy-done
  493.8 3.8 shard_map.188
  (182 shorter events, 22.2 us)
Async XLA Ops:
  7.2 179.8 %all-gather.10.cloned.1.call-start = ((), (), s32[]{:S(2)}) async-start(), calls=%async_computation.3 | async-start | bytes 10616832 | tf_op jit(solution)/shard_map/all_gather | solution.py:519
  111.3 6.9 %copy-start.12 = (bf16[2,256,2304]{2,1,0:T(8,128)(2,1)S(1)}, bf16[2,256,2304]{2,1,0:T(8,128)(2,1)}, u32[]{:S(2)}) copy-start(bf16[2,256,2304]{2,1,0:T(8,128)(2,1)} %param.12) | copy-start | bytes 7077892
  119.3 2.0 copy-start.39
  121.0 119.3 %all-gather.8.cloned.1.call-start = ((), (), s32[]{:S(2)}) async-start(), calls=%async_computation.2 | async-start | bytes 10616832 | tf_op jit(solution)/shard_map/all_gather | solution.py:519
  121.3 1.6 copy-start.41
  122.9 2.0 copy-start.40
  122.9 41.0 %slice-start.3 = ((s8[9437184]{0:T(1024)(128)(4,1)}), s8[4194304]{0:T(1024)(128)(4,1)S(1)}, s32[]{:S(2)}) async-start(s8[9437184]{0:T(1024)(128)(4,1)} %bitcast.129), calls=%async_computation.10 | async-start | bytes 8388608
  124.0 2.0 copy-start.4
  126.0 37.9 %copy-start.6 = (bf16[2048,256]{1,0:T(8,128)(2,1)}, bf16[2048,256]{1,0:T(8,128)(2,1)S(1)}, u32[]{:S(2)}) copy-start(bf16[2048,256]{1,0:T(8,128)(2,1)S(1)} %get-tuple-element.116.refs_2_.v_ref) | copy-start | bytes 3145732
  126.0 37.9 %slice-start.4 = ((s8[9437184]{0:T(1024)(128)(4,1)}), s8[4194304]{0:T(1024)(128)(4,1)S(1)}, s32[]{:S(2)}) async-start(s8[9437184]{0:T(1024)(128)(4,1)} %bitcast.129), calls=%async_computation.11 | async-start | bytes 8388608
  126.0 37.9 %slice-start.5 = ((s8[9437184]{0:T(1024)(128)(4,1)}), s8[1048576]{0:T(1024)(128)(4,1)S(1)}, s32[]{:S(2)}) async-start(s8[9437184]{0:T(1024)(128)(4,1)} %bitcast.129), calls=%async_computation.12 | async-start | bytes 2097152
  163.9 2.7 copy-start.13
  163.9 3.9 copy-start.20
  166.6 1.8 copy-start.10
  171.5 208.6 %all-gather.12.cloned.1.call-start = ((), (), s32[]{:S(2)}) async-start(), calls=%async_computation.4 | async-start | bytes 10616832 | tf_op jit(solution)/shard_map/all_gather | solution.py:533
  187.0 7.2 %copy-start.3 = (bf16[2048,256]{1,0:T(8,128)(2,1)S(1)}, bf16[2048,256]{1,0:T(8,128)(2,1)}, u32[]{:S(2)}) copy-start(bf16[2048,256]{1,0:T(8,128)(2,1)} %slice_bitcast_fusion.2.q_ref) | copy-start | bytes 3145732
  187.0 7.2 %copy-start.8 = (bf16[2048,256]{1,0:T(8,128)(2,1)S(1)}, bf16[2048,256]{1,0:T(8,128)(2,1)}, u32[]{:S(2)}) copy-start(bf16[2048,256]{1,0:T(8,128)(2,1)} %get-tuple-element.117.k_ref) | copy-start | bytes 3145732
  187.0 7.2 %copy-start.9 = (bf16[2048,256]{1,0:T(8,128)(2,1)S(1)}, bf16[2048,256]{1,0:T(8,128)(2,1)}, u32[]{:S(2)}) copy-start(bf16[2048,256]{1,0:T(8,128)(2,1)} %get-tuple-element.115.v_ref) | copy-start | bytes 3145732
  187.0 29.5 %slice-start = ((s8[9437184]{0:T(1024)(128)(4,1)}), s8[4194304]{0:T(1024)(128)(4,1)S(1)}, s32[]{:S(2)}) async-start(s8[9437184]{0:T(1024)(128)(4,1)} %bitcast.121), calls=%async_computation.7 | async-start | bytes 8388608
  187.0 29.5 %slice-start.1 = ((s8[9437184]{0:T(1024)(128)(4,1)}), s8[4194304]{0:T(1024)(128)(4,1)S(1)}, s32[]{:S(2)}) async-start(s8[9437184]{0:T(1024)(128)(4,1)} %bitcast.121), calls=%async_computation.8 | async-start | bytes 8388608
  194.2 22.3 %slice-start.2 = ((s8[9437184]{0:T(1024)(128)(4,1)}), s8[1048576]{0:T(1024)(128)(4,1)S(1)}, s32[]{:S(2)}) async-start(s8[9437184]{0:T(1024)(128)(4,1)} %bitcast.121), calls=%async_computation.9 | async-start | bytes 2097152
  213.5 1.7 copy-start.15
  213.5 2.4 copy-start.17
  213.8 2.4 copy-start.44
  213.8 2.4 copy-start.45
  213.8 7.4 %collective-permute-start = (f32[2048,256]{1,0:T(8,128)S(1)}, f32[2048,256]{1,0:T(8,128)S(1)}, u32[]{:S(2)}, u32[]{:S(2)}) collective-permute-start(f32[2048,256]{1,0:T(8,128)S(1)} %broadcast_select_fusion.1), channel_id=1, source_target_pairs={{0,1},{1,0},{2,3},{3,2},{4,5},{5,4},{6,7},{7,6},{8,9},{9,8},{10,11... | collective-permute-start | bytes 6291464 | tf_op jit(solution)/shard_map/ppermute | solution.py:537
  248.2 233.5 %all-gather.14.cloned.1.call-start = ((), (), s32[]{:S(2)}) async-start(), calls=%async_computation.5 | async-start | bytes 10616832 | tf_op jit(solution)/shard_map/all_gather | solution.py:550
  248.6 6.9 %copy-start.5 = (bf16[2048,256]{1,0:T(8,128)(2,1)S(1)}, bf16[2048,256]{1,0:T(8,128)(2,1)}, u32[]{:S(2)}) copy-start(bf16[2048,256]{1,0:T(8,128)(2,1)} %copy-done.4) | copy-start | bytes 3145732
  248.6 6.9 %copy-start.7 = (bf16[2048,256]{1,0:T(8,128)(2,1)S(1)}, bf16[2048,256]{1,0:T(8,128)(2,1)}, u32[]{:S(2)}) copy-start(bf16[2048,256]{1,0:T(8,128)(2,1)} %copy-done.6) | copy-start | bytes 3145732
  255.5 28.9 %slice-start.8 = ((s8[18874368]{0:T(1024)(128)(4,1)}), s8[4194304]{0:T(1024)(128)(4,1)S(1)}, s32[]{:S(2)}) async-start(s8[18874368]{0:T(1024)(128)(4,1)} %bitcast.133), calls=%async_computation.15 | async-start | bytes 8388608
  255.5 28.9 %slice-start.9 = ((s8[18874368]{0:T(1024)(128)(4,1)}), s8[4194304]{0:T(1024)(128)(4,1)S(1)}, s32[]{:S(2)}) async-start(s8[18874368]{0:T(1024)(128)(4,1)} %bitcast.133), calls=%async_computation.16 | async-start | bytes 8388608
  274.4 10.0 %slice-start.10 = ((s8[18874368]{0:T(1024)(128)(4,1)}), s8[4194304]{0:T(1024)(128)(4,1)S(1)}, s32[]{:S(2)}) async-start(s8[18874368]{0:T(1024)(128)(4,1)} %bitcast.133), calls=%async_computation.17 | async-start | bytes 8388608
  274.7 4.7 collective-permute-start.1
  275.2 5.5 %copy-start.28 = (f32[2048,128]{1,0:T(8,128)S(1)}, f32[2048,128]{1,0:T(8,128)}, u32[]{:S(2)}) copy-start(f32[2048,128]{1,0:T(8,128)} %get-tuple-element.49) | copy-start | bytes 3145732
  275.2 5.5 %copy-start.30 = (f32[2048,128]{1,0:T(8,128)S(1)}, f32[2048,128]{1,0:T(8,128)}, u32[]{:S(2)}) copy-start(f32[2048,128]{1,0:T(8,128)} %get-tuple-element.50) | copy-start | bytes 3145732
  275.2 9.2 %slice-start.11 = ((s8[18874368]{0:T(1024)(128)(4,1)}), s8[4194304]{0:T(1024)(128)(4,1)S(1)}, s32[]{:S(2)}) async-start(s8[18874368]{0:T(1024)(128)(4,1)} %bitcast.133), calls=%async_computation.18 | async-start | bytes 8388608
  280.7 2.0 copy-start.16
  280.7 3.7 slice-start.12
  284.4 3.0 copy-start.33
  284.5 2.9 copy-start.32
  287.4 4.2 copy-start.18
  291.5 198.6 %all-gather.16.cloned.1.call-start = ((), (), s32[]{:S(2)}) async-start(), calls=%async_computation.6 | async-start | bytes 10616832 | tf_op jit(solution)/shard_map/all_gather | solution.py:552
  291.5 2.3 copy-start.21
  291.5 2.3 copy-start.35
  293.9 7.7 %slice-start.13 = ((s8[18874368]{0:T(1024)(128)(4,1)}), s8[4194304]{0:T(1024)(128)(4,1)S(1)}, s32[]{:S(2)}) async-start(s8[18874368]{0:T(1024)(128)(4,1)} %bitcast.135), calls=%async_computation.20 | async-start | bytes 8388608
  296.1 5.5 %copy-start.37 = (bf16[2048,256]{1,0:T(8,128)(2,1)S(1)}, bf16[2048,256]{1,0:T(8,128)(2,1)}, u32[]{:S(2)}) copy-start(bf16[2048,256]{1,0:T(8,128)(2,1)} %copy-done.36) | copy-start | bytes 3145732
  296.1 5.5 %slice-start.14 = ((s8[18874368]{0:T(1024)(128)(4,1)}), s8[4194304]{0:T(1024)(128)(4,1)S(1)}, s32[]{:S(2)}) async-start(s8[18874368]{0:T(1024)(128)(4,1)} %bitcast.135), calls=%async_computation.21 | async-start | bytes 8388608
  296.1 6.6 %slice-start.15 = ((s8[18874368]{0:T(1024)(128)(4,1)}), s8[4194304]{0:T(1024)(128)(4,1)S(1)}, s32[]{:S(2)}) async-start(s8[18874368]{0:T(1024)(128)(4,1)} %bitcast.135), calls=%async_computation.22 | async-start | bytes 8388608
  296.1 7.8 %slice-start.16 = ((s8[18874368]{0:T(1024)(128)(4,1)}), s8[4194304]{0:T(1024)(128)(4,1)S(1)}, s32[]{:S(2)}) async-start(s8[18874368]{0:T(1024)(128)(4,1)} %bitcast.135), calls=%async_computation.23 | async-start | bytes 8388608
  296.1 8.4 %slice-start.17 = ((s8[18874368]{0:T(1024)(128)(4,1)}), s8[2097152]{0:T(1024)(128)(4,1)S(1)}, s32[]{:S(2)}) async-start(s8[18874368]{0:T(1024)(128)(4,1)} %bitcast.135), calls=%async_computation.24 | async-start | bytes 4194304
  304.4 4.0 copy-start.22
  310.8 4.0 copy-start.34
  310.8 53.8 %all-to-all-start = ((bf16[8,256,512]{1,2,0:T(8,128)(2,1)}), bf16[8,256,512]{1,2,0:T(8,128)(2,1)S(1)}, u32[]{:S(2)}, u32[]{:S(2)}) async-start(bf16[8,256,512]{1,2,0:T(8,128)(2,1)} %copy.25), calls=%async_computation | async-start | bytes 4194304 | tf_op jit(solution)/shard_map/all_to_all | solution.py:547
  365.9 9.2 %copy-start.43 = (f32[2304]{0:T(1024)S(1)}, f32[2304]{0:T(1024)}, u32[]{:S(2)}) copy-start(f32[2304]{0:T(1024)} %param.18) | copy-start | bytes 27652
  369.9 4.7 copy-start.11
  369.9 45.4 %all-to-all-start.1 = ((bf16[8,256,512]{1,2,0:T(8,128)(2,1)}), bf16[8,256,512]{1,2,0:T(8,128)(2,1)}, u32[]{:S(2)}, u32[]{:S(2)}) async-start(bf16[8,256,512]{1,2,0:T(8,128)(2,1)} %copy.26), calls=%async_computation.1 | async-start | bytes 4194304 | tf_op jit(solution)/shard_map/all_to_all | solution.py:547
  374.6 1.6 copy-start.26
  376.2 2.4 copy-start.24
  380.1 4.2 copy-start.1
  426.9 18.5 %slice-start.6 = ((s8[4718592]{0:T(1024)(128)(4,1)}), s8[4194304]{0:T(1024)(128)(4,1)S(1)}, s32[]{:S(2)}) async-start(s8[4718592]{0:T(1024)(128)(4,1)} %bitcast.131), calls=%async_computation.13 | async-start | bytes 8388608
  433.9 11.5 %slice-start.7 = ((s8[4718592]{0:T(1024)(128)(4,1)}), s8[524288]{0:T(1024)(128)(4,1)S(1)}, s32[]{:S(2)}) async-start(s8[4718592]{0:T(1024)(128)(4,1)} %bitcast.131), calls=%async_computation.14 | async-start | bytes 1048576
  450.1 1.8 copy-start.14
  481.7 3.7 copy-start.2
  490.1 3.7 copy-start
  (9 other events, 10.8 us)
Sparse Core Ops, SparseCore 0:
  121.2 65.7 all-gather.9
  189.1 51.1 all-gather.7
  248.3 51.1 all-gather.11
  301.5 73.6 all-gather.13
  376.6 64.3 all-gather.15

commit v3 on v2

v3 whole, which is shorter than its diff:
```python
import functools
import math
import jax
import jax.numpy as jnp
from jax import lax
from jax.experimental import pallas as pl
from jax.experimental.pallas import tpu as pltpu
from jax.sharding import PartitionSpec as P

EPS = 1e-6
ROPE_BASE = 1000000.0
ROPE_SCALE = 8.0
NEG_BIG = -1e30
HALF_PI = (1.5625, 0.0081787109375, 0.00011730194091796875, 3.129243850708008e-07, 9.920935796805404e-10)
BWD_BLK = 256
BF = jnp.bfloat16
F32 = jnp.float32
MESH = pl.DeviceIdType.MESH


def rms_scale(x_f32, weight):
    inv_rms = lax.rsqrt(jnp.mean(x_f32 * x_f32, axis=-1, keepdims=True) + EPS)
    return x_f32 * inv_rms * (1.0 + weight)


def pre_norm(x_f32, weight):
    return rms_scale(x_f32, weight).astype(BF)


def norm_rope(head_bf, weight, cosines, sines):
    half_dim = head_bf.shape[-1] // 2
    normed = rms_scale(head_bf.astype(F32), weight)
    first = normed[..., :half_dim]
    second = normed[..., half_dim:]
    rotated = jnp.concatenate([first * cosines - second * sines, second * cosines + first * sines], axis=-1)
    return rotated.astype(BF)


def nt(lhs, rhs):
    return lax.dot_general(lhs, rhs, (((1,), (1,)), ((), ())), preferred_element_type=F32)


def nn(lhs, rhs):
    return lax.dot_general(lhs, rhs, (((1,), (0,)), ((), ())), preferred_element_type=F32)


def tn(lhs, rhs):
    return lax.dot_general(lhs, rhs, (((0,), (0,)), ((), ())), preferred_element_type=F32)


def others_barrier(group, me):
    barrier = pltpu.get_barrier_semaphore()
    for step in range(1, group):
        pl.semaphore_signal(barrier, inc=1, device_id={'sp': lax.rem(me + step, group)}, device_id_type=MESH)
    pl.semaphore_wait(barrier, group - 1)


def block_of(index, size):
    return pl.ds(pl.multiple_of(index * size, size), size)


def fold(x, op):
    out = x[:, :128]
    for c in range(1, x.shape[1] // 128):
        out = op(out, x[:, c * 128:(c + 1) * 128])
    return out


def diagonal(size):
    return lax.broadcasted_iota(jnp.int32, (size, size), 0) == lax.broadcasted_iota(jnp.int32, (size, size), 1)


def as_row(column):
    size = column.shape[0]
    return jnp.sum(jnp.where(diagonal(size), jnp.broadcast_to(column, (size, size)), 0.0), axis=0, keepdims=True)


def as_column(row):
    size = row.shape[1]
    return jnp.sum(jnp.where(diagonal(size), jnp.broadcast_to(row, (size, size)), 0.0), axis=1, keepdims=True)


class Attention:
    def __init__(self, group, me, b, q_ref, k_ref, v_ref, o_ref, lse_ref, tok_ref, s_scr, acc, send_sem, recv_sem):
        self.group, self.me, self.b = group, me, b
        self.refs = q_ref, k_ref, v_ref, o_ref, lse_ref, tok_ref, s_scr, acc
        self.sems = send_sem, recv_sem
        self.blk, self.head = acc.shape
        self.mine = block_of(me, self.head)

    def copy_to(self, step):
        o_ref, tok_ref = self.refs[3], self.refs[5]
        peer = lax.rem(self.me + step, self.group)
        return pltpu.make_async_remote_copy(
            src_ref=o_ref.at[block_of(peer, self.blk), :],
            dst_ref=tok_ref.at[pl.ds(self.b * self.blk, self.blk), self.mine],
            send_sem=self.sems[0].at[self.b, step],
            recv_sem=self.sems[1].at[self.b, step],
            device_id={'sp': peer},
            device_id_type=MESH,
        )

    def blocks(self, first, last):
        q_ref, k_ref, v_ref, o_ref, lse_ref, _, s_scr, acc = self.refs
        blk, head = self.blk, self.head
        scale = head ** -0.5
        wide = 2 * blk
        ahead = lax.broadcasted_iota(jnp.int32, (blk, wide), 0) - lax.broadcasted_iota(jnp.int32, (blk, wide), 1)

        @pl.loop(first, last)
        def _(step):
            i = lax.rem(self.me + step, self.group)
            rows = block_of(i, blk)
            q = q_ref[rows, :]
            edge = i // 2
            cols = block_of(edge, wide)
            s = jnp.where(ahead + lax.rem(i, 2) * blk >= 0, nt(q, k_ref[cols, :]) * scale, NEG_BIG)
            s_scr[:, cols] = s

            def pass1(j, m):
                cols = block_of(j, wide)
                s = nt(q, k_ref[cols, :]) * scale
                s_scr[:, cols] = s
                return jnp.maximum(m, fold(s, jnp.maximum))

            m = lax.fori_loop(0, edge, pass1, fold(s, jnp.maximum))
            m = jnp.max(m, axis=1, keepdims=True)

            @pl.when(step > 1)
            def _():
                self.copy_to(step - 1).start()

            def pass2(j, l):
                cols = block_of(j, wide)
                p = jnp.exp(s_scr[:, cols] - m)
                s_scr[:, cols] = p
                return l + fold(p, jnp.add)

            l = lax.fori_loop(0, edge + 1, pass2, jnp.zeros((blk, min(128, blk)), F32))
            l = jnp.sum(l, axis=1, keepdims=True)
            inv = 1.0 / l
            acc[...] = jnp.zeros_like(acc)

            @pl.loop(0, edge + 1)
            def _(j):
                cols = block_of(j, wide)
                acc[...] += nn((s_scr[:, cols] * inv).astype(BF), v_ref[cols, :])

            o_ref[rows, :] = acc[...].astype(BF)
            lse_ref[:, rows] = as_row(m + jnp.log(l))

    def flush(self):
        o_ref, tok_ref = self.refs[3], self.refs[5]
        tok_ref[pl.ds(self.b * self.blk, self.blk), self.mine] = o_ref[block_of(self.me, self.blk), :]
        self.copy_to(self.group - 1).start()

    def finish(self):
        @pl.loop(1, self.group)
        def _(step):
            self.copy_to(step).wait()


RIGHT_0, RIGHT_1, RIGHT_F, LEFT_1, LEFT_0, LEFT_F, SIB, SIB_L0, SIB_L1, SIB_R0, SIB_R1, SIB_O0, SIB_O1 = range(13)


class Ring:
    def __init__(self, group, me, buf, send_sem, recv_sem):
        self.me, self.chips = me, group // 2
        self.core, self.chip = lax.rem(me, 2), me // 2
        self.buf, self.sems = buf, (send_sem, recv_sem)
        self.blk = buf.shape[2]
        self.right, self.left, self.far = self.device(1, 0), self.device(-1, 0), self.device(2, 0)
        self.plans = [self.plan(b) for b in range(buf.shape[0])]

    def device(self, chip_step, other):
        return 2 * lax.rem(self.chip + self.chips + chip_step, self.chips) + lax.rem(self.core + other, 2)

    def send(self, b, which, owner, rows, to):
        place = self.buf.at[b, owner, rows]
        return pltpu.make_async_remote_copy(
            src_ref=place,
            dst_ref=place,
            send_sem=self.sems[0].at[b, which],
            recv_sem=self.sems[1].at[b, which],
            device_id={'sp': to},
            device_id_type=MESH,
        )

    def plan(self, b):
        me, right, left, far, sib = self.me, self.right, self.left, self.far, self.device(0, 1)
        half = self.blk // 2
        halves = [pl.ds(0, half), pl.ds(half, half)]
        routes = ((RIGHT_0, me, 0, right), (RIGHT_1, me, 1, right), (LEFT_1, me, 1, left), (LEFT_0, me, 0, left),
                  (RIGHT_F, left, 0, right), (LEFT_F, right, 1, left), (SIB_L0, left, 0, sib), (SIB_L1, left, 1, sib),
                  (SIB_R0, right, 0, sib), (SIB_R1, right, 1, sib), (SIB_O0, far, 0, sib), (SIB_O1, far, 1, sib))
        table = {which: self.send(b, which, owner, halves[rows], to) for which, owner, rows, to in routes}
        table[SIB] = self.send(b, SIB, me, pl.ds(0, self.blk), sib)
        return table

    def go(self, b, *which):
        for w in which:
            self.plans[b][w].start()

    def got(self, b, *which):
        for w in which:
            self.plans[b][w].wait_recv()

    def open(self, b):
        self.go(b, RIGHT_0, LEFT_1, RIGHT_1, LEFT_0, SIB)

    def turn(self, b):
        self.got(b, RIGHT_0, LEFT_1)
        self.go(b, RIGHT_F, LEFT_F, SIB_L0, SIB_R1)

    def near(self, b):
        self.got(b, RIGHT_1, LEFT_0)
        self.go(b, SIB_L1, SIB_R0)

    def each_own(self, b, work):
        self.got(b, SIB)

        @pl.loop(0, 2)
        def _(t):
            work(b, self.device(0, t))

    def each_near(self, b, work):
        self.got(b, SIB_L0, SIB_R1, SIB_L1, SIB_R0)

        @pl.loop(0, 4)
        def _(t):
            work(b, self.device(1 + 2 * lax.rem(t, 2), t // 2))

    def each_far(self, b, work):
        self.got(b, RIGHT_F, LEFT_F)
        self.go(b, SIB_O0, SIB_O1)
        self.got(b, SIB_O0, SIB_O1)

        @pl.loop(0, 2)
        def _(t):
            work(b, self.device(2, t))

    def sent(self):
        for plan in self.plans:
            for copy in plan.values():
                copy.wait_send()


def table_block(pos_row, freq_row):
    angle = as_column(pos_row) / ROPE_SCALE * freq_row
    turn = jnp.floor(angle * (2.0 / math.pi) + 0.5)
    rest = angle
    for part in HALF_PI:
        rest = rest - turn * part
    sq = rest * rest
    sin_r = rest + rest * sq * (-1.6666654611e-1 + sq * (8.3321608736e-3 + sq * -1.9515295891e-4))
    cos_r = 1.0 - 0.5 * sq + sq * sq * (4.166664568298827e-2 + sq * (-1.388731625493765e-3 + sq * 2.443315711809948e-5))
    quarter = turn - 4.0 * jnp.floor(turn * 0.25)
    odd = (quarter == 1.0) | (quarter == 3.0)
    cosines = jnp.where(odd, sin_r, cos_r)
    sines = jnp.where(odd, cos_r, sin_r)
    cosines = jnp.where((quarter == 1.0) | (quarter == 2.0), -cosines, cosines)
    sines = jnp.where(quarter >= 2.0, -sines, sines)
    return cosines, sines


def first_kernel(group, batch, x_ref, pos_ref, freq_ref, wpre_ref, qn_ref, kn_ref, wq_ref, wk_ref, wv_ref, full_ref, cos_out, sin_out, tok_ref, *rest):
    per_out = [rest[b * 7:(b + 1) * 7] for b in range(batch)]
    buf, w_ref, pos_all, s_scr, acc, cos_ref, sin_ref, o_send, o_recv, send_sem, recv_sem, out_sem, w_sem, p_send, p_recv, keep_sem, table_sem = rest[batch * 7:batch * 7 + 17]
    kept = rest[batch * 7 + 17:]
    per = [kept[b * 6:(b + 1) * 6] + (per_out[b][6],) for b in range(batch)]
    outward = [[pltpu.make_async_copy(per[b][n], per_out[b][n], keep_sem.at[b, n]) for n in range(6)] for b in range(batch)]
    tables = [pltpu.make_async_copy(cos_ref, cos_out, table_sem.at[0]), pltpu.make_async_copy(sin_ref, sin_out, table_sem.at[1])]
    blk, _ = x_ref.shape[1:]
    head = qn_ref.shape[1]
    me = lax.axis_index('sp')
    loads = [pltpu.make_async_copy(ref.at[:, block_of(index, head)], w_ref.at[:, pl.ds(place * head, head)], w_sem.at[place])
             for place, (ref, index) in enumerate(((wq_ref, me), (wk_ref, me // 2), (wv_ref, me // 2)))]
    for load in loads:
        load.start()

    @pl.loop(0, batch * 4)
    def _(t):
        rows = block_of(lax.rem(t, 4), blk // 4)
        x = x_ref[t // 4, rows, :].astype(F32)
        inv = lax.rsqrt(jnp.mean(x * x, axis=-1, keepdims=True) + EPS)
        buf[t // 4, me, rows, :] = (x * inv * (1.0 + wpre_ref[...])).astype(BF)

    others_barrier(group, me)
    ring = Ring(group, me, buf, send_sem, recv_sem)

    def pos_copy(step):
        return pltpu.make_async_remote_copy(
            src_ref=pos_ref,
            dst_ref=pos_all.at[me],
            send_sem=p_send.at[step],
            recv_sem=p_recv.at[step],
            device_id={'sp': lax.rem(me + step, group)},
            device_id_type=MESH,
        )

    for step in range(1, group):
        pos_copy(step).start()

    def out_copy(b, owner):
        return pltpu.make_async_copy(buf.at[b, owner], full_ref.at[b, block_of(owner, blk), :], out_sem.at[b, owner])

    def norm_rope_block(raw, weight, cosines, sines):
        x = raw.astype(F32)
        normed = x * lax.rsqrt(jnp.mean(x * x, axis=-1, keepdims=True) + EPS) * (1.0 + weight)
        first, second = normed[:, :head // 2], normed[:, head // 2:]
        return jnp.concatenate([first * cosines - second * sines, second * cosines + first * sines], axis=1).astype(BF)

    def project(b, owner):
        q_ref, k_ref, v_ref, qw_ref, kw_ref = per[b][:5]
        out_copy(b, owner).start()
        rows = block_of(owner, blk)
        qkv = nn(buf[b, owner], w_ref[...]).astype(BF)
        cosines, sines = cos_ref[rows, :], sin_ref[rows, :]
        q_raw, k_raw = qkv[:, :head], qkv[:, head:2 * head]
        qw_ref[rows, :] = q_raw
        kw_ref[rows, :] = k_raw
        v_ref[rows, :] = qkv[:, 2 * head:]
        q_ref[rows, :] = norm_rope_block(q_raw, qn_ref[...], cosines, sines)
        k_ref[rows, :] = norm_rope_block(k_raw, kn_ref[...], cosines, sines)

    ring.open(0)
    pos_all[me] = pos_ref[...]
    for step in range(1, group):
        pos_copy(step).wait()

    @pl.loop(0, group)
    def _(owner):
        cosines, sines = table_block(pos_all[owner], freq_ref[...])
        cos_ref[block_of(owner, blk), :] = cosines
        sin_ref[block_of(owner, blk), :] = sines

    for copy in tables:
        copy.start()
    for load in loads:
        load.wait()
    attention = [Attention(group, me, b, *per[b][:3], *per[b][5:], tok_ref, s_scr, acc, o_send, o_recv) for b in range(batch)]
    ring.each_own(0, project)
    for b in range(batch):
        if b:
            ring.each_own(b, project)
            attention[b - 1].blocks(0, group // 2)
        ring.turn(b)
        if b + 1 < batch:
            ring.open(b + 1)
        if b:
            attention[b - 1].blocks(group // 2, group)
            attention[b - 1].flush()
            outward[b - 1][5].start()
        ring.near(b)
        ring.each_near(b, project)
        ring.each_far(b, project)
        for copy in outward[b][:5]:
            copy.start()
    attention[-1].blocks(0, group)
    attention[-1].flush()
    outward[-1][5].start()
    for b in range(batch):
        attention[b].finish()
    ring.sent()
    for copy in tables + sum(outward, []):
        copy.wait()
    for b in range(batch):
        @pl.loop(0, group)
        def _(owner):
            out_copy(b, owner).wait()


VMEM = pl.BlockSpec(memory_space=pltpu.VMEM)
ANYWHERE = pl.BlockSpec(memory_space=pl.ANY)
DMA = pltpu.SemaphoreType.DMA


def first(x, pos, freq, w_pre, q_norm, k_norm, w_q, w_k, w_v, group, cid):
    batch, blk, width = x.shape
    head = q_norm.shape[0]
    seq = group * blk
    assert group == 8
    heads_out = jax.ShapeDtypeStruct((seq, head), BF)
    table = jax.ShapeDtypeStruct((seq, head // 2), F32)
    outs = pl.pallas_call(
        functools.partial(first_kernel, group, batch),
        out_shape=(jax.ShapeDtypeStruct((batch, seq, width), BF), table, table, jax.ShapeDtypeStruct((batch * blk, group * head), BF))
        + ((heads_out,) * 6 + (jax.ShapeDtypeStruct((1, seq), F32),)) * batch,
        in_specs=[VMEM] * 6 + [ANYWHERE] * 3,
        out_specs=(ANYWHERE,) * 3 + (VMEM,) + ((ANYWHERE,) * 6 + (VMEM,)) * batch,
        scratch_shapes=[pltpu.VMEM((batch, group, blk, width), BF), pltpu.VMEM((width, 3 * head), BF), pltpu.VMEM((group, 1, blk), F32),
                        pltpu.VMEM((blk, seq), F32), pltpu.VMEM((blk, head), F32), pltpu.VMEM((seq, head // 2), F32), pltpu.VMEM((seq, head // 2), F32),
                        DMA((batch, group)), DMA((batch, group)), DMA((batch, 13)), DMA((batch, 13)), DMA((batch, group)), DMA((3,)), DMA((group,)), DMA((group,)),
                        DMA((batch, 6)), DMA((2,))] + [pltpu.VMEM((seq, head), BF)] * (6 * batch),
        cost_estimate=pl.CostEstimate(flops=90 * 10 ** 9, bytes_accessed=2 * batch * seq * width, transcendentals=seq * seq),
        compiler_params=pltpu.CompilerParams(vmem_limit_bytes=62 * 1024 * 1024, collective_id=cid, has_side_effects=True),
        name='first',
    )(x, pos, freq, w_pre[None, :], q_norm[None, :], k_norm[None, :], w_q, w_k, w_v)
    return outs[:4] + (tuple(outs[4 + 7 * b:11 + 7 * b] for b in range(batch)),)


def second_kernel(group, batch, tok_ref, wpost_ref, lse_ref, wo_hbm, x_hbm, dy_hbm, *rest):
    late_hbm, rest = rest[:3 + batch], rest[3 + batch:]
    y_hbm, dwpost_ref, dwo_ref, dq_ref, dk_ref, dv_ref = rest[:6]
    do_refs, dl_refs, rest = rest[6:6 + batch], rest[6 + batch:6 + 2 * batch], rest[6 + 2 * batch:]
    buf, dq_acc, dwo_acc, wo_ref, x_ref, dy_ref, p_scr, send_sem, recv_sem, wo_sem, act_sem, late_sem, y_sem = rest[:13]
    late = rest[13:]
    q_ref, k_ref, v_ref = late[:3]
    o_refs = late[3:]
    blk, width = x_ref.shape[1:]
    head = dwo_ref.shape[0]
    me = lax.axis_index('sp')
    mine = block_of(me, head)
    part = width // wo_sem.shape[0]
    wo_loads = [pltpu.make_async_copy(wo_hbm.at[:, pl.ds(n * part, part)], wo_ref.at[:, pl.ds(n * part, part)], wo_sem.at[n]) for n in range(width // part)]
    act_loads = [[pltpu.make_async_copy(src.at[b], dst.at[b], act_sem.at[b, n]) for n, (src, dst) in enumerate(((x_hbm, x_ref), (dy_hbm, dy_ref)))] for b in range(batch)]
    late_loads = [pltpu.make_async_copy(src, dst, late_sem.at[n]) for n, (src, dst) in enumerate(zip(late_hbm, late))]
    for load in wo_loads + sum(act_loads, []) + late_loads:
        load.start()
    dwpost_ref[...] = jnp.zeros_like(dwpost_ref)
    dwo_acc[...] = jnp.zeros_like(dwo_acc)
    y_copies = [pltpu.make_async_copy(x_ref.at[b], y_hbm.at[b], y_sem.at[b]) for b in range(batch)]

    def project(b):
        for n in range(width // part):
            if b == 0:
                wo_loads[n].wait()
            p_scr[:, n * part:(n + 1) * part] = nn(tok_ref[b * blk:(b + 1) * blk, :], wo_ref[:, n * part:(n + 1) * part]).astype(BF)
        for load in act_loads[b]:
            load.wait()
        gain = 1.0 + wpost_ref[...]
        rows_each = 32

        @pl.loop(0, blk // rows_each)
        def _(t):
            rows = block_of(t, rows_each)
            p = p_scr[rows, :].astype(F32)
            dy = dy_ref[b, rows, :].astype(F32)
            inv = lax.rsqrt(jnp.mean(p * p, axis=-1, keepdims=True) + EPS)
            unit = p * inv
            x_ref[b, rows, :] = (x_ref[b, rows, :].astype(F32) + unit * gain).astype(BF)
            scaled = dy * gain
            dwpost_ref[...] += jnp.sum(dy * unit, axis=0, keepdims=True)
            buf[b, me, rows, :] = (inv * (scaled - unit * jnp.mean(scaled * unit, axis=-1, keepdims=True))).astype(BF)

        y_copies[b].start()

    project(0)
    others_barrier(group, me)
    ring = Ring(group, me, buf, send_sem, recv_sem)

    def work(b, owner):
        rows = block_of(owner, blk)
        chunk = buf[b, owner]
        o = o_refs[b][rows, :]
        d_o = nt(chunk, wo_ref[mine, :]).astype(BF)
        do_refs[b][rows, :] = d_o
        dl_refs[b][:, rows] = as_row(jnp.sum(d_o.astype(F32) * o.astype(F32), axis=1, keepdims=True))
        dwo_acc[...] += tn(o, chunk)

    def backward(first, last):
        bwd_blocks(first, last, q_ref, k_ref, v_ref, do_refs[0], lse_ref, dl_refs[0], dq_acc, dk_ref, dv_ref)

    ring.open(0)
    for b in range(1, batch):
        project(b)
    for load in late_loads:
        load.wait()
    ring.each_own(0, work)
    for b in range(batch):
        if b:
            ring.each_own(b, work)
            bwd_start(dq_acc, dk_ref, dv_ref)
            backward(0, 3)
        ring.turn(b)
        if b + 1 < batch:
            ring.open(b + 1)
        if b:
            backward(3, group)
            dq_ref[...] = dq_acc[...].astype(BF)
        ring.near(b)
        ring.each_near(b, work)
        ring.each_far(b, work)
    dwo_ref[...] = dwo_acc[...].astype(BF)
    ring.sent()
    for copy in y_copies:
        copy.wait()


def second(tok, w_o, x, dy, w_post, q, k, v, lse, outs, group, cid):
    batch, blk, width = x.shape
    seq, head = q.shape
    assert batch == 2 and group == 8
    wide = jax.ShapeDtypeStruct((seq, head), F32)
    half = jax.ShapeDtypeStruct((seq, head), BF)
    row = jax.ShapeDtypeStruct((1, seq), F32)
    res = pl.pallas_call(
        functools.partial(second_kernel, group, batch),
        out_shape=(jax.ShapeDtypeStruct(x.shape, BF), jax.ShapeDtypeStruct((1, width), F32), jax.ShapeDtypeStruct((head, width), BF), half, wide, wide)
        + (half,) * batch + (row,) * batch,
        in_specs=[VMEM] * 3 + [ANYWHERE] * (6 + batch),
        out_specs=(ANYWHERE,) + (VMEM,) * (5 + 2 * batch),
        scratch_shapes=[pltpu.VMEM((batch, group, blk, width), BF), pltpu.VMEM((seq, head), F32), pltpu.VMEM((head, width), F32),
                        pltpu.VMEM(w_o.shape, BF), pltpu.VMEM(x.shape, BF), pltpu.VMEM(x.shape, BF), pltpu.VMEM((blk, width), BF),
                        DMA((batch, 13)), DMA((batch, 13)), DMA((3,)), DMA((batch, 2)), DMA((3 + batch,)), DMA((batch,))]
        + [pltpu.VMEM((seq, head), BF)] * (3 + batch),
        cost_estimate=pl.CostEstimate(flops=80 * 10 ** 9, bytes_accessed=2 * batch * seq * width, transcendentals=seq * seq),
        compiler_params=pltpu.CompilerParams(vmem_limit_bytes=63 * 1024 * 1024, collective_id=cid, has_side_effects=True),
        name='second',
    )(tok, w_post[None, :], lse, w_o, x, dy, q, k, v, *outs)
    return res[0], res[1][0], res[2:6], res[6:6 + batch], res[6 + batch:]


def bwd_start(*accs):
    for acc in accs:
        acc[...] = jnp.zeros_like(acc)


def bwd_blocks(first, last, q_ref, k_ref, v_ref, do_ref, lse_ref, dl_ref, dq_acc, dk_ref, dv_ref):
    seq, head = q_ref.shape
    scale = head ** -0.5
    wide = 2 * BWD_BLK
    ahead = lax.broadcasted_iota(jnp.int32, (BWD_BLK, wide), 1) - lax.broadcasted_iota(jnp.int32, (BWD_BLK, wide), 0)

    @pl.loop(first, last)
    def _(j):
        cols = block_of(j, BWD_BLK)
        k = k_ref[cols, :]
        v = v_ref[cols, :]

        def step(i, masked):
            rows = block_of(i, wide)
            q = q_ref[rows, :]
            do = do_ref[rows, :]
            st = nt(k, q) * scale
            if masked:
                st = jnp.where(ahead >= lax.rem(j, 2) * BWD_BLK, st, NEG_BIG)
            pt = jnp.exp(st - lse_ref[0:1, rows])
            dpt = nt(v, do)
            dst = (pt * (dpt - dl_ref[0:1, rows]) * scale).astype(BF)
            dv_ref[cols, :] += nn(pt.astype(BF), do)
            dk_ref[cols, :] += nn(dst, q)
            dq_acc[rows, :] += tn(dst, k)

        step(j // 2, True)

        @pl.loop(j // 2 + 1, seq // wide)
        def _(i):
            step(i, False)


def bwd_kernel(q_ref, k_ref, v_ref, do_ref, lse_ref, dl_ref, dq_ref, dk_ref, dv_ref, dq_acc):
    bwd_start(dq_acc, dk_ref, dv_ref)
    bwd_blocks(0, q_ref.shape[0] // BWD_BLK, q_ref, k_ref, v_ref, do_ref, lse_ref, dl_ref, dq_acc, dk_ref, dv_ref)
    dq_ref[...] = dq_acc[...].astype(BF)


def attn_bwd(q, k, v, do, lse, delta):
    seq, head = q.shape
    blk = BWD_BLK
    pairs = seq * (seq + blk) // 2
    return pl.pallas_call(
        bwd_kernel,
        out_shape=(jax.ShapeDtypeStruct((seq, head), BF), jax.ShapeDtypeStruct((seq, head), F32), jax.ShapeDtypeStruct((seq, head), F32)),
        in_specs=[pl.BlockSpec(memory_space=pltpu.VMEM)] * 6,
        out_specs=(pl.BlockSpec(memory_space=pltpu.VMEM),) * 3,
        scratch_shapes=[pltpu.VMEM((seq, head), F32)],
        cost_estimate=pl.CostEstimate(flops=10 * pairs * head, bytes_accessed=20 * seq * head, transcendentals=pairs),
        compiler_params=pltpu.CompilerParams(vmem_limit_bytes=32 * 1024 * 1024),
        name='attn_bwd',
    )(q, k, v, do, lse, delta)


def move_kernel(*refs):
    for src, dst in zip(refs[:len(refs) // 2], refs[len(refs) // 2:]):
        dst[...] = src[...].reshape(dst.shape)


def move(grid, out_shapes, in_specs, out_specs, operands):
    size = sum(s.size for s in out_shapes)
    return pl.pallas_call(
        move_kernel,
        grid=grid,
        out_shape=out_shapes,
        in_specs=in_specs,
        out_specs=out_specs,
        cost_estimate=pl.CostEstimate(flops=20 * size, bytes_accessed=4 * size, transcendentals=0),
        compiler_params=pltpu.CompilerParams(vmem_limit_bytes=32 * 1024 * 1024),
    )(*operands)


def spread_q(parts):
    group, rows, head = parts.shape
    return move((group,), (jax.ShapeDtypeStruct((rows, group * head), BF),),
                [pl.BlockSpec((1, rows, head), lambda c: (c, 0, 0))], (pl.BlockSpec((rows, head), lambda c: (0, c)),), (parts,))[0]


def spread_kv(parts):
    group, rows, head = parts.shape
    shape = jax.ShapeDtypeStruct((rows, group // 2 * head), BF)
    out = pl.BlockSpec((rows, head), lambda c: (0, c))
    return move((group // 2,), (shape, shape),
                [pl.BlockSpec((1, rows, head), lambda c: (2 * c, 0, 0)), pl.BlockSpec((1, rows, head), lambda c: (2 * c + 1, 0, 0))], (out, out), (parts, parts))


def place(whole):
    rows, wide = whole.shape
    spec = pl.BlockSpec((rows // 8, wide), lambda r: (r, 0))
    return move((8,), (jax.ShapeDtypeStruct((rows, wide), BF),), [spec], (spec,), (whole,))[0]


def solution(mesh):
    group = mesh.shape['sp']

    def device_step(x_in, dy_in, positions, w_q, w_k, w_v, w_o, w_pre, w_post, q_norm, k_norm):
        batch, seq_loc, width = x_in.shape
        head = q_norm.shape[0]
        heads = w_q.shape[1] // head
        kv_heads = w_k.shape[1] // head
        rep = group // kv_heads
        assert heads == group and rep == 2
        me = lax.axis_index('sp')
        even = (me % rep) == 0
        swap = [(d, d ^ 1) for d in range(group)]
        inv_freq = ROPE_BASE ** (-jnp.arange(head // 2, dtype=F32) * 2.0 / head)
        a_both, cosines, sines, tok, per = first(
            x_in, positions.astype(F32)[None, :], inv_freq[None, :], w_pre, q_norm, k_norm, w_q, w_k, w_v, group, 0)
        roper = functools.partial(norm_rope, cosines=cosines, sines=sines)

        y_out, dw_post, (dw_o, dq0, dk0, dv0), d_os, deltas = second(
            tok, w_o, x_in, dy_in, w_post, *per[0][:3], per[0][6], [p[5] for p in per], group, 1)
        dw_o_all = lax.all_gather(dw_o, 'sp', axis=0, tiled=True)

        d_mine, dqkv_tok = [], []
        dq_norm = dk_norm = 0.0
        for b in range(batch):
            q_rot, k_rot, v_raw, q_raw, k_raw, _, lse = per[b]
            if b == 0:
                dq_rot, dk_part, dv_part = dq0, dk0, dv0
            else:
                lse, _ = lax.optimization_barrier((lse, d_mine[b - 1]))
                dq_rot, dk_part, dv_part = attn_bwd(q_rot, k_rot, v_raw, d_os[b], lse, deltas[b])
            other = lax.ppermute(jnp.where(even, dv_part, dk_part), 'sp', swap)
            dkv = (jnp.where(even, dk_part, dv_part) + other).astype(BF)
            _, q_pull = jax.vjp(roper, q_raw, q_norm)
            _, k_pull = jax.vjp(roper, k_raw, k_norm)
            dq_proj, dqn = q_pull(dq_rot)
            dk_proj, dkn = k_pull(dkv)
            dq_norm = dq_norm + dqn
            dk_norm = dk_norm + jnp.where(even, dkn, 0.0)
            d_two = jnp.concatenate([dq_proj, jnp.where(even, dk_proj, dkv)], axis=1)
            d_mine.append(d_two)
            if b:
                d_two, dqkv_tok[b - 1] = lax.optimization_barrier((d_two, dqkv_tok[b - 1]))
            dqkv_tok.append(lax.all_to_all(d_two, 'sp', 0, 1, tiled=True))

        dw_q_part = sum(tn(a_both[b], d_mine[b][:, :head]) for b in range(batch)).astype(BF)
        dw_q_parts = lax.all_gather(dw_q_part, 'sp', axis=0, tiled=False)
        dw_kv_part = sum(tn(a_both[b], d_mine[b][:, head:]) for b in range(batch)).astype(BF)
        dw_kv_parts = lax.all_gather(dw_kv_part, 'sp', axis=0, tiled=False)
        dw_o_all = place(dw_o_all)
        dqkv_tok[1], dw_o_all = lax.optimization_barrier((dqkv_tok[1], dw_o_all))

        d_tok = jnp.concatenate(dqkv_tok, axis=0)
        d_tok = [d_tok[:, j * head:(j + 1) * head] for j in range(2 * group)]
        d_normed = (nt(jnp.concatenate(d_tok[0::2], axis=1), w_q)
                    + nt(jnp.concatenate(d_tok[1::4], axis=1), w_k)
                    + nt(jnp.concatenate(d_tok[3::4], axis=1), w_v)).astype(BF).reshape(batch, seq_loc, width)
        _, pre_pull = jax.vjp(pre_norm, x_in.astype(F32), w_pre)
        dx_norm, dw_pre = pre_pull(d_normed)
        dx_out = (dy_in.astype(F32) + dx_norm).astype(BF)
        dw_q_all = spread_q(dw_q_parts)
        dw_k_all, dw_v_all = spread_kv(dw_kv_parts)
        small = lax.psum((dw_pre, dw_post, dq_norm, dk_norm), 'sp')
        return (y_out, dx_out, dw_q_all, dw_k_all, dw_v_all, dw_o_all) + small

    token_spec = P('dp', 'sp', None)
    return jax.shard_map(device_step, mesh=mesh,
                         in_specs=(token_spec, token_spec, P(('dp', 'sp')), P(None, None), P(None, None), P(None, None), P(None, None), P(None), P(None), P(None), P(None)),
                         out_specs=(token_spec, token_spec, P('dp', None), P('dp', None), P('dp', None), P('dp', None), P('dp'), P('dp'), P('dp'), P('dp')),
                         check_vma=False)
```

time: 514 us -> 526 us (1.023)
  Pallas kernels: 190 us -> 244 us
  matrix products: 74.9 us -> 45.4 us
  starting transfers between devices: 9.86 us -> 21.4 us
  other arithmetic: 39.4 us -> 28.2 us
  waiting for transfers between devices: 99.6 us -> 91.3 us
    pallas_call x2, Pallas kernels: 138 us -> 218 us  [the longest x1 117 us: first(): pl.pallas_call(functools.partial(first_kernel, group, batch), out_shape=(...]
    pallas_call x2 -> x1, Pallas kernels: 38.2 us -> 13.5 us  [attn_bwd(): pl.pallas_call(bwd_kernel, out_shape=(jax.ShapeDtypeStruct((seq, head), B...]
    all_gather x3 -> x1, waiting for transfers between devices: 21.9 us -> 0.01 us  [device_step(): dw_o_all = lax.all_gather(dw_o, 'sp', axis=0, tiled=True)]
    dot_general x5 -> x3, matrix products: 37.2 us -> 23.1 us  [nt(): lax.dot_general(lhs, rhs, (((1,), (1,)), ((), ())), preferred_element_typ...]
    all_to_all x2, waiting for transfers between devices: 73.3 us -> 85 us  [device_step(): dqkv_tok.append(lax.all_to_all(d_two, 'sp', 0, 1, tiled=True))]
    all_gather x1, starting transfers between devices: 0.07 us -> 10.8 us  [device_step(): dw_q_parts = lax.all_gather(dw_q_part, 'sp', axis=0, tiled=False)]
    dot_general x2 -> x0, matrix products: 9.51 us -> none  [nn(): lax.dot_general(lhs, rhs, (((1,), (0,)), ((), ())), preferred_element_typ...]
    dot_general x6 -> x4, matrix products: 28.2 us -> 22.3 us  [tn(): lax.dot_general(lhs, rhs, (((0,), (0,)), ((), ())), preferred_element_typ...]
  transfers between devices with their start and end apart: 9 -> 7, of which waited for: 5 -> 4; matrix products, arithmetic and copies ran while one was open for 23% -> 18% of each run, Pallas kernels for 17% -> 4%
where the time goes in v3:
time: 526 us; the launch traced here: 517 us
  Pallas kernels  244 us (46%)
  waiting for transfers between devices  91.3 us (17%)
  local copies, waits for them, and re-layouts  46.8 us (9%)
  matrix products  45.4 us (9%)
  other arithmetic  28.2 us (5%)
  blocking collectives  24.3 us (5%)
  starting transfers between devices  21.4 us (4%)
  between operations  14.8 us (3%)
    pallas_call x1, Pallas kernels, first(): pl.pallas_call(functools.partial(first_kernel, group, batch), out_shape=(...  117 us
    pallas_call x1, Pallas kernels, second(): pl.pallas_call(functools.partial(second_kernel, group, batch), out_shape=...  100 us
    all_to_all x2, waiting for transfers between devices, device_step(): dqkv_tok.append(lax.all_to_all(d_two, 'sp', 0, 1, tiled=True))  85 us
    unnamed x91, local copies, waits for them, and re-layouts  33.1 us
    psum x1, blocking collectives, device_step(): small = lax.psum((dw_pre, dw_post, dq_norm, dk_norm), 'sp')  24.3 us
    dot_general x3, matrix products, nt(): lax.dot_general(lhs, rhs, (((1,), (1,)), ((), ())), preferred_element_typ...  23.1 us
    dot_general x4, matrix products, tn(): lax.dot_general(lhs, rhs, (((0,), (0,)), ((), ())), preferred_element_typ...  22.3 us
    pallas_call x1, Pallas kernels, attn_bwd(): pl.pallas_call(bwd_kernel, out_shape=(jax.ShapeDtypeStruct((seq, head), B...  13.5 us
  transfers between devices with their start and end apart: 7, of which 4 were waited for; matrix products, arithmetic and copies ran while one was open for 18% of the time, Pallas kernels for 4%

profile of v3, /device:TPU:80, one launch (start us, length us, event | category | flops | bytes accessed | tf_op | source)
XLA Modules:
  0.0 516.5 jit_solution(8487602863467081671)
XLA Ops:
  7.8 1.2 convert_element_type.69
  9.0 1.3 broadcast_in_dim.47.wpre_ref
  10.3 1.3 broadcast_in_dim.50.wpost_ref
  11.6 117.1 %first.1 = (bf16[2,2048,2304]{2,1,0:T(8,128)(2,1)}, f32[2048,128]{1,0:T(8,128)}, f32[2048,128]{1,0:T(8,128)}, bf16[512,2048]{1,0:T(8,128)(2,1)}, bf16[2048,256]{...) custom-call(bf16[2,256,2304]{2,1,0:T(8,128)(2,1)} %x_hbm.1, ...), custom_call_target="tpu_custom_call" | custom-call | flops 89999998976 | bytes 18874368 | tf_op jit(solution)/shard_map/first/pallas_call | solution.py:385
  128.7 100.5 %second.1 = (bf16[2,256,2304]{2,1,0:T(8,128)(2,1)}, f32[1,2304]{1,0:T(1,128)}, bf16[256,2304]{1,0:T(8,128)(2,1)}, bf16[2048,256]{1,0:T(8,128)(2,1)}, f32[2048,25...) custom-call(bf16[512,2048]{1,0:T(8,128)(2,1)} %get-tuple-element.46., ...), custom_call_target="tpu_custom_call" | custom-call | flops 80000000000 | bytes 18874368 | tf_op jit(solution)/shard_map/second/pallas_call | solution.py:497
  229.3 10.8 %all-gather.8.cloned.1.call-start = ((), (), s32[]{:S(2)}) async-start(), calls=%async_computation.3 | async-start | bytes 10616832 | tf_op jit(solution)/shard_map/all_gather | solution.py:658
  240.1 2.4 broadcast_select_fusion.1
  242.5 0.8 collective-permute-start
  244.2 2.9 collective-permute-done
  248.2 0.7 copy-done.12
  248.8 1.2 fusion.42
  250.1 0.9 fusion.38
  251.0 0.7 fusion.31
  251.7 1.0 fusion.52
  252.8 1.5 pad_maximum_fusion
  254.7 0.7 copy-done.4
  256.1 13.5 %attn_bwd.1 = (bf16[2048,256]{1,0:T(8,128)(2,1)S(1)}, f32[2048,256]{1,0:T(8,128)S(1)}, f32[2048,256]{1,0:T(8,128)S(1)}) custom-call(bf16[2048,256]{1,0:T(8,128)(2,1)S(1)} %copy-done.3, bf16[2048,256]{1,0:T(8,128)(2,1)S(1)} %copy-done.4, bf16[2048,256]{1,0:T(8,128)(2,1)S(1)} %copy-done.5, bf16[2048,256]{1,0:T(8,128)(2,1)S(1)} %copy-done.6, ...), custom_call_target="tpu_custom_call" | custom-call | flops 6039797760 | bytes 10485760 | tf_op jit(solution)/shard_map/attn_bwd/pallas_call | solution.py:562
  271.4 3.2 collective-permute-done.1
  274.6 1.4 fusion.75
  276.4 0.9 fusion.46
  277.4 0.7 fusion.33
  278.1 1.0 copy-done.22
  279.1 5.3 %fusion.2 = f32[2304,256]{1,0:T(8,128)S(1)} fusion(bf16[2048,256]{1,0:T(8,128)(2,1)S(1)} %fusion.33, bf16[2,2048,2304]{2,1,0:T(8,128)(2,1)} %get-tuple-element.77), kind=kOutput, calls=%fused_computation.2 | convolution fusion | flops 2415919104 | bytes 12845056 | tf_op jit(solution)/shard_map/dot_general | solution.py:48
  284.4 7.6 %fusion.28 = bf16[2304,256]{1,0:T(8,128)(2,1)} fusion(f32[2304,256]{1,0:T(8,128)S(1)} %fusion.2, bf16[2048,256]{1,0:T(8,128)(2,1)S(1)} %fusion.31, bf16[2,2048,2304]{2,1,0:T(8,128)(2,1)} %get-tuple-element.77), kind=kOutput, calls=%fused_computation.31 | convolution fusion | flops 2417098752 | bytes 14024704 | tf_op jit(solution)/shard_map/dot_general | solution.py:48
  292.5 0.9 fusion.50
  293.5 1.2 fusion.51
  294.6 1.0 copy-done.27
  295.6 5.4 %fusion = f32[2304,256]{1,0:T(8,128)S(1)} fusion(bf16[2048,256]{1,0:T(8,128)(2,1)S(1)} %fusion.51, bf16[2,2048,2304]{2,1,0:T(8,128)(2,1)} %get-tuple-element.77), kind=kOutput, calls=%fused_computation | convolution fusion | flops 2415919104 | bytes 12845056 | tf_op jit(solution)/shard_map/dot_general | solution.py:48
  301.3 1.7 slice-done.4
  303.0 1.9 slice-done.5
  304.9 0.6 slice-done.6
  305.5 4.0 fusion.25
  309.5 2.4 copy.21
  311.9 4.6 all-to-all-start
  316.5 2.7 pad_maximum_fusion.1
  319.2 47.1 %all-to-all-done = bf16[8,256,512]{1,2,0:T(8,128)(2,1)S(1)} async-done(((bf16[8,256,512]{1,2,0:T(8,128)(2,1)}), bf16[8,256,512]{1,2,0:T(8,128)(2,1)S(1)}, u32[]{:S(2)}, u32[]{:S(2)}) %all-to-all-start) | async-done | bytes 2097184 | tf_op jit(solution)/shard_map/all_to_all | solution.py:655
  366.3 1.3 copy-done.18
  367.6 3.9 copy.22
  371.5 4.7 all-to-all-start.1
  376.9 1.1 copy-done.19
  378.0 1.5 constant_dynamic-update-slice_fusion.1
  379.5 3.7 copy-done.1
  383.2 4.7 shard_map.186
  387.9 37.9 %all-to-all-done.1 = bf16[8,256,512]{1,2,0:T(8,128)(2,1)} async-done(((bf16[8,256,512]{1,2,0:T(8,128)(2,1)}), bf16[8,256,512]{1,2,0:T(8,128)(2,1)}, u32[]{:S(2)}, u32[]{:S(2)}) %all-to-all-start.1) | async-done | bytes 2097184 | tf_op jit(solution)/shard_map/all_to_all | solution.py:655
  425.8 3.1 constant_dynamic-update-slice_fusion
  428.9 1.0 slice_dynamic-update-slice_fusion.7
  429.9 1.0 slice_dynamic-update-slice_fusion.6
  430.9 1.0 slice_dynamic-update-slice_fusion.5
  431.9 1.0 slice_dynamic-update-slice_fusion.4
  432.9 1.0 slice_dynamic-update-slice_fusion.3
  433.9 1.0 slice_dynamic-update-slice_fusion.2
  434.8 1.0 slice_dynamic-update-slice_fusion.1
  435.8 1.7 fusion.77
  437.6 7.0 %fusion.53 = f32[512,2304]{1,0:T(8,128)} fusion(bf16[2304,1024]{1,0:T(8,128)(2,1)} %wk_ref.1, bf16[512,256]{0,1:T(8,128)(2,1)S(1)} %get-tuple-element.104, bf16[512,256]{0,1:T(8,128)(2,1)S(1)} %get-tuple-element.105, bf16[512,256]{0,1:T(8,128)(2,1)S(1)} %get-tuple-element.106, bf16[512,256]{0,1:T(8,128)(2,1)S(1)} %get-tuple-element.107), kind=kOutput, calls=%fused_computation.82 | convolution fusion | flops 2420113408 | bytes 10485760 | tf_op jit(solution)/shard_map/dot_general | solution.py:40
  444.6 11.4 %convolution_add_fusion = f32[512,2304]{1,0:T(8,128)} fusion(f32[512,2304]{1,0:T(8,128)} %fusion.53, bf16[512,2048]{0,1:T(8,128)(2,1)S(1)} %get-tuple-element.108, bf16[2304,2048]{1,0:T(8,128)(2,1)} %wq_ref.1), kind=kOutput, calls=%fused_computation.20 | convolution fusion | flops 4833017856 | bytes 20971520 | tf_op jit(solution)/shard_map/dot_general | solution.py:40
  455.9 4.7 fusion.18
  460.7 1.8 fusion.13
  462.5 24.3 %all-reduce.8 = (f32[2304]{0:T(1024)}, f32[2304]{0:T(1024)}, f32[256]{0:T(256)}, f32[256]{0:T(256)}) all-reduce(f32[2304]{0:T(1024)S(1)} %get-tuple-element.90, f32[2304]{0:T(1024)S(1)} %reduce, f32[256]{0:T(256)S(1)} %add.140, f32[256]{0:T(256)S(1)} %select_add_fusion), channel_id=1, replica_groups=mesh['dp'=4,'sp'=8] {'sp'}, use_global_device_ids=true, to_apply=%region_11.12 | all-reduce | flops 5120 | bytes 40960 | tf_op jit(solution)/shard_map/psum | solution.py:674
  486.8 5.4 %fusion.15 = bf16[2,256,2304]{2,1,0:T(8,128)(2,1)} fusion(bf16[2,256,2304]{2,1,0:T(8,128)(2,1)S(1)} %copy-done.9, bf16[2,256,2304]{2,1,0:T(8,128)(2,1)} %dy_hbm.1, f32[2,256]{1,0:T(2,128)S(1)} %multiply_multiply_fusion.4, f32[2,256]{1,0:T(2,128)S(1)} %fusion.72, f32[2304]{0:T(1024)S(1)} %broadcast_add_fusion, bf16[512,2304]{1,0:T(8,128)(2,1)} %copy-done.10), kind=kLoop, calls=%fused_computation.24 | loop fusion | flops 11796480 | bytes 9450496 | tf_op jit(solution)/shard_map/convert_element_type | solution.py:671
  492.2 3.7 copy-done.2
  495.9 4.7 shard_map.187
  500.6 3.7 copy-done
  504.3 3.9 shard_map.188
  508.2 1.4 copy.32
  (108 shorter events, 7.4 us)
Async XLA Ops:
  7.2 372.3 %all-gather.6.cloned.1.call-start = ((), (), s32[]{:S(2)}) async-start(), calls=%async_computation.2 | async-start | bytes 10616832 | tf_op jit(solution)/shard_map/all_gather | solution.py:632
  229.3 262.9 %all-gather.8.cloned.1.call-start = ((), (), s32[]{:S(2)}) async-start(), calls=%async_computation.3 | async-start | bytes 10616832 | tf_op jit(solution)/shard_map/all_gather | solution.py:658
  240.1 3.2 copy-start.29
  240.1 7.0 %copy-start.16 = (f32[2048,256]{1,0:T(8,128)S(1)}, f32[2048,256]{1,0:T(8,128)}, u32[]{:S(2)}) copy-start(f32[2048,256]{1,0:T(8,128)} %get-tuple-element.64) | copy-start | bytes 6291460
  242.5 1.2 copy-start.14
  242.5 4.6 collective-permute-start
  243.3 0.8 copy-start.32
  243.3 0.8 copy-start.33
  243.3 3.8 copy-start.15
  244.2 3.4 copy-start.20
  244.2 3.4 copy-start.21
  247.6 1.2 copy-start.12
  251.7 2.7 copy-start.8
  252.7 1.7 copy-start.25
  252.7 2.0 copy-start.3
  252.7 2.7 copy-start.4
  252.7 3.0 copy-start.5
  252.8 3.3 copy-start.6
  252.8 3.3 copy-start.7
  269.6 1.2 copy-start.11
  269.9 4.7 collective-permute-start.1
  278.1 1.0 copy-start.22
  284.4 7.7 %copy-start.13 = (bf16[2048,256]{1,0:T(8,128)(2,1)S(1)}, bf16[2048,256]{1,0:T(8,128)(2,1)}, u32[]{:S(2)}) copy-start(bf16[2048,256]{1,0:T(8,128)(2,1)} %get-tuple-element.72) | copy-start | bytes 3145732
  292.0 208.6 %all-gather.10.cloned.1.call-start = ((), (), s32[]{:S(2)}) async-start(), calls=%async_computation.4 | async-start | bytes 10616832 | tf_op jit(solution)/shard_map/all_gather | solution.py:660
  292.1 1.3 copy-start.24
  293.4 7.6 %slice-start.2 = ((s8[18874368]{0:T(1024)(128)(4,1)}), s8[4194304]{0:T(1024)(128)(4,1)S(1)}, s32[]{:S(2)}) async-start(s8[18874368]{0:T(1024)(128)(4,1)} %bitcast.55), calls=%async_computation.7 | async-start | bytes 8388608
  294.6 1.0 copy-start.27
  295.6 5.5 %copy-start.26 = (bf16[2048,256]{1,0:T(8,128)(2,1)S(1)}, bf16[2048,256]{1,0:T(8,128)(2,1)}, u32[]{:S(2)}) copy-start(bf16[2048,256]{1,0:T(8,128)(2,1)} %copy-done.25) | copy-start | bytes 3145732
  295.6 5.7 %slice-start.3 = ((s8[18874368]{0:T(1024)(128)(4,1)}), s8[4194304]{0:T(1024)(128)(4,1)S(1)}, s32[]{:S(2)}) async-start(s8[18874368]{0:T(1024)(128)(4,1)} %bitcast.55), calls=%async_computation.8 | async-start | bytes 8388608
  295.6 7.4 %slice-start.4 = ((s8[18874368]{0:T(1024)(128)(4,1)}), s8[4194304]{0:T(1024)(128)(4,1)S(1)}, s32[]{:S(2)}) async-start(s8[18874368]{0:T(1024)(128)(4,1)} %bitcast.55), calls=%async_computation.9 | async-start | bytes 8388608
  295.6 9.3 %slice-start.5 = ((s8[18874368]{0:T(1024)(128)(4,1)}), s8[4194304]{0:T(1024)(128)(4,1)S(1)}, s32[]{:S(2)}) async-start(s8[18874368]{0:T(1024)(128)(4,1)} %bitcast.55), calls=%async_computation.10 | async-start | bytes 8388608
  295.6 9.9 %slice-start.6 = ((s8[18874368]{0:T(1024)(128)(4,1)}), s8[2097152]{0:T(1024)(128)(4,1)S(1)}, s32[]{:S(2)}) async-start(s8[18874368]{0:T(1024)(128)(4,1)} %bitcast.55), calls=%async_computation.11 | async-start | bytes 4194304
  305.5 4.0 copy-start.17
  311.9 4.6 copy-start.23
  311.9 54.4 %all-to-all-start = ((bf16[8,256,512]{1,2,0:T(8,128)(2,1)}), bf16[8,256,512]{1,2,0:T(8,128)(2,1)S(1)}, u32[]{:S(2)}, u32[]{:S(2)}) async-start(bf16[8,256,512]{1,2,0:T(8,128)(2,1)} %copy.21), calls=%async_computation | async-start | bytes 4194304 | tf_op jit(solution)/shard_map/all_to_all | solution.py:655
  366.3 1.3 copy-start.18
  371.5 4.7 copy-start.31
  371.5 4.8 copy-start.9
  371.5 54.3 %all-to-all-start.1 = ((bf16[8,256,512]{1,2,0:T(8,128)(2,1)}), bf16[8,256,512]{1,2,0:T(8,128)(2,1)}, u32[]{:S(2)}, u32[]{:S(2)}) async-start(bf16[8,256,512]{1,2,0:T(8,128)(2,1)} %copy.22), calls=%async_computation.1 | async-start | bytes 4194304 | tf_op jit(solution)/shard_map/all_to_all | solution.py:655
  376.2 0.7 copy-start.30
  376.3 1.8 copy-start.19
  379.5 3.7 copy-start.1
  437.6 18.4 %slice-start = ((s8[4718592]{0:T(1024)(128)(4,1)}), s8[4194304]{0:T(1024)(128)(4,1)S(1)}, s32[]{:S(2)}) async-start(s8[4718592]{0:T(1024)(128)(4,1)} %bitcast.53), calls=%async_computation.5 | async-start | bytes 8388608
  444.6 11.4 %slice-start.1 = ((s8[4718592]{0:T(1024)(128)(4,1)}), s8[524288]{0:T(1024)(128)(4,1)S(1)}, s32[]{:S(2)}) async-start(s8[4718592]{0:T(1024)(128)(4,1)} %bitcast.53), calls=%async_computation.6 | async-start | bytes 1048576
  460.7 1.8 copy-start.10
  492.2 3.7 copy-start.2
  500.6 3.7 copy-start
  504.3 3.9 copy-start.28
Sparse Core Ops, SparseCore 0:
  229.4 53.5 all-gather.5
  292.2 75.3 all-gather.7
  369.2 73.4 all-gather.9

commit v4 on v3

--- a/solution.py
+++ b/solution.py
@@ -13,18 +13,20 @@
 NEG_BIG = -1e30
 HALF_PI = (1.5625, 0.0081787109375, 0.00011730194091796875, 3.129243850708008e-07, 9.920935796805404e-10)
 BWD_BLK = 256
+MIB = 1024 * 1024
+SENDS = 13
 BF = jnp.bfloat16
 F32 = jnp.float32
 MESH = pl.DeviceIdType.MESH
 
 
+def lane_mean(x):
+    return jnp.mean(x, axis=-1, keepdims=True)
+
+
 def rms_scale(x_f32, weight):
-    inv_rms = lax.rsqrt(jnp.mean(x_f32 * x_f32, axis=-1, keepdims=True) + EPS)
+    inv_rms = lax.rsqrt(lane_mean(x_f32 * x_f32) + EPS)
     return x_f32 * inv_rms * (1.0 + weight)
-
-
-def pre_norm(x_f32, weight):
-    return rms_scale(x_f32, weight).astype(BF)
 
 
 def norm_rope(head_bf, weight, cosines, sines):
@@ -100,15 +102,17 @@
             device_id_type=MESH,
         )
 
-    def blocks(self, first, last):
+    def blocks(self, hook=None):
         q_ref, k_ref, v_ref, o_ref, lse_ref, _, s_scr, acc = self.refs
         blk, head = self.blk, self.head
         scale = head ** -0.5
         wide = 2 * blk
         ahead = lax.broadcasted_iota(jnp.int32, (blk, wide), 0) - lax.broadcasted_iota(jnp.int32, (blk, wide), 1)
 
-        @pl.loop(first, last)
+        @pl.loop(0, self.group)
         def _(step):
+            if hook is not None:
+                pl.when(step == self.group // 2)(hook)
             i = lax.rem(self.me + step, self.group)
             rows = block_of(i, blk)
             q = q_ref[rows, :]
@@ -216,28 +220,29 @@
         self.got(b, RIGHT_1, LEFT_0)
         self.go(b, SIB_L1, SIB_R0)
 
-    def each_own(self, b, work):
-        self.got(b, SIB)
-
-        @pl.loop(0, 2)
+    def each(self, b, work, middle):
+        @pl.loop(0, 2 * self.chips)
         def _(t):
-            work(b, self.device(0, t))
-
-    def each_near(self, b, work):
-        self.got(b, SIB_L0, SIB_R1, SIB_L1, SIB_R0)
-
-        @pl.loop(0, 4)
-        def _(t):
-            work(b, self.device(1 + 2 * lax.rem(t, 2), t // 2))
-
-    def each_far(self, b, work):
-        self.got(b, RIGHT_F, LEFT_F)
-        self.go(b, SIB_O0, SIB_O1)
-        self.got(b, SIB_O0, SIB_O1)
-
-        @pl.loop(0, 2)
-        def _(t):
-            work(b, self.device(2, t))
+            @pl.when(t == 0)
+            def _():
+                self.got(b, SIB)
+
+            @pl.when(t == 2)
+            def _():
+                middle(b)
+                self.near(b)
+                self.got(b, SIB_L0, SIB_R1, SIB_L1, SIB_R0)
+
+            @pl.when(t == 6)
+            def _():
+                self.got(b, RIGHT_F, LEFT_F)
+                self.go(b, SIB_O0, SIB_O1)
+                self.got(b, SIB_O0, SIB_O1)
+
+            own, far = t < 2, t >= 6
+            chip_step = jnp.where(own, 0, jnp.where(far, 2, 1 + 2 * lax.rem(t, 2)))
+            other = jnp.where(own | far, lax.rem(t, 2), (t - 2) // 2)
+            work(b, self.device(chip_step, other))
 
     def sent(self):
         for plan in self.plans:
@@ -264,11 +269,11 @@
 
 
 def first_kernel(group, batch, x_ref, pos_ref, freq_ref, wpre_ref, qn_ref, kn_ref, wq_ref, wk_ref, wv_ref, full_ref, cos_out, sin_out, tok_ref, *rest):
-    per_out = [rest[b * 7:(b + 1) * 7] for b in range(batch)]
-    buf, w_ref, pos_all, s_scr, acc, cos_ref, sin_ref, o_send, o_recv, send_sem, recv_sem, out_sem, w_sem, p_send, p_recv, keep_sem, table_sem = rest[batch * 7:batch * 7 + 17]
-    kept = rest[batch * 7 + 17:]
-    per = [kept[b * 6:(b + 1) * 6] + (per_out[b][6],) for b in range(batch)]
-    outward = [[pltpu.make_async_copy(per[b][n], per_out[b][n], keep_sem.at[b, n]) for n in range(6)] for b in range(batch)]
+    per_out = [rest[:7], rest[7:12]]
+    buf, w_ref, pos_all, s_scr, acc, cos_ref, sin_ref, o_send, o_recv, send_sem, recv_sem, out_sem, w_sem, p_send, p_recv, keep_sem, table_sem = rest[12:29]
+    kept = rest[29:]
+    per = [kept[:6] + (per_out[0][6],), kept[6:]]
+    outward = [[pltpu.make_async_copy(per[b][n], per_out[b][n], keep_sem.at[b, n]) for n in range(6 - b)] for b in range(batch)]
     tables = [pltpu.make_async_copy(cos_ref, cos_out, table_sem.at[0]), pltpu.make_async_copy(sin_ref, sin_out, table_sem.at[1])]
     blk, _ = x_ref.shape[1:]
     head = qn_ref.shape[1]
@@ -282,7 +287,7 @@
     def _(t):
         rows = block_of(lax.rem(t, 4), blk // 4)
         x = x_ref[t // 4, rows, :].astype(F32)
-        inv = lax.rsqrt(jnp.mean(x * x, axis=-1, keepdims=True) + EPS)
+        inv = lax.rsqrt(lane_mean(x * x) + EPS)
         buf[t // 4, me, rows, :] = (x * inv * (1.0 + wpre_ref[...])).astype(BF)
 
     others_barrier(group, me)
@@ -306,7 +311,7 @@
 
     def norm_rope_block(raw, weight, cosines, sines):
         x = raw.astype(F32)
-        normed = x * lax.rsqrt(jnp.mean(x * x, axis=-1, keepdims=True) + EPS) * (1.0 + weight)
+        normed = x * lax.rsqrt(lane_mean(x * x) + EPS) * (1.0 + weight)
         first, second = normed[:, :head // 2], normed[:, head // 2:]
         return jnp.concatenate([first * cosines - second * sines, second * cosines + first * sines], axis=1).astype(BF)
 
@@ -338,29 +343,22 @@
         copy.start()
     for load in loads:
         load.wait()
-    attention = [Attention(group, me, b, *per[b][:3], *per[b][5:], tok_ref, s_scr, acc, o_send, o_recv) for b in range(batch)]
-    ring.each_own(0, project)
+    attention = Attention(group, me, 0, *per[0][:3], *per[0][5:], tok_ref, s_scr, acc, o_send, o_recv)
+
+    def middle(b):
+        if b:
+            attention.blocks(lambda: ring.turn(b))
+            attention.flush()
+            outward[0][5].start()
+        else:
+            ring.turn(b)
+            ring.open(b + 1)
+
     for b in range(batch):
-        if b:
-            ring.each_own(b, project)
-            attention[b - 1].blocks(0, group // 2)
-        ring.turn(b)
-        if b + 1 < batch:
-            ring.open(b + 1)
-        if b:
-            attention[b - 1].blocks(group // 2, group)
-            attention[b - 1].flush()
-            outward[b - 1][5].start()
-        ring.near(b)
-        ring.each_near(b, project)
-        ring.each_far(b, project)
+        ring.each(b, project, middle)
         for copy in outward[b][:5]:
             copy.start()
-    attention[-1].blocks(0, group)
-    attention[-1].flush()
-    outward[-1][5].start()
-    for b in range(batch):
-        attention[b].finish()
+    attention.finish()
     ring.sent()
     for copy in tables + sum(outward, []):
         copy.wait()
@@ -384,35 +382,43 @@
     table = jax.ShapeDtypeStruct((seq, head // 2), F32)
     outs = pl.pallas_call(
         functools.partial(first_kernel, group, batch),
-        out_shape=(jax.ShapeDtypeStruct((batch, seq, width), BF), table, table, jax.ShapeDtypeStruct((batch * blk, group * head), BF))
-        + ((heads_out,) * 6 + (jax.ShapeDtypeStruct((1, seq), F32),)) * batch,
+        out_shape=(jax.ShapeDtypeStruct((batch, seq, width), BF), table, table, jax.ShapeDtypeStruct((blk, group * head), BF))
+        + (heads_out,) * 6 + (jax.ShapeDtypeStruct((1, seq), F32),) + (heads_out,) * 5,
         in_specs=[VMEM] * 6 + [ANYWHERE] * 3,
-        out_specs=(ANYWHERE,) * 3 + (VMEM,) + ((ANYWHERE,) * 6 + (VMEM,)) * batch,
+        out_specs=(ANYWHERE,) * 3 + (VMEM,) + (ANYWHERE,) * 6 + (VMEM,) + (ANYWHERE,) * 5,
         scratch_shapes=[pltpu.VMEM((batch, group, blk, width), BF), pltpu.VMEM((width, 3 * head), BF), pltpu.VMEM((group, 1, blk), F32),
                         pltpu.VMEM((blk, seq), F32), pltpu.VMEM((blk, head), F32), pltpu.VMEM((seq, head // 2), F32), pltpu.VMEM((seq, head // 2), F32),
-                        DMA((batch, group)), DMA((batch, group)), DMA((batch, 13)), DMA((batch, 13)), DMA((batch, group)), DMA((3,)), DMA((group,)), DMA((group,)),
-                        DMA((batch, 6)), DMA((2,))] + [pltpu.VMEM((seq, head), BF)] * (6 * batch),
+                        DMA((1, group)), DMA((1, group)), DMA((batch, SENDS)), DMA((batch, SENDS)), DMA((batch, group)), DMA((3,)), DMA((group,)), DMA((group,)),
+                        DMA((batch, 6)), DMA((2,))] + [pltpu.VMEM((seq, head), BF)] * 11,
         cost_estimate=pl.CostEstimate(flops=90 * 10 ** 9, bytes_accessed=2 * batch * seq * width, transcendentals=seq * seq),
-        compiler_params=pltpu.CompilerParams(vmem_limit_bytes=62 * 1024 * 1024, collective_id=cid, has_side_effects=True),
+        compiler_params=pltpu.CompilerParams(vmem_limit_bytes=62 * MIB, collective_id=cid, has_side_effects=True),
         name='first',
     )(x, pos, freq, w_pre[None, :], q_norm[None, :], k_norm[None, :], w_q, w_k, w_v)
-    return outs[:4] + (tuple(outs[4 + 7 * b:11 + 7 * b] for b in range(batch)),)
+    return outs[:4] + ((outs[4:11], outs[11:16]),)
 
 
 def second_kernel(group, batch, tok_ref, wpost_ref, lse_ref, wo_hbm, x_hbm, dy_hbm, *rest):
-    late_hbm, rest = rest[:3 + batch], rest[3 + batch:]
+    late_hbm, rest = rest[:7], rest[7:]
+    lse1_ref, rest = rest[0], rest[1:]
     y_hbm, dwpost_ref, dwo_ref, dq_ref, dk_ref, dv_ref = rest[:6]
     do_refs, dl_refs, rest = rest[6:6 + batch], rest[6 + batch:6 + 2 * batch], rest[6 + 2 * batch:]
     buf, dq_acc, dwo_acc, wo_ref, x_ref, dy_ref, p_scr, send_sem, recv_sem, wo_sem, act_sem, late_sem, y_sem = rest[:13]
-    late = rest[13:]
-    q_ref, k_ref, v_ref = late[:3]
-    o_refs = late[3:]
+    tok1_ref, s_scr, acc, o_send, o_recv, o1_ref = rest[13:19]
+    late = rest[19:]
+    q1_ref, k1_ref, v1_ref, q_ref, k_ref, v_ref, o0_ref = late
+    o_refs = (o0_ref, o1_ref)
+    toks = (tok_ref, tok1_ref)
     blk, width = x_ref.shape[1:]
     head = dwo_ref.shape[0]
     me = lax.axis_index('sp')
     mine = block_of(me, head)
     part = width // wo_sem.shape[0]
-    wo_loads = [pltpu.make_async_copy(wo_hbm.at[:, pl.ds(n * part, part)], wo_ref.at[:, pl.ds(n * part, part)], wo_sem.at[n]) for n in range(width // part)]
+
+    def wo_load(n):
+        cols = block_of(n, part)
+        return pltpu.make_async_copy(wo_hbm.at[:, cols], wo_ref.at[:, cols], wo_sem.at[n])
+
+    wo_loads = [wo_load(n) for n in range(width // part)]
     act_loads = [[pltpu.make_async_copy(src.at[b], dst.at[b], act_sem.at[b, n]) for n, (src, dst) in enumerate(((x_hbm, x_ref), (dy_hbm, dy_ref)))] for b in range(batch)]
     late_loads = [pltpu.make_async_copy(src, dst, late_sem.at[n]) for n, (src, dst) in enumerate(zip(late_hbm, late))]
     for load in wo_loads + sum(act_loads, []) + late_loads:
@@ -422,10 +428,13 @@
     y_copies = [pltpu.make_async_copy(x_ref.at[b], y_hbm.at[b], y_sem.at[b]) for b in range(batch)]
 
     def project(b):
-        for n in range(width // part):
+        @pl.loop(0, width // part)
+        def _(n):
             if b == 0:
-                wo_loads[n].wait()
-            p_scr[:, n * part:(n + 1) * part] = nn(tok_ref[b * blk:(b + 1) * blk, :], wo_ref[:, n * part:(n + 1) * part]).astype(BF)
+                wo_load(n).wait()
+            cols = block_of(n, part)
+            p_scr[:, cols] = nn(toks[b][...], wo_ref[:, cols]).astype(BF)
+
         for load in act_loads[b]:
             load.wait()
         gain = 1.0 + wpost_ref[...]
@@ -436,12 +445,12 @@
             rows = block_of(t, rows_each)
             p = p_scr[rows, :].astype(F32)
             dy = dy_ref[b, rows, :].astype(F32)
-            inv = lax.rsqrt(jnp.mean(p * p, axis=-1, keepdims=True) + EPS)
+            inv = lax.rsqrt(lane_mean(p * p) + EPS)
             unit = p * inv
             x_ref[b, rows, :] = (x_ref[b, rows, :].astype(F32) + unit * gain).astype(BF)
             scaled = dy * gain
             dwpost_ref[...] += jnp.sum(dy * unit, axis=0, keepdims=True)
-            buf[b, me, rows, :] = (inv * (scaled - unit * jnp.mean(scaled * unit, axis=-1, keepdims=True))).astype(BF)
+            buf[b, me, rows, :] = (inv * (scaled - unit * lane_mean(scaled * unit))).astype(BF)
 
         y_copies[b].start()
 
@@ -458,57 +467,57 @@
         dl_refs[b][:, rows] = as_row(jnp.sum(d_o.astype(F32) * o.astype(F32), axis=1, keepdims=True))
         dwo_acc[...] += tn(o, chunk)
 
-    def backward(first, last):
-        bwd_blocks(first, last, q_ref, k_ref, v_ref, do_refs[0], lse_ref, dl_refs[0], dq_acc, dk_ref, dv_ref)
+    def backward(hook):
+        bwd_blocks(0, group, 3, hook, q_ref, k_ref, v_ref, do_refs[0], lse_ref, dl_refs[0], dq_acc, dk_ref, dv_ref)
 
     ring.open(0)
-    for b in range(1, batch):
-        project(b)
     for load in late_loads:
         load.wait()
-    ring.each_own(0, work)
+    attention = Attention(group, me, 0, q1_ref, k1_ref, v1_ref, o1_ref, lse1_ref, tok1_ref, s_scr, acc, o_send, o_recv)
+    attention.blocks()
+    attention.flush()
+    ring.turn(0)
+    attention.finish()
+    project(1)
+    ring.open(1)
+
+    def middle(b):
+        if b:
+            bwd_start(dq_acc, dk_ref, dv_ref)
+            backward(lambda: ring.turn(b))
+            dq_ref[...] = dq_acc[...].astype(BF)
+
     for b in range(batch):
-        if b:
-            ring.each_own(b, work)
-            bwd_start(dq_acc, dk_ref, dv_ref)
-            backward(0, 3)
-        ring.turn(b)
-        if b + 1 < batch:
-            ring.open(b + 1)
-        if b:
-            backward(3, group)
-            dq_ref[...] = dq_acc[...].astype(BF)
-        ring.near(b)
-        ring.each_near(b, work)
-        ring.each_far(b, work)
+        ring.each(b, work, middle)
     dwo_ref[...] = dwo_acc[...].astype(BF)
     ring.sent()
     for copy in y_copies:
         copy.wait()
 
 
-def second(tok, w_o, x, dy, w_post, q, k, v, lse, outs, group, cid):
+def second(tok, w_o, x, dy, w_post, lse, late, group, cid):
     batch, blk, width = x.shape
-    seq, head = q.shape
+    seq, head = late[0].shape
     assert batch == 2 and group == 8
     wide = jax.ShapeDtypeStruct((seq, head), F32)
     half = jax.ShapeDtypeStruct((seq, head), BF)
     row = jax.ShapeDtypeStruct((1, seq), F32)
     res = pl.pallas_call(
         functools.partial(second_kernel, group, batch),
-        out_shape=(jax.ShapeDtypeStruct(x.shape, BF), jax.ShapeDtypeStruct((1, width), F32), jax.ShapeDtypeStruct((head, width), BF), half, wide, wide)
+        out_shape=(row, jax.ShapeDtypeStruct(x.shape, BF), jax.ShapeDtypeStruct((1, width), F32), jax.ShapeDtypeStruct((head, width), BF), half, wide, wide)
         + (half,) * batch + (row,) * batch,
-        in_specs=[VMEM] * 3 + [ANYWHERE] * (6 + batch),
-        out_specs=(ANYWHERE,) + (VMEM,) * (5 + 2 * batch),
+        in_specs=[VMEM] * 3 + [ANYWHERE] * 10,
+        out_specs=(VMEM, ANYWHERE) + (VMEM,) * (5 + 2 * batch),
         scratch_shapes=[pltpu.VMEM((batch, group, blk, width), BF), pltpu.VMEM((seq, head), F32), pltpu.VMEM((head, width), F32),
                         pltpu.VMEM(w_o.shape, BF), pltpu.VMEM(x.shape, BF), pltpu.VMEM(x.shape, BF), pltpu.VMEM((blk, width), BF),
-                        DMA((batch, 13)), DMA((batch, 13)), DMA((3,)), DMA((batch, 2)), DMA((3 + batch,)), DMA((batch,))]
-        + [pltpu.VMEM((seq, head), BF)] * (3 + batch),
+                        DMA((batch, SENDS)), DMA((batch, SENDS)), DMA((3,)), DMA((batch, 2)), DMA((7,)), DMA((batch,)),
+                        pltpu.VMEM(tok.shape, BF), pltpu.VMEM((blk, seq), F32), pltpu.VMEM((blk, head), F32), DMA((1, group)), DMA((1, group))]
+        + [pltpu.VMEM((seq, head), BF)] * 8,
         cost_estimate=pl.CostEstimate(flops=80 * 10 ** 9, bytes_accessed=2 * batch * seq * width, transcendentals=seq * seq),
-        compiler_params=pltpu.CompilerParams(vmem_limit_bytes=63 * 1024 * 1024, collective_id=cid, has_side_effects=True),
+        compiler_params=pltpu.CompilerParams(vmem_limit_bytes=63 * MIB, collective_id=cid, has_side_effects=True),
         name='second',
-    )(tok, w_post[None, :], lse, w_o, x, dy, q, k, v, *outs)
-    return res[0], res[1][0], res[2:6], res[6:6 + batch], res[6 + batch:]
+    )(tok, w_post[None, :], lse, w_o, x, dy, *late)
+    return res[0], res[1], res[2][0], res[3:7], res[7:7 + batch], res[7 + batch:]
 
 
 def bwd_start(*accs):
@@ -516,7 +525,7 @@
         acc[...] = jnp.zeros_like(acc)
 
 
-def bwd_blocks(first, last, q_ref, k_ref, v_ref, do_ref, lse_ref, dl_ref, dq_acc, dk_ref, dv_ref):
+def bwd_blocks(first, last, hook_at, hook, q_ref, k_ref, v_ref, do_ref, lse_ref, dl_ref, dq_acc, dk_ref, dv_ref):
     seq, head = q_ref.shape
     scale = head ** -0.5
     wide = 2 * BWD_BLK
@@ -524,6 +533,8 @@
 
     @pl.loop(first, last)
     def _(j):
+        if hook is not None:
+            pl.when(j == hook_at)(hook)
         cols = block_of(j, BWD_BLK)
         k = k_ref[cols, :]
         v = v_ref[cols, :]
@@ -551,7 +562,7 @@
 
 def bwd_kernel(q_ref, k_ref, v_ref, do_ref, lse_ref, dl_ref, dq_ref, dk_ref, dv_ref, dq_acc):
     bwd_start(dq_acc, dk_ref, dv_ref)
-    bwd_blocks(0, q_ref.shape[0] // BWD_BLK, q_ref, k_ref, v_ref, do_ref, lse_ref, dl_ref, dq_acc, dk_ref, dv_ref)
+    bwd_blocks(0, q_ref.shape[0] // BWD_BLK, 0, None, q_ref, k_ref, v_ref, do_ref, lse_ref, dl_ref, dq_acc, dk_ref, dv_ref)
     dq_ref[...] = dq_acc[...].astype(BF)
 
 
@@ -566,9 +577,119 @@
         out_specs=(pl.BlockSpec(memory_space=pltpu.VMEM),) * 3,
         scratch_shapes=[pltpu.VMEM((seq, head), F32)],
         cost_estimate=pl.CostEstimate(flops=10 * pairs * head, bytes_accessed=20 * seq * head, transcendentals=pairs),
-        compiler_params=pltpu.CompilerParams(vmem_limit_bytes=32 * 1024 * 1024),
+        compiler_params=pltpu.CompilerParams(vmem_limit_bytes=32 * MIB),
         name='attn_bwd',
     )(q, k, v, do, lse, delta)
+
+
+def dw_kernel(d0_ref, d1_ref, a_hbm, out_ref, acc, a_buf, a_sem):
+    seq, pair = d0_ref.shape
+    width = a_buf.shape[2]
+    head = pair // 2
+    chunk = a_buf.shape[1]
+    per_seq = seq // chunk
+
+    def a_load(n):
+        return pltpu.make_async_copy(a_hbm.at[n // per_seq, block_of(lax.rem(n, per_seq), chunk), :], a_buf.at[lax.rem(n, 2)], a_sem.at[lax.rem(n, 2)])
+
+    a_load(0).start()
+    acc[...] = jnp.zeros_like(acc)
+
+    @pl.loop(0, 2 * per_seq)
+    def _(n):
+        @pl.when(n + 1 < 2 * per_seq)
+        def _():
+            a_load(n + 1).start()
+
+        a_load(n).wait()
+        rows = block_of(lax.rem(n, per_seq), chunk)
+
+        def add(d_ref):
+            @pl.loop(0, 2)
+            def _(h):
+                part = block_of(h, head)
+                acc[part, :] += tn(d_ref[rows, part], a_buf[lax.rem(n, 2)])
+
+        pl.when(n < per_seq)(lambda: add(d0_ref))
+        pl.when(n >= per_seq)(lambda: add(d1_ref))
+
+    @pl.loop(0, width // head)
+    def _(r):
+        cols = block_of(r, head)
+        out_ref[cols, :] = acc[:, cols].T.astype(BF)
+
+
+def weight_grad(d_mine, a_both):
+    seq, pair = d_mine[0].shape
+    width = a_both.shape[2]
+    return pl.pallas_call(
+        dw_kernel,
+        out_shape=jax.ShapeDtypeStruct((width, pair), BF),
+        in_specs=[VMEM, VMEM, ANYWHERE],
+        out_specs=VMEM,
+        scratch_shapes=[pltpu.VMEM((pair, width), F32), pltpu.VMEM((2, 512, width), BF), DMA((2,))],
+        cost_estimate=pl.CostEstimate(flops=4 * seq * pair * width, bytes_accessed=4 * seq * width, transcendentals=0),
+        compiler_params=pltpu.CompilerParams(vmem_limit_bytes=48 * MIB),
+        name='weight_grad',
+    )(*d_mine, a_both)
+
+
+def dx_kernel(t0_ref, t1_ref, x_ref, dy_ref, wpre_ref, wq_hbm, wk_hbm, wv_hbm, dx_ref, sum_ref, da, w_buf, w_sem):
+    batch, blk, _ = x_ref.shape
+    head = w_buf.shape[2] // 4
+    chips = wk_hbm.shape[1] // head
+
+    def w_loads(c):
+        slot = lax.rem(c, 2)
+        sources = (wq_hbm.at[:, block_of(2 * c, head)], wk_hbm.at[:, block_of(c, head)], wq_hbm.at[:, block_of(2 * c + 1, head)], wv_hbm.at[:, block_of(c, head)])
+        return [pltpu.make_async_copy(src, w_buf.at[slot, :, pl.ds(n * head, head)], w_sem.at[slot, n]) for n, src in enumerate(sources)]
+
+    for load in w_loads(0):
+        load.start()
+    da[...] = jnp.zeros_like(da)
+
+    @pl.loop(0, chips)
+    def _(c):
+        @pl.when(c + 1 < chips)
+        def _():
+            for load in w_loads(c + 1):
+                load.start()
+
+        for load in w_loads(c):
+            load.wait()
+        for b, t_ref in enumerate((t0_ref, t1_ref)):
+            da[b * blk:(b + 1) * blk, :] += nt(t_ref[:, block_of(c, 4 * head)], w_buf[lax.rem(c, 2)])
+
+    gain = 1.0 + wpre_ref[...]
+    rows_each = 32
+    sum_ref[...] = jnp.zeros_like(sum_ref)
+
+    @pl.loop(0, batch * blk // rows_each)
+    def _(t):
+        per_b = blk // rows_each
+        rows = block_of(lax.rem(t, per_b), rows_each)
+        x = x_ref[t // per_b, rows, :].astype(F32)
+        d = da[block_of(t, rows_each), :].astype(BF).astype(F32)
+        inv = lax.rsqrt(lane_mean(x * x) + EPS)
+        unit = x * inv
+        scaled = d * gain
+        sum_ref[...] += jnp.sum(d * unit, axis=0, keepdims=True)
+        dx_ref[t // per_b, rows, :] = (dy_ref[t // per_b, rows, :].astype(F32) + inv * (scaled - unit * lane_mean(scaled * unit))).astype(BF)
+
+
+def input_grad(tokens, x, dy, w_pre, w_q, w_k, w_v, head):
+    batch, blk, width = x.shape
+    size = batch * blk * tokens[0].shape[1] * width
+    return pl.pallas_call(
+        dx_kernel,
+        out_shape=(jax.ShapeDtypeStruct(x.shape, BF), jax.ShapeDtypeStruct((1, width), F32)),
+        in_specs=[VMEM] * 5 + [ANYWHERE] * 3,
+        out_specs=(VMEM, VMEM),
+        scratch_shapes=[pltpu.VMEM((batch * blk, width), F32), pltpu.VMEM((2, width, 4 * head), BF), DMA((2, 4))],
+        cost_estimate=pl.CostEstimate(flops=2 * size, bytes_accessed=4 * width * width, transcendentals=0),
+        compiler_params=pltpu.CompilerParams(vmem_limit_bytes=48 * MIB),
+        name='input_grad',
+    )(*tokens, x, dy, w_pre[None, :], w_q, w_k, w_v)
 
 
 def move_kernel(*refs):
@@ -585,22 +706,33 @@
         in_specs=in_specs,
         out_specs=out_specs,
         cost_estimate=pl.CostEstimate(flops=20 * size, bytes_accessed=4 * size, transcendentals=0),
-        compiler_params=pltpu.CompilerParams(vmem_limit_bytes=32 * 1024 * 1024),
+        compiler_params=pltpu.CompilerParams(vmem_limit_bytes=60 * MIB),
     )(*operands)
 
 
-def spread_q(parts):
-    group, rows, head = parts.shape
-    return move((group,), (jax.ShapeDtypeStruct((rows, group * head), BF),),
-                [pl.BlockSpec((1, rows, head), lambda c: (c, 0, 0))], (pl.BlockSpec((rows, head), lambda c: (0, c)),), (parts,))[0]
-
-
-def spread_kv(parts):
-    group, rows, head = parts.shape
-    shape = jax.ShapeDtypeStruct((rows, group // 2 * head), BF)
-    out = pl.BlockSpec((rows, head), lambda c: (0, c))
-    return move((group // 2,), (shape, shape),
-                [pl.BlockSpec((1, rows, head), lambda c: (2 * c, 0, 0)), pl.BlockSpec((1, rows, head), lambda c: (2 * c + 1, 0, 0))], (out, out), (parts, parts))
+def spread(parts):
+    group, rows, pair = parts.shape
+    head = pair // 2
+    tile = rows // 2
+    narrow = jax.ShapeDtypeStruct((rows, group // 2 * head), BF)
+
+    def body(even, odd, q_out, k_out, v_out):
+        q_out[:, :head] = even[0, :, :head]
+        q_out[:, head:] = odd[0, :, :head]
+        k_out[...] = even[0, :, head:]
+        v_out[...] = odd[0, :, head:]
+
+    thin = pl.BlockSpec((tile, head), lambda r, c: (r, c))
+    return pl.pallas_call(
+        body,
+        grid=(2, group // 2),
+        out_shape=(jax.ShapeDtypeStruct((rows, group * head), BF), narrow, narrow),
+        in_specs=[pl.BlockSpec((1, tile, pair), lambda r, c: (2 * c, r, 0)), pl.BlockSpec((1, tile, pair), lambda r, c: (2 * c + 1, r, 0))],
+        out_specs=(pl.BlockSpec((tile, 2 * head), lambda r, c: (r, c)), thin, thin),
+        cost_estimate=pl.CostEstimate(flops=20 * parts.size, bytes_accessed=4 * parts.size, transcendentals=0),
+        compiler_params=pltpu.CompilerParams(vmem_limit_bytes=60 * MIB),
+        name='spread',
+    )(parts, parts)
 
 
 def place(whole):
@@ -613,7 +745,7 @@
     group = mesh.shape['sp']
 
     def device_step(x_in, dy_in, positions, w_q, w_k, w_v, w_o, w_pre, w_post, q_norm, k_norm):
-        batch, seq_loc, width = x_in.shape
+        batch, _, _ = x_in.shape
         head = q_norm.shape[0]
         heads = w_q.shape[1] // head
         kv_heads = w_k.shape[1] // head
@@ -627,18 +759,18 @@
             x_in, positions.astype(F32)[None, :], inv_freq[None, :], w_pre, q_norm, k_norm, w_q, w_k, w_v, group, 0)
         roper = functools.partial(norm_rope, cosines=cosines, sines=sines)
 
-        y_out, dw_post, (dw_o, dq0, dk0, dv0), d_os, deltas = second(
-            tok, w_o, x_in, dy_in, w_post, *per[0][:3], per[0][6], [p[5] for p in per], group, 1)
+        lse1, y_out, dw_post, (dw_o, dq0, dk0, dv0), d_os, deltas = second(
+            tok, w_o, x_in, dy_in, w_post, per[0][6], (*per[1][:3], *per[0][:3], per[0][5]), group, 1)
         dw_o_all = lax.all_gather(dw_o, 'sp', axis=0, tiled=True)
 
         d_mine, dqkv_tok = [], []
         dq_norm = dk_norm = 0.0
         for b in range(batch):
-            q_rot, k_rot, v_raw, q_raw, k_raw, _, lse = per[b]
+            q_rot, k_rot, v_raw, q_raw, k_raw = per[b][:5]
             if b == 0:
                 dq_rot, dk_part, dv_part = dq0, dk0, dv0
             else:
-                lse, _ = lax.optimization_barrier((lse, d_mine[b - 1]))
+                lse, _ = lax.optimization_barrier((lse1, d_mine[b - 1]))
                 dq_rot, dk_part, dv_part = attn_bwd(q_rot, k_rot, v_raw, d_os[b], lse, deltas[b])
             other = lax.ppermute(jnp.where(even, dv_part, dk_part), 'sp', swap)
             dkv = (jnp.where(even, dk_part, dv_part) + other).astype(BF)
@@ -654,28 +786,17 @@
                 d_two, dqkv_tok[b - 1] = lax.optimization_barrier((d_two, dqkv_tok[b - 1]))
             dqkv_tok.append(lax.all_to_all(d_two, 'sp', 0, 1, tiled=True))
 
-        dw_q_part = sum(tn(a_both[b], d_mine[b][:, :head]) for b in range(batch)).astype(BF)
-        dw_q_parts = lax.all_gather(dw_q_part, 'sp', axis=0, tiled=False)
-        dw_kv_part = sum(tn(a_both[b], d_mine[b][:, head:]) for b in range(batch)).astype(BF)
-        dw_kv_parts = lax.all_gather(dw_kv_part, 'sp', axis=0, tiled=False)
+        dw_all = lax.all_gather(weight_grad(d_mine, a_both), 'sp', axis=0, tiled=False)
         dw_o_all = place(dw_o_all)
         dqkv_tok[1], dw_o_all = lax.optimization_barrier((dqkv_tok[1], dw_o_all))
-
-        d_tok = jnp.concatenate(dqkv_tok, axis=0)
-        d_tok = [d_tok[:, j * head:(j + 1) * head] for j in range(2 * group)]
-        d_normed = (nt(jnp.concatenate(d_tok[0::2], axis=1), w_q)
-                    + nt(jnp.concatenate(d_tok[1::4], axis=1), w_k)
-                    + nt(jnp.concatenate(d_tok[3::4], axis=1), w_v)).astype(BF).reshape(batch, seq_loc, width)
-        _, pre_pull = jax.vjp(pre_norm, x_in.astype(F32), w_pre)
-        dx_norm, dw_pre = pre_pull(d_normed)
-        dx_out = (dy_in.astype(F32) + dx_norm).astype(BF)
-        dw_q_all = spread_q(dw_q_parts)
-        dw_k_all, dw_v_all = spread_kv(dw_kv_parts)
+        dx_out, dw_pre = input_grad(dqkv_tok, x_in, dy_in, w_pre, w_q, w_k, w_v, head)
+        dw_q_all, dw_k_all, dw_v_all = spread(dw_all)
+        dw_pre = dw_pre[0]
         small = lax.psum((dw_pre, dw_post, dq_norm, dk_norm), 'sp')
         return (y_out, dx_out, dw_q_all, dw_k_all, dw_v_all, dw_o_all) + small
 
     token_spec = P('dp', 'sp', None)
     return jax.shard_map(device_step, mesh=mesh,
-                         in_specs=(token_spec, token_spec, P(('dp', 'sp')), P(None, None), P(None, None), P(None, None), P(None, None), P(None), P(None), P(None), P(None)),
-                         out_specs=(token_spec, token_spec, P('dp', None), P('dp', None), P('dp', None), P('dp', None), P('dp'), P('dp'), P('dp'), P('dp')),
+                         in_specs=(token_spec, token_spec, P(('dp', 'sp'))) + (P(None, None),) * 4 + (P(None),) * 4,
+                         out_specs=(token_spec, token_spec) + (P('dp', None),) * 4 + (P('dp'),) * 4,
                          check_vma=False)

time: 526 us -> 469 us (0.89)
  the two profiles are of different devices: /device:TPU:80 before, /device:TPU:120 now
where the time goes in v4:
time: 469 us; the launch traced here: 468 us
  Pallas kernels  289 us (62%)
  blocking collectives  72.6 us (15%)
  waiting for transfers between devices  55.6 us (12%)
  other arithmetic  16.5 us (4%)
  between operations  14.5 us (3%)
  local copies, waits for them, and re-layouts  12.9 us (3%)
  starting transfers between devices  6.72 us (1%)
    pallas_call x1, Pallas kernels, second(): pl.pallas_call(functools.partial(second_kernel, group, batch), out_shape=...  112 us
    pallas_call x1, Pallas kernels, first(): pl.pallas_call(functools.partial(first_kernel, group, batch), out_shape=(...  98.1 us
    all_to_all x1, waiting for transfers between devices, device_step(): dqkv_tok.append(lax.all_to_all(d_two, 'sp', 0, 1, tiled=True))  49.6 us
    all_to_all x1, blocking collectives, device_step(): dqkv_tok.append(lax.all_to_all(d_two, 'sp', 0, 1, tiled=True))  48.2 us
    psum x1, blocking collectives, device_step(): small = lax.psum((dw_pre, dw_post, dq_norm, dk_norm), 'sp')  24.4 us
    pallas_call x1, Pallas kernels, input_grad(): pl.pallas_call(dx_kernel, out_shape=(jax.ShapeDtypeStruct(x.shape, BF), j...  21.6 us
    pallas_call x1, Pallas kernels, weight_grad(): pl.pallas_call(dw_kernel, out_shape=jax.ShapeDtypeStruct((width, pair), B...  19.5 us
    pallas_call x1, Pallas kernels, spread(): pl.pallas_call(body, grid=(2, group // 2), out_shape=(jax.ShapeDtypeStruc...  15.1 us
  transfers between devices with their start and end apart: 5, of which 3 were waited for; matrix products, arithmetic and copies ran while one was open for 4% of the time, Pallas kernels for 14%

profile of v4, /device:TPU:120, one launch (start us, length us, event | category | flops | bytes accessed | tf_op | source)
XLA Modules:
  0.0 467.7 jit_solution(13005089658285262481)
XLA Ops:
  7.2 0.1 all-gather.4.cloned.1.call-start
  7.3 0.5 multiply_power_fusion.freq_ref
  7.8 1.2 convert_element_type.45
  9.0 1.3 broadcast_in_dim.43.wpre_ref
  10.3 1.3 broadcast_in_dim.46.wpost_ref
  11.6 98.1 %first.1 = (bf16[2,2048,2304]{2,1,0:T(8,128)(2,1)}, f32[2048,128]{1,0:T(8,128)}, f32[2048,128]{1,0:T(8,128)}, bf16[256,2048]{1,0:T(8,128)(2,1)}, bf16[2048,256]{...) custom-call(bf16[2,256,2304]{2,1,0:T(8,128)(2,1)} %x_ref.3, ...), custom_call_target="tpu_custom_call" | custom-call | flops 89999998976 | bytes 18874368 | tf_op jit(solution)/shard_map/first/pallas_call | solution.py:383
  109.8 111.6 %second.1 = (f32[1,2048]{1,0:T(1,128)}, bf16[2,256,2304]{2,1,0:T(8,128)(2,1)}, f32[1,2304]{1,0:T(1,128)}, bf16[256,2304]{1,0:T(8,128)(2,1)}, bf16[2048,256]{1,0:...) custom-call(bf16[256,2048]{1,0:T(8,128)(2,1)} %get-tuple-element.48., ...), custom_call_target="tpu_custom_call" | custom-call | flops 80000000000 | bytes 18874368 | tf_op jit(solution)/shard_map/second/pallas_call | solution.py:505
  221.4 0.1 all-gather.4.cloned.1.call-update
  221.5 0.2 all-gather.6.cloned.1.call-start
  221.7 0.0 copy-start.17
  221.7 0.0 copy-start.13
  221.7 2.0 broadcast_select_fusion.1
  223.8 0.0 copy-start.11
  223.8 1.1 collective-permute-start
  224.8 0.0 copy-done.17
  224.9 0.2 convert_element_type.46
  225.0 0.0 copy-done.11
  225.0 0.3 fusion.8
  225.4 0.2 copy-done.19
  225.6 0.0 copy-done.20
  225.6 0.0 copy-start.15
  225.6 3.0 collective-permute-done
  228.6 0.0 copy-done.13
  228.6 0.4 fusion.27
  229.1 0.5 multiply_add_fusion.7
  229.6 0.8 copy-done.9
  230.4 1.2 fusion.11
  231.7 0.9 fusion.7
  232.6 0.7 fusion
  233.4 1.0 fusion.21
  234.4 0.2 pad_maximum_fusion.d0_ref
  234.6 1.0 copy-done.2
  235.6 0.3 copy-done.3
  235.9 0.3 copy-done.4
  236.2 0.3 copy-done.5
  236.5 13.4 %attn_bwd.1 = (bf16[2048,256]{1,0:T(8,128)(2,1)S(1)}, f32[2048,256]{1,0:T(8,128)S(1)}, f32[2048,256]{1,0:T(8,128)S(1)}) custom-call(bf16[2048,256]{1,0:T(8,128)(2,1)S(1)} %copy-done.2, bf16[2048,256]{1,0:T(8,128)(2,1)S(1)} %copy-done.3, bf16[2048,256]{1,0:T(8,128)(2,1)S(1)} %copy-done.4, bf16[2048,256]{1,0:T(8,128)(2,1)S(1)} %copy-done.5, ...), custom_call_target="tpu_custom_call" | custom-call | flops 6039797760 | bytes 10485760 | tf_op jit(solution)/shard_map/attn_bwd/pallas_call | solution.py:573
  250.0 0.3 broadcast_select_fusion
  250.3 0.5 collective-permute-start.1
  250.8 0.4 copy-done.10
  251.2 0.3 fusion.16
  251.6 0.1 copy-done.8
  251.6 0.3 fusion.12
  252.0 0.2 convert_element_type.53
  252.2 2.8 collective-permute-done.1
  255.0 0.5 fusion.26
  255.5 0.5 multiply_add_fusion.3
  255.9 0.9 fusion.19
  256.9 0.9 fusion.15
  257.9 0.7 fusion.2
  258.6 1.0 fusion.20
  259.5 1.5 pad_maximum_fusion.1.d1_ref
  261.0 19.5 %weight_grad.1 = bf16[2304,512]{1,0:T(8,128)(2,1)} custom-call(bf16[2048,512]{1,0:T(8,128)(2,1)S(1)} %pad_maximum_fusion.d0_ref, bf16[2048,512]{1,0:T(8,128)(2,1)} %pad_maximum_fusion.1.d1_ref, bf16[2,2048,2304]{2,1,0:T(8,128)(2,1)} %get-tuple-element.79.a_hbm), custom_call_target="tpu_custom_call" | custom-call | flops 9663676416 | bytes 18874368 | tf_op jit(solution)/shard_map/weight_grad/pallas_call | solution.py:625
  280.6 0.1 all-gather.6.cloned.1.call-update
  280.6 48.2 %all_to_all.38 = bf16[8,256,512]{2,1,0:T(8,128)(2,1)S(1)} all-to-all(bf16[8,256,512]{2,1,0:T(8,128)(2,1)S(1)} %bitcast.12), channel_id=1, replica_groups=mesh['dp'=4,'sp'=8] {'sp'}, dimensions={0} | all-to-all | bytes 4194304 | tf_op jit(solution)/shard_map/all_to_all | solution.py:787
  328.8 0.3 copy.23
  329.1 4.9 %all-to-all-start.1 = ((bf16[8,256,512]{2,1,0:T(8,128)(2,1)}), bf16[8,256,512]{2,1,0:T(8,128)(2,1)}, u32[]{:S(2)}, u32[]{:S(2)}) async-start(bf16[8,256,512]{2,1,0:T(8,128)(2,1)} %bitcast.5), calls=%async_computation.1 | async-start | bytes 4194304 | tf_op jit(solution)/shard_map/all_to_all | solution.py:787
  334.0 49.6 %all-to-all-done.1 = bf16[8,256,512]{2,1,0:T(8,128)(2,1)} async-done(((bf16[8,256,512]{2,1,0:T(8,128)(2,1)}), bf16[8,256,512]{2,1,0:T(8,128)(2,1)}, u32[]{:S(2)}, u32[]{:S(2)}) %all-to-all-start.1) | async-done | bytes 2097184 | tf_op jit(solution)/shard_map/all_to_all | solution.py:787
  383.7 3.2 copy.24
  386.9 9.6 %shard_map.186 = bf16[2048,2304]{1,0:T(8,128)(2,1)} custom-call(bf16[2048,2304]{1,0:T(8,128)(2,1)} %all-gather.4.cloned.1.call-done.refs_0_), custom_call_target="tpu_custom_call" | custom-call | flops 94371840 | bytes 18874368 | tf_op jit(solution)/shard_map/pallas_call | solution.py:702
  396.5 1.8 copy-done
  398.3 21.6 %input_grad.1 = (bf16[2,256,2304]{2,1,0:T(8,128)(2,1)}, f32[1,2304]{1,0:T(1,128)S(1)}) custom-call(bf16[256,4096]{1,0:T(8,128)(2,1)S(1)} %bitcast.13, bf16[256,4096]{1,0:T(8,128)(2,1)S(1)} %bitcast.14, bf16[2,256,2304]{2,1,0:T(8,128)(2,1)} %x_ref.3, bf16[2,256,2304]{2,1,0:T(8,128)(2,1)} %dy_ref.1, f32[1,2304]{1,0:T(1,128)S(1)} %copy-done.1, ...), custom_call_target="tpu_custom_call" | custom-call | flops 9663676416 | bytes 21233664 | tf_op jit(solution)/shard_map/input_grad/pallas_call | solution.py:683
  420.0 24.4 %all-reduce.8 = (f32[2304]{0:T(1024)}, f32[2304]{0:T(1024)}, f32[256]{0:T(256)}, f32[256]{0:T(256)}) all-reduce(f32[2304]{0:T(1024)S(1)} %reduce, f32[2304]{0:T(1024)S(1)} %reduce.1, f32[256]{0:T(256)S(1)} %add.97, f32[256]{0:T(256)S(1)} %select_add_fusion), channel_id=1, replica_groups=mesh['dp'=4,'sp'=8] {'sp'}, use_global_device_ids=true, to_apply=%region_8.9 | all-reduce | flops 5120 | bytes 40960 | tf_op jit(solution)/shard_map/psum | solution.py:795
  444.4 15.1 %spread.1 = (bf16[2304,2048]{1,0:T(8,128)(2,1)}, bf16[2304,1024]{1,0:T(8,128)(2,1)}, bf16[2304,1024]{1,0:T(8,128)(2,1)}) custom-call(bf16[8,2304,512]{2,1,0:T(8,128)(2,1)} %bitcast.15, bf16[8,2304,512]{2,1,0:T(8,128)(2,1)} %bitcast.16), custom_call_target="tpu_custom_call" | custom-call | flops 188743680 | bytes 37748736 | tf_op jit(solution)/shard_map/spread/pallas_call | solution.py:726
  459.5 1.4 copy.26
  (41 shorter events, 0.2 us)
Async XLA Ops:
  7.2 379.7 %all-gather.4.cloned.1.call-start = ((), (), s32[]{:S(2)}) async-start(), calls=%async_computation.2 | async-start | bytes 10616832 | tf_op jit(solution)/shard_map/all_gather | solution.py:764
  221.5 223.0 %all-gather.6.cloned.1.call-start = ((), (), s32[]{:S(2)}) async-start(), calls=%async_computation.3 | async-start | bytes 21233664 | tf_op jit(solution)/shard_map/all_gather | solution.py:789
  221.7 3.1 copy-start.17
  221.7 6.9 %copy-start.13 = (f32[2048,256]{1,0:T(8,128)S(1)}, f32[2048,256]{1,0:T(8,128)}, u32[]{:S(2)}) copy-start(f32[2048,256]{1,0:T(8,128)} %get-tuple-element.65) | copy-start | bytes 6291460
  223.8 1.2 copy-start.11
  223.8 4.8 %collective-permute-start = (f32[2048,256]{1,0:T(8,128)S(1)}, f32[2048,256]{1,0:T(8,128)S(1)}, u32[]{:S(2)}, u32[]{:S(2)}) collective-permute-start(f32[2048,256]{1,0:T(8,128)S(1)} %broadcast_select_fusion.1), channel_id=1, source_target_pairs={{0,1},{1,0},{2,3},{3,2},{4,5},{5,4},{6,7},{7,6},{8,9},{9,8},{10,11... | collective-permute-start | bytes 6291464 | tf_op jit(solution)/shard_map/ppermute | solution.py:775
  224.8 0.7 copy-start.19
  224.8 0.7 copy-start.20
  224.8 3.8 copy-start.12
  225.6 3.5 copy-start.14
  225.6 3.5 copy-start.15
  229.1 1.3 copy-start.9
  233.4 1.2 copy-start.6
  233.4 1.2 copy-start.7
  234.3 1.2 copy-start.2
  234.4 1.5 copy-start.3
  234.4 1.8 copy-start.4
  234.4 2.1 copy-start.5
  250.0 1.2 copy-start.10
  250.0 1.6 copy-start.8
  250.3 4.7 %collective-permute-start.1 = (f32[2048,256]{1,0:T(8,128)S(1)}, f32[2048,256]{1,0:T(8,128)S(1)}, u32[]{:S(2)}, u32[]{:S(2)}) collective-permute-start(f32[2048,256]{1,0:T(8,128)S(1)} %broadcast_select_fusion), channel_id=1, source_target_pairs={{0,1},{1,0},{2,3},{3,2},{4,5},{5,4},{6,7},{7,6},{8,9},{9,8},{10,11... | collective-permute-start | bytes 6291464 | tf_op jit(solution)/shard_map/ppermute | solution.py:775
  329.1 4.9 %copy-start.18 = (f32[1,2304]{1,0:T(1,128)S(1)}, f32[1,2304]{1,0:T(1,128)}, u32[]{:S(2)}) copy-start(f32[1,2304]{1,0:T(1,128)} %get-tuple-element.85) | copy-start | bytes 27652
  329.1 54.6 %all-to-all-start.1 = ((bf16[8,256,512]{2,1,0:T(8,128)(2,1)}), bf16[8,256,512]{2,1,0:T(8,128)(2,1)}, u32[]{:S(2)}, u32[]{:S(2)}) async-start(bf16[8,256,512]{2,1,0:T(8,128)(2,1)} %bitcast.5), calls=%async_computation.1 | async-start | bytes 4194304 | tf_op jit(solution)/shard_map/all_to_all | solution.py:787
  386.9 9.6 %copy-start.1 = (f32[1,2304]{1,0:T(1,128)S(1)}, f32[1,2304]{1,0:T(1,128)}, u32[]{:S(2)}) copy-start(f32[1,2304]{1,0:T(1,128)} %broadcast_in_dim.43.wpre_ref) | copy-start | bytes 27652
  396.5 1.8 copy-start
  444.4 15.1 %copy-start.16 = (bf16[2,256,2304]{2,1,0:T(8,128)(2,1)S(1)}, bf16[2,256,2304]{2,1,0:T(8,128)(2,1)}, u32[]{:S(2)}) copy-start(bf16[2,256,2304]{2,1,0:T(8,128)(2,1)} %get-tuple-element.125) | copy-start | bytes 7077892
Sparse Core Ops, SparseCore 0:
  221.6 52.0 all-gather.3
  280.7 130.6 all-gather.5
